TPU v7x, 256 devices: a whole 4x4x8 slice. The times are simulated.
256 devices in a mesh: seq: 8 (over z), exp: 8 (over x, core), tp: 4 (over y).
Axes of the slice: x: 4, y: 4, z: 8, core: 2. Of those that a mesh axis runs over, the one named last changes fastest.
Arguments:
- query_heads: bfloat16 [8192, 32, 128], P(('seq', 'exp'), 'tp'), may hold values from -10 to 10
- key_heads: bfloat16 [8192, 8, 128], P(('seq', 'exp'), 'tp'), may hold values from -10 to 10
- value_head_rows: bfloat16 [8192, 8, 128], P(('seq', 'exp'), 'tp'), may hold values from -6 to 6
- state_input: bfloat16 [8192, 4096], P(('seq', 'exp'), 'tp'), may hold values from -6 to 6
- state_gate: bfloat16 [8192, 4096], P(('seq', 'exp'), 'tp'), may hold values from -6 to 6
- state_inflow: bfloat16 [8192, 8, 128], P(('seq', 'exp'), 'tp'), may hold values from -6 to 6
- state_readout: bfloat16 [8192, 8, 128], P(('seq', 'exp'), 'tp'), may hold values from -6 to 6
- step_size: float32 [8192, 64], P(('seq', 'exp'), 'tp'), may hold values from 0.01 to 0.1
- log_decay: float32 [8192, 64], P(('seq', 'exp'), 'tp'), may hold values from -1 to 0
- skip_scale: float32 [64], P('tp'), may hold values from 0.5 to 2
- state_gain: float32 [4096], P('tp'), may hold values from 0.25 to 1.75
- hidden_in: bfloat16 [8192, 2048], P(('seq', 'exp')), may hold values from -400 to 400
- mlp_gain: float32 [2048], replicated, may hold values from 0.25 to 1.75
- router_weight: bfloat16 [2048, 8], replicated, may hold values from -0.125 to 0.125
- expert_ids: int32 [8192, 2], P(('seq', 'exp')), may hold values from 0 to 7, as said below
- slot_index: int32 [8192, 2], P(('seq', 'exp')), may hold values from -1 to 39, as said below
- gate_up: bfloat16 [8, 7168, 2, 2048], P('exp', ('seq', 'tp')), may hold values from -0.125 to 0.125
- down_proj: bfloat16 [8, 7168, 2048], P('exp', ('seq', 'tp')), may hold values from -0.0625 to 0.0625
Outputs:
- window_out: bfloat16 [8192, 32, 128], P(('seq', 'exp'), 'tp')
- state_out: bfloat16 [8192, 4096], P(('seq', 'exp'), 'tp')
- routed_out: bfloat16 [8192, 2048], P(('seq', 'exp'), 'tp')
Inputs may be any that keep to these rules, and one draw needn't show every extreme that they name: `expert_ids`: the 2 ids of a row differ. slot_index[t, k] is the place of the choice expert_ids[t, k] in that expert's buffer of 40 places for the 128 rows of the device block that holds row t (rows b * 128 to b * 128 + 127); the live places of one expert within one block are distinct; -1 marks a dropped choice.
All inputs are finite; a program needn't handle non-finite values.
Results may differ from a plain program's by a relative error of at most 0.02.
Values may be sent and summed in bfloat16 or wider, within the bound.
A program may use at most 128 MiB of HBM per device.

v0:
```python
import math

import jax
import jax.numpy as jnp
from jax import lax
from jax.sharding import Mesh
from jax.sharding import PartitionSpec as P

EXPERTS = 8
WINDOW = 4096
HP = 64
NS = 128
STRETCH = 128
CAP = 40
EXP = ("exp_0", "exp_1")
SEQ_EXP = ("seq", "exp_0", "exp_1")


EPSILON = 1e-05


def in_one_piece(arrays, axis, dim, along):
    ends, at = ([], 0)
    for a in arrays[:-1]:
        at += a.shape[along]
        ends.append(at)
    both = jnp.concatenate(arrays, axis=along)
    return tuple(jnp.split(lax.all_gather(both, axis, axis=dim, tiled=True), ends, axis=along))


def from_behind(block, axis, distance):
    devices = range(lax.axis_size(axis))
    route = [(i - distance, i) for i in devices if i - distance in devices]
    return lax.ppermute(block, axis, route)


def filled_with(shard, identity):
    return jax.tree.map(
        lambda part, zero: jnp.zeros_like(part) + jnp.asarray(zero, part.dtype), shard, identity
    )


def prefix_by_axis(shard, axes, combine, identity):
    before = start = filled_with(shard, identity)
    running = shard
    for axis in reversed(axes):
        peers, here = (lax.axis_size(axis), lax.axis_index(axis))
        pieces = jax.tree.map(
            lambda part, kind: lax.all_gather(part.astype(kind), axis),
            running,
            jax.tree.map(lambda a: jnp.bfloat16 if a.dtype == jnp.float32 else a.dtype, shard),
        )
        inside, running = (start, start)
        for k in range(peers):
            passed = k < here
            running = combine(
                running, jax.tree.map(lambda part, own: part[k].astype(own.dtype), pieces, shard)
            )
            inside = jax.tree.map(lambda new, old: jnp.where(passed, new, old), running, inside)
        before = combine(inside, before)
    return before


def sent_to_all(shard, axis):
    peers = lax.axis_size(axis)
    return lax.all_to_all(
        jnp.broadcast_to(shard[None], (peers, *shard.shape)), axis, 0, 0, tiled=True
    )


def joined_along(pieces, dim):
    pieces = jnp.moveaxis(pieces, 0, dim)
    lengths = pieces.shape
    return pieces.reshape(*lengths[:dim], lengths[dim] * lengths[dim + 1], *lengths[dim + 2 :])


def gather_directly(shard, axis, dim):
    pieces = sent_to_all(shard, axis)
    return joined_along(pieces, dim)


def cut_along(shard, dim, peers):
    lengths = shard.shape
    pieces = shard.reshape(*lengths[:dim], peers, lengths[dim] // peers, *lengths[dim + 1 :])
    return jnp.moveaxis(pieces, dim, 0)


def sum_at_owner(shard, axis, dim):
    pieces = cut_along(shard, dim, lax.axis_size(axis))
    arrived = lax.all_to_all(pieces, axis, split_axis=0, concat_axis=0, tiled=True)
    return arrived.astype(jnp.float32).sum(axis=0)


def combine_states(earlier, later):
    earlier_decay, earlier_state = earlier
    later_decay, later_state = later
    return (earlier_decay * later_decay, later_decay[..., None, None] * earlier_state + later_state)


def attend_range(running, query_rows, query_pos, key_row_list, value_rows, key_start):
    total_keys = key_row_list.shape[0]
    block_width = math.gcd(total_keys, 1024)
    blocks = total_keys // block_width
    shared_heads = key_row_list.shape[1]
    head_dim = key_row_list.shape[2]
    score_scale = 1.0 / math.sqrt(head_dim)
    key_blocks = key_row_list.reshape(blocks, block_width, shared_heads, head_dim)
    value_blocks = value_rows.reshape(blocks, block_width, shared_heads, head_dim)

    def one_block(carried, packed):
        run_max, run_sum, accumulated = carried
        key_block, value_block, counter = packed
        scores = (
            jnp.einsum("qkgd,jkd->kgqj", query_rows, key_block, preferred_element_type=jnp.float32)
            * score_scale
        )
        key_pos = key_start + counter * block_width + jnp.arange(block_width, dtype=jnp.int32)
        visible = (
            (key_pos[None, :] <= query_pos[:, None])
            & (key_pos[None, :] > query_pos[:, None] - WINDOW)
            & (key_pos[None, :] >= 0)
        )
        scores = jnp.where(visible, scores, -jnp.inf)
        new_max = jnp.maximum(run_max, jnp.max(scores, axis=-1))
        safe_max = jnp.where(new_max == -jnp.inf, 0.0, new_max)
        weights = jnp.exp(scores - safe_max[..., None])
        rescale = jnp.exp(run_max - safe_max)
        run_sum = run_sum * rescale + jnp.sum(weights, axis=-1)
        accumulated = accumulated * rescale[..., None] + jnp.einsum(
            "kgqj,jkd->kgqd",
            weights.astype(jnp.bfloat16),
            value_block,
            preferred_element_type=jnp.float32,
        )
        return ((new_max, run_sum, accumulated), None)

    running, _ = lax.scan(
        one_block, running, (key_blocks, value_blocks, jnp.arange(blocks, dtype=jnp.int32))
    )
    return running


def attention(query_heads, key_heads, value_head_rows):
    row_count, query_count, head_dim = query_heads.shape
    shared_heads = key_heads.shape[1]
    group_width = query_count // shared_heads
    seq_count = lax.axis_size("seq")
    exp_count = lax.axis_size(EXP)
    seq_index = lax.axis_index("seq")
    position = seq_index * exp_count + lax.axis_index(EXP)
    query_pos = position * row_count + jnp.arange(row_count, dtype=jnp.int32)
    query_rows = query_heads.reshape(row_count, shared_heads, group_width, head_dim)
    running = (
        jnp.full((shared_heads, group_width, row_count), -jnp.inf, jnp.float32),
        jnp.zeros((shared_heads, group_width, row_count), jnp.float32),
        jnp.zeros((shared_heads, group_width, row_count, head_dim), jnp.float32),
    )
    group_keys, group_values = in_one_piece((key_heads, value_head_rows), EXP, 0, 1)
    group_rows = row_count * exp_count
    relay_depth = min(-(-WINDOW // group_rows), seq_count - 1)
    own_start = seq_index * group_rows
    stacked = jnp.stack((group_keys, group_values))
    buffer = jnp.zeros((2, relay_depth) + group_keys.shape, jnp.bfloat16)

    def relay_group(counter, carried):
        moving, stored = carried
        moving = from_behind(moving, "seq", 1)
        stored = lax.dynamic_update_index_in_dim(stored, moving, relay_depth - 1 - counter, 1)
        return (moving, stored)

    stored = lax.fori_loop(0, relay_depth, relay_group, (stacked, buffer))[1]
    window_rows = stored.reshape(2, relay_depth * group_rows, shared_heads, head_dim)
    running = attend_range(
        running,
        query_rows,
        query_pos,
        window_rows[0],
        window_rows[1],
        own_start - relay_depth * group_rows,
    )
    running = attend_range(running, query_rows, query_pos, group_keys, group_values, own_start)
    run_max, run_sum, accumulated = running
    outputs = accumulated / run_sum[..., None]
    outputs = jnp.transpose(outputs, (2, 0, 1, 3)).reshape(row_count, query_count, head_dim)
    return outputs.astype(jnp.bfloat16)


def state_space(
    state_input,
    state_gate,
    state_inflow,
    state_readout,
    step_size,
    log_decay,
    skip_scale,
    state_gain,
):
    row_count, channels = state_input.shape
    heads = step_size.shape[1]
    groups = state_inflow.shape[1]
    per_group = heads // groups
    stretch_count = row_count // STRETCH
    inputs = state_input.reshape(stretch_count, STRETCH, groups, per_group, HP)
    inflow = state_inflow.reshape(stretch_count, STRETCH, groups, NS)
    readout = state_readout.reshape(stretch_count, STRETCH, groups, NS)
    step_rows = step_size.reshape(stretch_count, STRETCH, groups, per_group)
    cumulative = jnp.cumsum(log_decay.reshape(stretch_count, STRETCH, groups, per_group), axis=1)
    read_write = jnp.einsum("cign,cjgn->cijg", readout, inflow, preferred_element_type=jnp.float32)
    causal = (jnp.arange(STRETCH)[:, None] >= jnp.arange(STRETCH)[None, :])[None, :, :, None, None]
    decay_gap = cumulative[:, :, None] - cumulative[:, None]
    decay_mat = jnp.where(causal, jnp.exp(jnp.where(causal, decay_gap, 0.0)), 0.0)
    mixing = (decay_mat * read_write[..., None] * step_rows[:, None]).astype(jnp.bfloat16)
    intra = jnp.einsum("cijgk,cjgkp->cigkp", mixing, inputs, preferred_element_type=jnp.float32)
    stretch_total = cumulative[:, -1]
    weight_in = jnp.exp(stretch_total[:, None] - cumulative) * step_rows
    weighted = (weight_in[..., None] * inflow[:, :, :, None, :]).astype(jnp.bfloat16)
    stretch_state = jnp.einsum(
        "cjgkn,cjgkp->cgknp", weighted, inputs, preferred_element_type=jnp.float32
    )

    def carry_stretch(carried, packed):
        stretch_decay, state_piece = packed
        return (stretch_decay[..., None, None] * carried + state_piece, carried)

    initial = jnp.zeros((groups, per_group, NS, HP), jnp.float32)
    device_state, entering_local = lax.scan(
        carry_stretch, initial, (jnp.exp(stretch_total), stretch_state)
    )
    device_decay = jnp.exp(jnp.sum(stretch_total, axis=0))
    summary = (device_decay, device_state)
    identity = (jnp.ones_like(device_decay), jnp.zeros_like(device_state))
    entering = prefix_by_axis(summary, SEQ_EXP, combine_states, identity)[1]
    prefix = jnp.exp(jnp.cumsum(stretch_total, axis=0) - stretch_total)
    stretch_entering = entering_local + prefix[..., None, None] * entering[None]
    inter = jnp.exp(cumulative)[..., None] * jnp.einsum(
        "cign,cgknp->cigkp", readout.astype(jnp.float32), stretch_entering
    )
    skip_rows = skip_scale.reshape(groups, per_group)
    output = intra + inter + skip_rows[:, :, None] * inputs.astype(jnp.float32)
    gate_rows = state_gate.reshape(stretch_count, STRETCH, groups, per_group, HP).astype(
        jnp.float32
    )
    gated = output * jax.nn.silu(gate_rows)
    mean_square = jnp.mean(gated * gated, axis=(3, 4), keepdims=True)
    normed = gated * lax.rsqrt(mean_square + EPSILON)
    return (normed.reshape(row_count, channels) * state_gain).astype(jnp.bfloat16)


def routed(hidden_in, mlp_gain, router_weight, expert_ids, slot_index, gate_up, down_proj):
    row_count = hidden_in.shape[0]
    hidden = hidden_in.astype(jnp.float32)
    mean_square = jnp.mean(hidden * hidden, axis=-1, keepdims=True)
    normed = (hidden * lax.rsqrt(mean_square + EPSILON) * mlp_gain).astype(jnp.bfloat16)
    logits = jnp.dot(normed, router_weight, preferred_element_type=jnp.float32)
    gate_values = jax.nn.sigmoid(logits)
    one_hot = expert_ids[..., None] == jnp.arange(EXPERTS, dtype=jnp.int32)
    chosen = jnp.sum(jnp.where(one_hot, gate_values[:, None, :], 0.0), axis=-1)
    mixing = chosen / jnp.sum(chosen, axis=1, keepdims=True)
    is_live = slot_index >= 0
    target = jnp.where(is_live, expert_ids * CAP + slot_index, -1)
    tp_count = lax.axis_size("tp")
    tp_index = lax.axis_index("tp")
    quarter = CAP // tp_count
    place_ids = (
        jnp.arange(EXPERTS, dtype=jnp.int32)[None, :] * CAP
        + tp_index * quarter
        + jnp.arange(quarter, dtype=jnp.int32)[:, None]
    )
    picker = jnp.any(place_ids[:, :, None, None] == target[None, None], axis=-1)
    picker = picker.reshape(quarter * EXPERTS, row_count).astype(jnp.bfloat16)
    outgoing = jnp.dot(picker, normed, preferred_element_type=jnp.float32).astype(jnp.bfloat16)
    outgoing = outgoing.reshape(quarter, EXPERTS, normed.shape[1])
    received = lax.all_to_all(outgoing, EXP, split_axis=1, concat_axis=0, tiled=True)
    all_rows = gather_directly(received, "seq", 0)
    wide_gate_up, wide_down = (
        lax.all_gather(gate_up, "tp", axis=1, tiled=True),
        lax.all_gather(down_proj, "tp", axis=1, tiled=True),
    )
    projected = jnp.einsum(
        "rld,lfsd->srlf", all_rows, wide_gate_up, preferred_element_type=jnp.float32
    )
    hidden_units = (jax.nn.silu(projected[0]) * projected[1]).astype(jnp.bfloat16)
    summed = lax.psum_scatter(
        jnp.einsum(
            "rlf,lfd->rld", hidden_units, wide_down, preferred_element_type=jnp.float32
        ).astype(jnp.bfloat16),
        "seq",
        scatter_dimension=0,
        tiled=True,
    ).astype(jnp.float32)
    returned_rows = lax.all_to_all(
        summed.astype(jnp.bfloat16), EXP, split_axis=0, concat_axis=1, tiled=True
    ).astype(summed.dtype)
    flat_rows = returned_rows.reshape(quarter * EXPERTS, returned_rows.shape[2])
    in_quarter = is_live & (slot_index // quarter == tp_index)
    place = (slot_index - tp_index * quarter) * EXPERTS + expert_ids
    picked = flat_rows[jnp.where(in_quarter, place, 0)]
    partial_value = jnp.sum(jnp.where(in_quarter, mixing, 0.0)[..., None] * picked, axis=1)
    return sum_at_owner(partial_value.astype(jnp.bfloat16), "tp", 1).astype(jnp.bfloat16)


def local(
    query_heads,
    key_heads,
    value_head_rows,
    state_input,
    state_gate,
    state_inflow,
    state_readout,
    step_size,
    log_decay,
    skip_scale,
    state_gain,
    hidden_in,
    mlp_gain,
    router_weight,
    expert_ids,
    slot_index,
    gate_up,
    down_proj,
):
    window_out = attention(query_heads, key_heads, value_head_rows)
    state_out = state_space(
        state_input,
        state_gate,
        state_inflow,
        state_readout,
        step_size,
        log_decay,
        skip_scale,
        state_gain,
    )
    routed_out = routed(
        hidden_in, mlp_gain, router_weight, expert_ids, slot_index, gate_up, down_proj
    )
    return (window_out, state_out, routed_out)


def solution(mesh):
    finer = Mesh(
        mesh.devices.reshape(mesh.shape["seq"], 4, 2, mesh.shape["tp"]),
        ("seq", "exp_0", "exp_1", "tp"),
    )
    placed = (
        P(SEQ_EXP, "tp", None),
        P(SEQ_EXP, "tp", None),
        P(SEQ_EXP, "tp", None),
        P(SEQ_EXP, "tp"),
        P(SEQ_EXP, "tp"),
        P(SEQ_EXP, "tp", None),
        P(SEQ_EXP, "tp", None),
        P(SEQ_EXP, "tp"),
        P(SEQ_EXP, "tp"),
        P("tp"),
        P("tp"),
        P(SEQ_EXP, None),
        P(),
        P(),
        P(SEQ_EXP, None),
        P(SEQ_EXP, None),
        P(EXP, ("seq", "tp"), None, None),
        P(EXP, ("seq", "tp"), None),
    )
    return jax.shard_map(
        local,
        mesh=finer,
        in_specs=placed,
        out_specs=(P(SEQ_EXP, "tp", None), P(SEQ_EXP, "tp"), P(SEQ_EXP, "tp")),
        check_vma=False,
    )
```

profile of v0, /device:TPU:128, one launch (start us, length us, event | category | flops | bytes accessed | tf_op | source)
XLA Modules:
  0.0 391.9 jit_solution(15563480847970389350)
XLA Ops:
  9.0 1.8 all-gather
  10.9 9.7 %all_gather.35 = bf16[4,2,8]{2,1,0:T(2,128)(2,1)S(1)} all-gather(bf16[1,2,8]{2,1,0:T(2,128)(2,1)S(1)} %fusion.187), channel_id=1, replica_groups=mesh['seq'=8,'exp_0'=4,'exp_1'=2,'tp'=4] {'exp_0'}, dimensions={0}, use_global_device_ids=true | all-gather | bytes 160 | tf_op jit(solution)/shard_map/all_gather | solution.py:49
  24.4 2.2 all-gather.1
  30.7 2.0 copy.240
  34.6 16.8 %all_to_all.34 = bf16[10,8,2048]{2,0,1:T(8,128)(2,1)S(1)} all-to-all(bf16[10,8,2048]{2,0,1:T(8,128)(2,1)S(1)} %copy.239), channel_id=1, replica_groups=mesh['seq'=8,'exp_0'=4,'exp_1'=2,'tp'=4] {'exp_0','exp_1'}, dimensions={1} | all-to-all | bytes 655360 | tf_op jit(solution)/shard_map/all_to_all | solution.py:273
  51.5 1.8 broadcast_in_dim.171
  53.4 7.3 %all-to-all-start.1 = ((bf16[8,80,1,2048]{3,1,2,0:T(8,128)(2,1)}), bf16[8,80,1,2048]{3,1,2,0:T(8,128)(2,1)}, u32[]{:S(2)}, u32[]{:S(2)}) async-start(bf16[8,80,1,2048]{3,1,2,0:T(8,128)(2,1)} %broadcast_in_dim.171), calls=%async_computation.1 | async-start | bytes 5242880 | tf_op jit(solution)/shard_map/all_to_all | solution.py:66
  64.6 61.5 %all_gather.36 = bf16[8,2,8]{2,1,0:T(2,128)(2,1)S(1)} all-gather(bf16[1,2,8]{2,1,0:T(2,128)(2,1)S(1)} %fusion.184), channel_id=1, replica_groups=mesh['seq'=8,'exp_0'=4,'exp_1'=2,'tp'=4] {'seq'}, dimensions={0}, use_global_device_ids=true | all-gather | bytes 288 | tf_op jit(solution)/shard_map/all_gather | solution.py:49
  128.3 2.2 fusion.112
  133.4 2.8 broadcast_in_dim.162.clone
  136.2 130.0 %while.9 = (s32[]{:T(128)}, bf16[2,1024,2,128]{3,2,1,0:T(2,128)(2,1)S(1)}, bf16[2,4,1024,2,128]{4,2,3,1,0:T(8,128)(2,1)}, s32[]{:T(128)}, s32[]{:T(128)}, /*index=5*/s32[]{:T(128)}, s32[]{:T(128)}) while((s32[]{:T(128)}, bf16[2,1024,2,128]{3,2,1,0:T(2,128)(2,1)S(1)}, bf16[2,4,1024,2,128]{4,2,3,1,0:T(8,128)(2,1)}, s32[]{:T(128)}, s32[]{:T(128)}, ...), condition=%wide.region_1.2_spmd, body=%wide.region_0.1_spmd.sunk | while | flops 6 | bytes 8388775 | solution.py:171
  136.2 2.5 collective-permute-start
  138.7 24.3 %collective-permute-done = bf16[2,1024,2,128]{3,2,1,0:T(2,128)(2,1)S(1)} collective-permute-done((bf16[2,1024,2,128]{3,2,1,0:T(2,128)(2,1)S(1)}, bf16[2,1024,2,128]{3,2,1,0:T(2,128)(2,1)S(1)}, u32[]{:S(2)}, u32[]{:S(2)}) %collective-permute-start) | collective-permute-done | bytes 1048608 | tf_op jit(solution)/shard_map/while/body/eval_jaxpr/ppermute | solution.py:34
  164.9 1.9 collective-permute-start
  166.8 24.2 %collective-permute-done = bf16[2,1024,2,128]{3,2,1,0:T(2,128)(2,1)S(1)} collective-permute-done((bf16[2,1024,2,128]{3,2,1,0:T(2,128)(2,1)S(1)}, bf16[2,1024,2,128]{3,2,1,0:T(2,128)(2,1)S(1)}, u32[]{:S(2)}, u32[]{:S(2)}) %collective-permute-start) | collective-permute-done | bytes 1048608 | tf_op jit(solution)/shard_map/while/body/eval_jaxpr/ppermute | solution.py:34
  192.9 1.9 collective-permute-start
  194.8 23.4 %collective-permute-done = bf16[2,1024,2,128]{3,2,1,0:T(2,128)(2,1)S(1)} collective-permute-done((bf16[2,1024,2,128]{3,2,1,0:T(2,128)(2,1)S(1)}, bf16[2,1024,2,128]{3,2,1,0:T(2,128)(2,1)S(1)}, u32[]{:S(2)}, u32[]{:S(2)}) %collective-permute-start) | collective-permute-done | bytes 1048608 | tf_op jit(solution)/shard_map/while/body/eval_jaxpr/ppermute | solution.py:34
  220.2 1.9 collective-permute-start
  222.1 42.2 %collective-permute-done = bf16[2,1024,2,128]{3,2,1,0:T(2,128)(2,1)S(1)} collective-permute-done((bf16[2,1024,2,128]{3,2,1,0:T(2,128)(2,1)S(1)}, bf16[2,1024,2,128]{3,2,1,0:T(2,128)(2,1)S(1)}, u32[]{:S(2)}, u32[]{:S(2)}) %collective-permute-start) | collective-permute-done | bytes 1048608 | tf_op jit(solution)/shard_map/while/body/eval_jaxpr/ppermute | solution.py:34
  266.2 4.0 %slice_bitcast_fusion = (bf16[4,1024,2,128]{3,1,2,0:T(8,128)(2,1)}, bf16[4,1024,2,128]{3,1,2,0:T(8,128)(2,1)S(1)}) fusion(bf16[2,4,1024,2,128]{4,2,3,1,0:T(8,128)(2,1)} %get-tuple-element.236), kind=kLoop, calls=%fused_computation.48 | loop fusion | bytes 8388608 | tf_op jit(solution)/shard_map/reshape;squeeze | solution.py:108
  270.2 10.1 %fusion.36 = f32[2,640,1,896]{3,1,0,2:T(8,128)} fusion(bf16[640,2048,1]{1,0,2:T(8,128)(2,1)} %bitcast.53, bf16[1,896,2,2048]{3,1,2,0:T(8,128)(2,1)} %all-gather.14.cloned.1.call-done), kind=kOutput, calls=%fused_computation.46 | convolution fusion | flops 4697620480 | bytes 14548992 | tf_op jit(solution)/shard_map/rld,lfsd->srlf/dot_general | solution.py:279
  280.3 7.9 %fusion.31 = bf16[640,1,2048]{2,0,1:T(8,128)(2,1)} fusion(bf16[1,896,2048]{2,1,0:T(8,128)(2,1)} %all-gather.16.cloned.1.call-done, f32[2,640,1,896]{3,1,0,2:T(8,128)} %fusion.36), kind=kOutput, calls=%fused_computation.41 | convolution fusion | flops 2353561600 | bytes 10878976 | tf_op jit(solution)/shard_map/rlf,lfd->rld/dot_general | solution.py:284
  288.7 47.4 %while.10 = (s32[]{:T(128)}, f32[2,4,128]{2,1,0:T(4,128)S(1)}, f32[2,4,128]{2,1,0:T(4,128)S(1)}, f32[2,4,128,128]{3,2,1,0:T(8,128)}, s32[4]{0:T(128)}, /*index=5...) while((s32[]{:T(128)}, f32[2,4,128]{2,1,0:T(4,128)S(1)}, ...), condition=%wide.region_5.6_spmd.clone, body=%wide.region_2.5_spmd.clone.sunk | while | flops 549335296 | bytes 32326360 | solution.py:137
  291.1 2.7 fusion.219
  293.8 3.2 fusion.220
  297.2 3.1 fusion.222
  302.8 2.7 fusion.219
  305.5 3.2 fusion.220
  308.9 3.3 fusion.222
  314.7 2.7 fusion.219
  317.4 3.2 fusion.220
  320.9 3.3 fusion.222
  324.2 1.3 dynamic_slice.52
  326.6 2.7 fusion.219
  329.3 3.2 fusion.220
  332.8 3.3 fusion.222
  336.1 1.9 fusion.27
  339.0 1.4 fusion.61
  341.5 3.0 fusion.45
  345.1 1.8 reduce.3
  348.0 3.4 all-to-all-start.2
  351.5 1.4 multiply_reduce_fusion.1
  352.9 6.7 %all-to-all-done.2 = bf16[8,2,10240]{2,1,0:T(2,128)(2,1)S(1)} async-done(((bf16[8,2,10240]{2,1,0:T(2,128)(2,1)}), bf16[8,2,10240]{2,1,0:T(2,128)(2,1)S(1)}, u32[]{:S(2)}, u32[]{:S(2)}) %all-to-all-start.2) | async-done | bytes 327712 | tf_op jit(solution)/shard_map/all_to_all | solution.py:291
  360.9 1.5 gather_fusion
  362.4 2.2 reshape.529
  364.7 4.8 %multiply_reduce_fusion = bf16[128,2048]{1,0:T(8,128)(2,1)S(1)} fusion(f32[128,2,2048]{2,1,0:T(2,128)} %reshape.529, f32[128,2]{1,0:T(8,128)S(1)} %copy.238), kind=kLoop, calls=%fused_computation.47 | loop fusion | flops 786432 | bytes 2622464 | tf_op jit(solution)/shard_map/reduce_sum | solution.py:298
  370.7 4.5 %all-to-all-start.3 = ((bf16[4,128,512]{2,1,0:T(8,128)(2,1)}), bf16[4,128,512]{2,1,0:T(8,128)(2,1)S(1)}, u32[]{:S(2)}, u32[]{:S(2)}) async-start(bf16[4,128,512]{2,1,0:T(8,128)(2,1)} %copy.245), calls=%async_computation.4 | async-start | bytes 1048576 | tf_op jit(solution)/shard_map/all_to_all | solution.py:90
  376.3 8.0 %all-to-all-done.3 = bf16[4,128,512]{2,1,0:T(8,128)(2,1)S(1)} async-done(((bf16[4,128,512]{2,1,0:T(8,128)(2,1)}), bf16[4,128,512]{2,1,0:T(8,128)(2,1)S(1)}, u32[]{:S(2)}, u32[]{:S(2)}) %all-to-all-start.3) | async-done | bytes 524320 | tf_op jit(solution)/shard_map/all_to_all | solution.py:90
  (232 shorter events, 42.6 us)
Async XLA Ops:
  7.2 55.5 %copy-start = (bf16[128,2,128]{2,1,0:T(2,128)(2,1)S(1)}, bf16[128,2,128]{2,1,0:T(2,128)(2,1)}, u32[]{:S(2)}) copy-start(bf16[128,2,128]{2,1,0:T(2,128)(2,1)} %param.28) | copy-start | bytes 196612
  7.2 23.5 %copy-start.3 = (bf16[1,224,2,2048]{3,2,1,0:T(2,128)(2,1)S(1)}, bf16[1,224,2,2048]{3,2,1,0:T(2,128)(2,1)}, u32[]{:S(2)}) copy-start(bf16[1,224,2,2048]{3,2,1,0:T(2,128)(2,1)} %param.38) | copy-start | bytes 5505028
  7.2 121.1 %all-gather.10.cloned.1.call-start = ((), (), s32[]{:S(2)}) async-start(), calls=%async_computation.6 | async-start | bytes 1310720 | tf_op jit(solution)/shard_map/all_gather | solution.py:49
  8.4 15.4 %copy-start.13 = (f32[1,128,2,8]{1,3,2,0:T(8,128)}, f32[1,128,2,8]{1,3,2,0:T(8,128)S(1)}, u32[]{:S(2)}) copy-start(f32[1,128,2,8]{1,3,2,0:T(8,128)S(1)} %copy.228) | copy-start | bytes 24580
  10.8 18.2 %copy-start.31 = (f32[2,8]{1,0:T(2,128)}, f32[2,8]{1,0:T(2,128)S(1)}, u32[]{:S(2)}) copy-start(f32[2,8]{1,0:T(2,128)S(1)} %convert_bitcast_fusion.1) | copy-start | bytes 196
  26.6 6.8 %copy-start.6 = (bf16[128,2048]{1,0:T(8,128)(2,1)S(1)}, bf16[128,2048]{1,0:T(8,128)(2,1)}, u32[]{:S(2)}) copy-start(bf16[128,2048]{1,0:T(8,128)(2,1)} %param.33) | copy-start | bytes 1572868
  27.2 6.3 %copy-start.21 = (f32[2,8]{1,0:T(2,128)}, f32[2,8]{1,0:T(2,128)S(1)}, u32[]{:S(2)}) copy-start(f32[2,8]{1,0:T(2,128)S(1)} %get-tuple-element.383) | copy-start | bytes 196
  27.2 6.4 %copy-start.43 = (bf16[2048,8]{0,1:T(8,128)(2,1)S(1)}, bf16[2048,8]{0,1:T(8,128)(2,1)}, u32[]{:S(2)}) copy-start(bf16[2048,8]{0,1:T(8,128)(2,1)} %param.35) | copy-start | bytes 98308
  27.2 6.4 %copy-start.44 = (f32[2048]{0:T(1024)S(1)}, f32[2048]{0:T(1024)}, u32[]{:S(2)}) copy-start(f32[2048]{0:T(1024)} %param.34) | copy-start | bytes 24580
  28.2 102.7 %all-gather.8.cloned.1.call-start = ((), (), s32[]{:S(2)}) async-start(), calls=%async_computation.5 | async-start | bytes 1179648 | tf_op jit(solution)/shard_map/all_gather | solution.py:28
  29.9 3.9 %copy-start.29 = (s32[128,2]{0,1:T(2,128)S(1)}, s32[128,2]{0,1:T(2,128)}, u32[]{:S(2)}) copy-start(s32[128,2]{0,1:T(2,128)} %param.36) | copy-start | bytes 3076
  30.0 4.0 %copy-start.30 = (s32[128,2]{0,1:T(2,128)S(1)}, s32[128,2]{0,1:T(2,128)}, u32[]{:S(2)}) copy-start(s32[128,2]{0,1:T(2,128)} %param.37) | copy-start | bytes 3076
  30.7 239.5 %all-gather.14.cloned.1.call-start = ((), (), s32[]{:S(2)}) async-start(), calls=%async_computation.8 | async-start | bytes 9175040 | tf_op jit(solution)/shard_map/all_gather | solution.py:276
  32.7 247.5 %all-gather.16.cloned.1.call-start = ((), (), s32[]{:S(2)}) async-start(), calls=%async_computation.9 | async-start | bytes 4587520 | tf_op jit(solution)/shard_map/all_gather | solution.py:277
  51.5 9.2 %copy-start.4 = (bf16[128,1024]{1,0:T(8,128)(2,1)S(1)}, bf16[128,1024]{1,0:T(8,128)(2,1)}, u32[]{:S(2)}) copy-start(bf16[128,1024]{1,0:T(8,128)(2,1)} %param.25) | copy-start | bytes 786436
  51.5 10.2 %copy-start.9 = (bf16[128,1024]{1,0:T(8,128)(2,1)S(1)}, bf16[128,1024]{1,0:T(8,128)(2,1)}, u32[]{:S(2)}) copy-start(bf16[128,1024]{1,0:T(8,128)(2,1)} %param.26) | copy-start | bytes 786436
  51.5 11.1 %copy-start.11 = (bf16[128,2,128]{2,1,0:T(2,128)(2,1)S(1)}, bf16[128,2,128]{2,1,0:T(2,128)(2,1)}, u32[]{:S(2)}) copy-start(bf16[128,2,128]{2,1,0:T(2,128)(2,1)} %param.27) | copy-start | bytes 196612
  53.4 10.2 %copy-start.45 = (f32[16]{0:T(128)S(1)}, f32[16]{0:T(128)}, u32[]{:S(2)}) copy-start(f32[16]{0:T(128)} %param.31) | copy-start | bytes 196
  53.4 10.9 %copy-start.10 = (bf16[128,8,128]{2,1,0:T(8,128)(2,1)S(1)}, bf16[128,8,128]{2,1,0:T(8,128)(2,1)}, u32[]{:S(2)}) copy-start(bf16[128,8,128]{2,1,0:T(8,128)(2,1)} %param.22) | copy-start | bytes 786436
  53.4 74.9 %copy-start.19 = (f32[2,8]{1,0:T(2,128)S(1)}, f32[2,8]{1,0:T(2,128)}, u32[]{:S(2)}) copy-start(f32[2,8]{1,0:T(2,128)} %get-tuple-element.379) | copy-start | bytes 196
  53.4 216.8 %all-to-all-start.1 = ((bf16[8,80,1,2048]{3,1,2,0:T(8,128)(2,1)}), bf16[8,80,1,2048]{3,1,2,0:T(8,128)(2,1)}, u32[]{:S(2)}, u32[]{:S(2)}) async-start(bf16[8,80,1,2048]{3,1,2,0:T(8,128)(2,1)} %broadcast_in_dim.171), calls=%async_computation.1 | async-start | bytes 5242880 | tf_op jit(solution)/shard_map/all_to_all | solution.py:66
  60.7 280.6 %all-gather.12.cloned.1.call-start = ((), (), s32[]{:S(2)}) async-start(), calls=%async_computation.7 | async-start | bytes 2359296 | tf_op jit(solution)/shard_map/all_gather | solution.py:49
  127.3 3.5 copy-start.23
  127.3 3.5 copy-start.25
  127.3 3.5 copy-start.27
  130.6 214.0 %reduce-scatter.2.cloned.1.call-start = ((), (), s32[]{:S(2)}) async-start(), calls=%async_computation.10 | async-start | bytes 2949120 | tf_op jit(solution)/shard_map/reduce_scatter | solution.py:283
  136.2 26.9 %collective-permute-start = (bf16[2,1024,2,128]{3,2,1,0:T(2,128)(2,1)S(1)}, bf16[2,1024,2,128]{3,2,1,0:T(2,128)(2,1)S(1)}, u32[]{:S(2)}, u32[]{:S(2)}) collective-permute-start(bf16[2,1024,2,128]{3,2,1,0:T(2,128)(2,1)S(1)} %get-tuple-element.494), channel_id=1, source_target_pairs={{0,32},{32,64},{64,96},{96,128},{128,160},{160,192},{192,224},{1,3... | collective-permute-start | bytes 3145736 | tf_op jit(solution)/shard_map/while/body/eval_jaxpr/ppermute | solution.py:34
  164.9 26.1 %collective-permute-start = (bf16[2,1024,2,128]{3,2,1,0:T(2,128)(2,1)S(1)}, bf16[2,1024,2,128]{3,2,1,0:T(2,128)(2,1)S(1)}, u32[]{:S(2)}, u32[]{:S(2)}) collective-permute-start(bf16[2,1024,2,128]{3,2,1,0:T(2,128)(2,1)S(1)} %get-tuple-element.494), channel_id=1, source_target_pairs={{0,32},{32,64},{64,96},{96,128},{128,160},{160,192},{192,224},{1,3... | collective-permute-start | bytes 3145736 | tf_op jit(solution)/shard_map/while/body/eval_jaxpr/ppermute | solution.py:34
  192.9 25.4 %collective-permute-start = (bf16[2,1024,2,128]{3,2,1,0:T(2,128)(2,1)S(1)}, bf16[2,1024,2,128]{3,2,1,0:T(2,128)(2,1)S(1)}, u32[]{:S(2)}, u32[]{:S(2)}) collective-permute-start(bf16[2,1024,2,128]{3,2,1,0:T(2,128)(2,1)S(1)} %get-tuple-element.494), channel_id=1, source_target_pairs={{0,32},{32,64},{64,96},{96,128},{128,160},{160,192},{192,224},{1,3... | collective-permute-start | bytes 3145736 | tf_op jit(solution)/shard_map/while/body/eval_jaxpr/ppermute | solution.py:34
  220.2 44.2 %collective-permute-start = (bf16[2,1024,2,128]{3,2,1,0:T(2,128)(2,1)S(1)}, bf16[2,1024,2,128]{3,2,1,0:T(2,128)(2,1)S(1)}, u32[]{:S(2)}, u32[]{:S(2)}) collective-permute-start(bf16[2,1024,2,128]{3,2,1,0:T(2,128)(2,1)S(1)} %get-tuple-element.494), channel_id=1, source_target_pairs={{0,32},{32,64},{64,96},{96,128},{128,160},{160,192},{192,224},{1,3... | collective-permute-start | bytes 3145736 | tf_op jit(solution)/shard_map/while/body/eval_jaxpr/ppermute | solution.py:34
  293.8 3.4 copy-start.1
  305.5 3.5 copy-start.1
  317.3 3.5 copy-start.1
  329.3 3.5 copy-start.1
  336.1 2.8 copy-start.2
  336.1 2.8 copy-start.46
  338.9 2.4 copy-start.17
  341.5 9.9 %copy-start.7 = (f32[128,1024]{0,1:T(8,128)S(1)}, f32[128,1024]{0,1:T(8,128)}, u32[]{:S(2)}) copy-start(f32[128,1024]{0,1:T(8,128)} %copy.235) | copy-start | bytes 1572868
  341.5 9.9 %copy-start.8 = (f32[128,1024]{0,1:T(8,128)S(1)}, f32[128,1024]{0,1:T(8,128)}, u32[]{:S(2)}) copy-start(f32[128,1024]{0,1:T(8,128)} %copy.236) | copy-start | bytes 1572868
  341.5 9.9 %copy-start.12 = (f32[128,128,2]{1,0,2:T(8,128)S(1)}, f32[128,128,2]{1,0,2:T(8,128)}, u32[]{:S(2)}) copy-start(f32[128,128,2]{1,0,2:T(8,128)} %copy.231) | copy-start | bytes 393220
  341.5 9.9 %copy-start.14 = (f32[1,128,2,8]{1,3,2,0:T(8,128)S(1)}, f32[1,128,2,8]{1,3,2,0:T(8,128)}, u32[]{:S(2)}) copy-start(f32[1,128,2,8]{1,3,2,0:T(8,128)} %copy-done.13) | copy-start | bytes 24580
  341.5 9.9 %copy-start.15 = (pred[128,128]{1,0:T(8,128)(4,1)S(1)}, pred[128,128]{1,0:T(8,128)(4,1)}, u32[]{:S(2)}) copy-start(pred[128,128]{1,0:T(8,128)(4,1)} %iota_compare_fusion) | copy-start | bytes 49156
  341.5 9.9 %copy-start.16 = (f32[128,16]{0,1:T(8,128)S(1)}, f32[128,16]{0,1:T(8,128)}, u32[]{:S(2)}) copy-start(f32[128,16]{0,1:T(8,128)} %param.29) | copy-start | bytes 24580
  341.5 9.9 %copy-start.47 = (f32[2,8]{1,0:T(2,128)S(1)}, f32[2,8]{1,0:T(2,128)}, u32[]{:S(2)}) copy-start(f32[2,8]{1,0:T(2,128)} %mul.543) | copy-start | bytes 196
  348.0 11.6 %all-to-all-start.2 = ((bf16[8,2,10240]{2,1,0:T(2,128)(2,1)}), bf16[8,2,10240]{2,1,0:T(2,128)(2,1)S(1)}, u32[]{:S(2)}, u32[]{:S(2)}) async-start(bf16[8,2,10240]{2,1,0:T(2,128)(2,1)} %reshape.558), calls=%async_computation.3 | async-start | bytes 655360 | tf_op jit(solution)/shard_map/all_to_all | solution.py:291
  362.4 12.9 %copy-start.5 = (f32[1,128,2,8,64]{1,4,3,2,0:T(8,128)S(1)}, f32[1,128,2,8,64]{1,4,3,2,0:T(8,128)}, u32[]{:S(2)}) copy-start(f32[1,128,2,8,64]{1,4,3,2,0:T(8,128)} %get-tuple-element.387) | copy-start | bytes 1572868
  364.7 10.9 %copy-start.18 = (f32[1024]{0:T(1024)S(1)}, f32[1024]{0:T(1024)}, u32[]{:S(2)}) copy-start(f32[1024]{0:T(1024)} %param.32) | copy-start | bytes 12292
  370.7 13.6 %all-to-all-start.3 = ((bf16[4,128,512]{2,1,0:T(8,128)(2,1)}), bf16[4,128,512]{2,1,0:T(8,128)(2,1)S(1)}, u32[]{:S(2)}, u32[]{:S(2)}) async-start(bf16[4,128,512]{2,1,0:T(8,128)(2,1)} %copy.245), calls=%async_computation.4 | async-start | bytes 1048576 | tf_op jit(solution)/shard_map/all_to_all | solution.py:90
  (17 other events, 41.3 us)
Sparse Core Ops, SparseCore 0:
  28.3 27.9 all-gather.9
  58.6 26.4 all-gather.7
  87.0 76.8 all-gather.13
  165.5 47.2 all-gather.15
  215.0 48.7 all-gather.11
  288.3 41.8 reduce-scatter.1
where the time goes:
time: 393 us; the launch traced here: 392 us
  waiting for transfers between devices  130 us (33%)
  blocking collectives  92 us (23%)
  matrix products  50.8 us (13%)
  local copies, waits for them, and re-layouts  44.4 us (11%)
  other arithmetic  33.2 us (8%)
  starting transfers between devices  24 us (6%)
  between operations  15 us (4%)
    ppermute x4, waiting for transfers between devices, from_behind(): return lax.ppermute(block, axis, route)  114 us
    all_gather x4, blocking collectives, prefix_by_axis(): lax.all_gather(part.astype(kind), axis)  75.2 us
    all_to_all x1, blocking collectives, routed(): lax.all_to_all(outgoing, EXP, split_axis=1, concat_axis=0, tiled=True)  16.8 us
    dot_general x5, matrix products, one_block(): jnp.einsum('kgqj,jkd->kgqd', weights.astype(jnp.bfloat16), value_block, p...  14.4 us
    reduce_sum x5, other arithmetic, one_block(): run_sum = run_sum * rescale + jnp.sum(weights, axis=-1)  13.8 us
    dot_general x5, matrix products, one_block(): jnp.einsum('qkgd,jkd->kgqj', query_rows, key_block, preferred_element_typ...  12.6 us
    dot_general x1, matrix products, routed(): jnp.einsum('rld,lfsd->srlf', all_rows, wide_gate_up, preferred_element_ty...  10.1 us
    ppermute x4, starting transfers between devices, from_behind(): return lax.ppermute(block, axis, route)  8.28 us
  transfers between devices with their start and end apart: 13, of which 6 were waited for; matrix products, arithmetic and copies ran while one was open for 27% of the time, Pallas kernels for 0%

commit v1 on v0

v1 whole, which is shorter than its diff:
```python
import functools
import math

import jax
import jax.numpy as jnp
from jax import lax
from jax.experimental import pallas as pl
from jax.experimental.pallas import tpu as pltpu
from jax.sharding import PartitionSpec as P

EXPERTS = 8
CAP = 40
STEPS = 8
CORES = 8
TPS = 4
QUARTER = 10
PAD = 16
ROWS = 80
EPSILON = 1e-05
VM = pltpu.VMEM
MESH = pl.DeviceIdType.MESH
F32 = jnp.float32
BF16 = jnp.bfloat16


def rcopy(src, dst, ss, rs, dev):
    return pltpu.make_async_remote_copy(
        src_ref=src, dst_ref=dst, send_sem=ss, recv_sem=rs, device_id=dev, device_id_type=MESH
    )


def guarded(cond, fn):
    if cond is True:
        fn()
    else:
        pl.when(cond)(fn)


def greet(groups):
    barrier = pltpu.get_barrier_semaphore()
    count = 0
    for axis, size, shifts in groups:
        me = lax.axis_index(axis)
        for d in shifts:
            pl.semaphore_signal(
                barrier, inc=1, device_id={axis: lax.rem(me + d, size)}, device_id_type=MESH
            )
            count += 1
    pl.semaphore_wait(barrier, count)


def spread_kernel(
    kv_in, rows_in, pack, st_in, dec_s, dec_o,
    kv, rows, ent,
    disp, st_rx, t_tx, t_rx, ent_tx, inner, carry,
    z_s, z_r, x_s, x_r, p_s, p_r, f_s, f_r,
    d_s, d_r, rf_s, rf_r, rb_s, rb_r, sa_s, sa_r, st_s, st_r, se_s, se_r,
):
    s = lax.axis_index("seq")
    e = lax.axis_index("exp")
    x = e // 2
    c = lax.rem(e, 2)
    partner = e + 1 - 2 * c
    nxt = lax.rem(s + 1, STEPS)
    prv = lax.rem(s + STEPS - 1, STEPS)
    greet((("exp", CORES, range(1, CORES)), ("seq", STEPS, range(1, STEPS))))
    pending = []

    def send(copy, cond=True):
        guarded(cond, copy.start)
        pending.append((copy, cond))

    def slot_of(k):
        return 32 if k == 4 else k * 8 + e

    def block(k):
        return kv_in if k == 0 else kv.at[:, slot_of(k)]

    def kv_hop(k):
        return rcopy(
            block(k - 1), kv.at[:, slot_of(k)], z_s.at[k - 1], z_r.at[k - 1], {"seq": nxt}
        )

    def kv_across(g, k):
        for dx in range(1, 4):
            tx = lax.rem(x + dx, 4)
            if k == 0:
                cond = tx > x
            elif k == 4:
                cond = (tx < x) & (s >= 4)
            else:
                cond = s >= k
            send(
                rcopy(
                    block(k), kv.at[:, g * 8 + e], x_s.at[k, dx], x_r.at[g, dx],
                    {"exp": 2 * tx + c},
                ),
                cond,
            )
        if k == 0:
            cond = c == 0
        elif k == 4:
            cond = (c == 1) & (s >= 4)
        else:
            cond = s >= k
        send(
            rcopy(block(k), kv.at[:, g * 8 + e], p_s.at[k], p_r.at[g], {"exp": partner}), cond
        )

    def kv_forward(g):
        for dx in range(1, 4):
            sx = lax.rem(x + 4 - dx, 4)
            cond = ((sx < x) | (s >= 4)) if g == 0 else s >= g
            slot = kv.at[:, g * 8 + 2 * sx + c]
            arrived = rcopy(slot, slot, x_s.at[g, dx], x_r.at[g, dx], {"exp": 2 * sx + c})
            onward = rcopy(slot, slot, f_s.at[g, dx], f_r.at[g, dx], {"exp": partner})

            def pass_on(arrived=arrived, onward=onward):
                arrived.wait_recv()
                onward.start()

            guarded(cond, pass_on)
            pending.append((onward, cond))

    def kv_finish(g):
        slot = kv.at[:, g * 8 + partner]
        cond = ((c == 1) | (s >= 4)) if g == 0 else s >= g
        guarded(cond, rcopy(slot, slot, p_s.at[g], p_r.at[g], {"exp": partner}).wait_recv)
        for dx in range(1, 4):
            sx = lax.rem(x + 4 - dx, 4)
            cond = ((sx < x) | (s >= 4)) if g == 0 else s >= g
            slot = kv.at[:, g * 8 + 2 * sx + 1 - c]
            guarded(
                cond, rcopy(slot, slot, f_s.at[g, dx], f_r.at[g, dx], {"exp": partner}).wait_recv
            )

    for d in range(1, CORES):
        to = lax.rem(e + d, CORES)
        send(rcopy(rows_in.at[to], disp.at[e], d_s.at[d], d_r.at[d], {"exp": to}))
    send(kv_hop(1), s < STEPS - 1)
    for d in range(1, CORES):
        to = lax.rem(e + d, CORES)
        send(rcopy(st_in.at[to], st_rx.at[e], sa_s.at[d], sa_r.at[d], {"exp": to}))
    kv_across(0, 0)
    kv[:, pl.ds(e, 1)] = kv_in[...][:, None]
    disp[pl.ds(e, 1)] = rows_in[pl.ds(e, 1)]
    st_rx[pl.ds(e, 1)] = st_in[pl.ds(e, 1)]

    for d in range(1, CORES):
        frm = lax.rem(e + CORES - d, CORES)
        rcopy(disp.at[frm], disp.at[frm], d_s.at[d], d_r.at[d], {"exp": frm}).wait_recv()
    packed = jnp.dot(
        pack[...], disp[...].reshape(CORES * PAD, -1), preferred_element_type=F32
    ).astype(BF16)
    rows[pl.ds(s, 1)] = packed[None]

    def rows_up(j):
        at = rows.at[lax.rem(s + STEPS - j, STEPS)]
        return rcopy(at, at, rf_s.at[j], rf_r.at[j], {"seq": nxt})

    def rows_down(j):
        at = rows.at[lax.rem(s + j, STEPS)]
        return rcopy(at, at, rb_s.at[j], rb_r.at[j], {"seq": prv})

    def rows_up_arrived(j):
        at = rows.at[lax.rem(s + STEPS - 1 - j, STEPS)]
        return rcopy(at, at, rf_s.at[j], rf_r.at[j], {"seq": prv})

    def rows_down_arrived(j):
        at = rows.at[lax.rem(s + 1 + j, STEPS)]
        return rcopy(at, at, rb_s.at[j], rb_r.at[j], {"seq": nxt})

    send(rows_up(0))
    send(rows_down(0))

    for d in range(1, CORES):
        frm = lax.rem(e + CORES - d, CORES)
        rcopy(st_rx.at[frm], st_rx.at[frm], sa_s.at[d], sa_r.at[d], {"exp": frm}).wait_recv()
    for h in range(2):
        part = slice(64 * h, 64 * h + 64)
        run = jnp.zeros((64, 128), F32)
        for k in range(CORES):
            inner[k, part, :] = run
            run = run * dec_s[k, h] + st_rx[k, part, :].astype(F32)
        t_tx[part, :] = run.astype(BF16)
    for d in range(1, STEPS):
        to = lax.rem(s + d, STEPS)
        send(rcopy(t_tx, t_rx.at[s], st_s.at[d], st_r.at[d], {"seq": to}), s + d < STEPS)

    def kv_arrive(k):
        slot = kv.at[:, slot_of(k)]
        guarded(
            s >= k, rcopy(slot, slot, z_s.at[k - 1], z_r.at[k - 1], {"seq": prv}).wait_recv
        )
        if k < 4:
            send(kv_hop(k + 1), (s >= k) & (s < STEPS - 1))
        kv_across(0 if k == 4 else k, k)

    for j in range(4):
        kv_arrive(j + 1)
        if j < 3:
            rows_up_arrived(j).wait_recv()
            if j < 2:
                send(rows_up(j + 1))
        if j >= 1:
            kv_forward(j)
        if j == 0:
            for d in range(1, STEPS):
                frm = lax.rem(s + STEPS - d, STEPS)
                at = t_rx.at[frm]
                guarded(
                    d <= s, rcopy(at, at, st_s.at[d], st_r.at[d], {"seq": frm}).wait_recv
                )
            carry[...] = jnp.zeros_like(carry)
            for k in range(STEPS - 1):

                def fold(k=k):
                    for h in range(2):
                        part = slice(64 * h, 64 * h + 64)
                        carry[part, :] = carry[part, :] * dec_o[k, h] + t_rx[
                            k, part, :
                        ].astype(F32)

                pl.when(k < s)(fold)
            for h in range(2):
                part = slice(64 * h, 64 * h + 64)
                moved = carry[part, :]
                for k in range(CORES):
                    ent_tx[k, part, :] = (inner[k, part, :] + moved).astype(BF16)
                    moved = moved * dec_s[k, h]
            for d in range(1, CORES):
                to = lax.rem(e + d, CORES)
                send(rcopy(ent_tx.at[to], ent.at[e], se_s.at[d], se_r.at[d], {"exp": to}))
            ent[pl.ds(e, 1)] = ent_tx[pl.ds(e, 1)]
        rows_down_arrived(j).wait_recv()
        if j < 3:
            send(rows_down(j + 1))
    kv_forward(0)
    for g in (1, 2, 3, 0):
        kv_finish(g)
    for d in range(1, CORES):
        frm = lax.rem(e + CORES - d, CORES)
        rcopy(ent.at[frm], ent.at[frm], se_s.at[d], se_r.at[d], {"exp": frm}).wait_recv()
    for copy, cond in pending:
        guarded(cond, copy.wait_send)


def spread(kv_in, rows_in, pack, st_in, dec_s, dec_o):
    vm = pl.BlockSpec(memory_space=VM)
    sm = pl.BlockSpec(memory_space=pltpu.SMEM)
    width = rows_in.shape[-1]
    dma = pltpu.SemaphoreType.DMA
    return pl.pallas_call(
        spread_kernel,
        out_shape=(
            jax.ShapeDtypeStruct((4, 33, 128, 128), BF16),
            jax.ShapeDtypeStruct((STEPS, ROWS, width), BF16),
            jax.ShapeDtypeStruct((CORES, 128, 128), BF16),
        ),
        in_specs=[vm, vm, vm, vm, sm, sm],
        out_specs=(vm, vm, vm),
        scratch_shapes=[
            VM((CORES, PAD, width), BF16),
            VM((CORES, 128, 128), BF16),
            VM((128, 128), BF16),
            VM((STEPS, 128, 128), BF16),
            VM((CORES, 128, 128), BF16),
            VM((CORES, 128, 128), F32),
            VM((128, 128), F32),
            dma((4,)), dma((4,)), dma((5, 4)), dma((4, 4)), dma((5,)), dma((4,)),
            dma((4, 4)), dma((4, 4)),
            dma((8,)), dma((8,)), dma((3,)), dma((3,)), dma((4,)), dma((4,)),
            dma((8,)), dma((8,)), dma((8,)), dma((8,)), dma((8,)), dma((8,)),
        ],
        compiler_params=pltpu.CompilerParams(
            collective_id=1, has_side_effects=True, vmem_limit_bytes=40 << 20
        ),
        cost_estimate=pl.CostEstimate(
            flops=30_000_000_000, bytes_accessed=20_000_000, transcendentals=0
        ),
        name="spread",
    )(kv_in, rows_in, pack, st_in, dec_s, dec_o)


def attention_kernel(q, kv, out):
    s = lax.axis_index("seq")
    e = lax.axis_index("exp")
    row = lax.broadcasted_iota(jnp.int32, (128, 1024), 0)
    col = lax.broadcasted_iota(jnp.int32, (128, 1024), 1)
    place = col // 128
    inside = lax.rem(col, 128)
    far_ok = s >= 4
    near = (place < e) | ((place == e) & (inside <= row)) | ((place > e) & far_ok)
    vrow = lax.broadcasted_iota(jnp.int32, (1024, 128), 0) // 128
    v_ok = (vrow <= e) | far_ok
    last = (lax.broadcasted_iota(jnp.int32, (128, 128), 1) > lax.broadcasted_iota(
        jnp.int32, (128, 128), 0)) & far_ok
    scale = 1.0 / math.sqrt(128)

    def chunk(carried, query, keys, values, mask):
        top, total, acc = carried
        scores = lax.dot_general(
            query, keys, (((1,), (1,)), ((), ())), preferred_element_type=F32
        ) * scale
        if mask is not None:
            scores = jnp.where(mask, scores, -1e30)
        new = jnp.maximum(top, jnp.max(scores, axis=1, keepdims=True))
        weights = jnp.exp(scores - new)
        if mask is not None:
            weights = jnp.where(mask, weights, 0.0)
        factor = jnp.exp(top - new)
        total = total * factor + jnp.sum(weights, axis=1, keepdims=True)
        acc = acc * factor + jnp.dot(
            weights.astype(BF16), values, preferred_element_type=F32
        )
        return new, total, acc

    def one_head(h, _):
        group = h // 4
        query = q[h]
        k0 = kv[group, 0:8].reshape(1024, 128)
        v0 = jnp.where(v_ok, kv[2 + group, 0:8].reshape(1024, 128), jnp.zeros((), BF16))
        state = (
            jnp.full((128, 1), -1e30, F32),
            jnp.zeros((128, 1), F32),
            jnp.zeros((128, 128), F32),
        )
        state = chunk(state, query, k0, v0, near)
        vl = jnp.where(far_ok, kv[2 + group, 32], jnp.zeros((), BF16))
        state = chunk(state, query, kv[group, 32], vl, last)

        def more(k, carried):
            keys = kv[group, pl.ds(k * 8, 8)].reshape(1024, 128)
            values = kv[2 + group, pl.ds(k * 8, 8)].reshape(1024, 128)
            return chunk(carried, query, keys, values, None)

        _, total, acc = lax.fori_loop(1, jnp.minimum(s, 3) + 1, more, state)
        out[h] = (acc / total).astype(BF16)
        return 0

    lax.fori_loop(0, 8, one_head, 0)


def attention(q, kv):
    vm = pl.BlockSpec(memory_space=VM)
    return pl.pallas_call(
        attention_kernel,
        out_shape=jax.ShapeDtypeStruct((8, 128, 128), BF16),
        in_specs=[vm, vm],
        out_specs=vm,
        compiler_params=pltpu.CompilerParams(vmem_limit_bytes=40 << 20),
        cost_estimate=pl.CostEstimate(
            flops=10_000_000_000, bytes_accessed=5_000_000, transcendentals=4_000_000
        ),
        name="attend",
    )(q, kv)


def summary_kernel(inputs, inflow, weight_in, out):
    for pair in range(8):
        vectors = inflow[:, 128 * (pair // 4):128 * (pair // 4) + 128].astype(F32)
        both = inputs[:, 128 * pair:128 * pair + 128]
        for h in range(2):
            head = 2 * pair + h
            weighted = (weight_in[:, head:head + 1] * vectors).astype(BF16)
            res = lax.dot_general(
                both, weighted, (((0,), (0,)), ((), ())), preferred_element_type=F32
            )
            out[pair, 64 * h:64 * h + 64, :] = res[64 * h:64 * h + 64].astype(BF16)


def summary(inputs, inflow, weight_in):
    vm = pl.BlockSpec(memory_space=VM)
    return pl.pallas_call(
        summary_kernel,
        out_shape=jax.ShapeDtypeStruct((8, 128, 128), BF16),
        in_specs=[vm] * 3,
        out_specs=vm,
        cost_estimate=pl.CostEstimate(
            flops=1_000_000_000, bytes_accessed=1_000_000, transcendentals=0
        ),
        name="summary",
    )(inputs, inflow, weight_in)


def state_kernel(inputs, gate, inflow, readout, cum, cum_t, step_t, skip, gain, ent, out, gated):
    low = lax.broadcasted_iota(jnp.int32, (128, 128), 1) < 64
    causal = lax.broadcasted_iota(jnp.int32, (128, 128), 0) >= lax.broadcasted_iota(
        jnp.int32, (128, 128), 1)
    for g in range(2):
        cols = slice(128 * g, 128 * g + 128)
        read = readout[:, cols]
        rw = lax.dot_general(
            read, inflow[:, cols], (((1,), (1,)), ((), ())), preferred_element_type=F32
        )
        square = jnp.zeros((128, 1), F32)
        for p in range(4):
            pair = 4 * g + p
            at = slice(128 * pair, 128 * pair + 128)
            both = inputs[:, at]
            parts = []
            scales = []
            for h in range(2):
                head = 2 * pair + h
                own = cum[:, head:head + 1]
                gap = jnp.where(causal, own - cum_t[head:head + 1, :], 0.0)
                mixing = jnp.where(causal, jnp.exp(gap), 0.0) * rw * step_t[head:head + 1, :]
                parts.append(
                    jnp.dot(mixing.astype(BF16), both, preferred_element_type=F32)
                )
                scales.append(jnp.exp(own))
            intra = jnp.where(low, parts[0], parts[1])
            scale = jnp.where(low, scales[0], scales[1])
            inter = scale * lax.dot_general(
                read, ent[pair], (((1,), (1,)), ((), ())), preferred_element_type=F32
            )
            mixed = intra + inter + skip[:, at] * both.astype(F32)
            v = gate[:, at].astype(F32)
            value = mixed * (v / (1.0 + jnp.exp(-v)))
            gated[:, 128 * p:128 * p + 128] = value
            square = square + jnp.sum(value * value, axis=1, keepdims=True)
        inv = lax.rsqrt(square / 512.0 + EPSILON)
        wide = slice(512 * g, 512 * g + 512)
        out[:, wide] = (gated[...] * inv * gain[:, wide]).astype(BF16)


def state_out_of(inputs, gate, inflow, readout, cum, cum_t, step_t, skip, gain, ent):
    vm = pl.BlockSpec(memory_space=VM)
    return pl.pallas_call(
        state_kernel,
        out_shape=jax.ShapeDtypeStruct((128, 1024), BF16),
        in_specs=[vm] * 10,
        out_specs=vm,
        scratch_shapes=[VM((128, 512), F32)],
        cost_estimate=pl.CostEstimate(
            flops=4_000_000_000, bytes_accessed=2_000_000, transcendentals=400_000
        ),
        name="state",
    )(inputs, gate, inflow, readout, cum, cum_t, step_t, skip, gain, ent)


def gather_kernel(
    part, unpack, weigh, out,
    tx, rx, slots_tx, slots, mine_tx, mine,
    r_s, r_r, x_s, x_r, y_s, y_r,
):
    s = lax.axis_index("seq")
    e = lax.axis_index("exp")
    t = lax.axis_index("tp")
    nxt = lax.rem(s + 1, STEPS)
    prv = lax.rem(s + STEPS - 1, STEPS)
    greet(
        (
            ("exp", CORES, range(1, CORES)),
            ("seq", STEPS, (1, STEPS - 1)),
            ("tp", TPS, range(1, TPS)),
        )
    )
    pending = []
    width = part.shape[-1] // 4

    def columns(stream):
        return slice(width * stream, width * stream + width)

    def ring(stream, j):
        to = nxt if stream < 2 else prv
        return rcopy(
            tx.at[stream, j], rx.at[stream, j], r_s.at[stream, j], r_r.at[stream, j], {"seq": to}
        )

    def owner(stream, j):
        if stream < 2:
            return lax.rem(s + 2 * STEPS - 1 - j, STEPS)
        return lax.rem(s + 1 + j, STEPS)

    order = (0, 2, 1, 3)
    for j in range(STEPS - 1):
        for stream in order:
            q = owner(stream, j)
            value = part[q, :, columns(stream)]
            if j > 0:
                ring(stream, j - 1).wait_recv()
                value = (value.astype(F32) + rx[stream, j - 1].astype(F32)).astype(BF16)
            tx[stream, j] = value
            copy = ring(stream, j)
            copy.start()
            pending.append(copy)
    for stream in order:
        ring(stream, STEPS - 2).wait_recv()
        total = part[s, :, columns(stream)].astype(F32) + rx[stream, STEPS - 2].astype(F32)
        spaced = jnp.dot(unpack[...], total.astype(BF16), preferred_element_type=F32)
        slots_tx[:, :, columns(stream)] = spaced.astype(BF16).reshape(CORES, PAD, width)
    for d in range(1, CORES):
        to = lax.rem(e + d, CORES)
        copy = rcopy(slots_tx.at[to], slots.at[e], x_s.at[d], x_r.at[d], {"exp": to})
        copy.start()
        pending.append(copy)
    slots[pl.ds(e, 1)] = slots_tx[pl.ds(e, 1)]
    for d in range(1, CORES):
        frm = lax.rem(e + CORES - d, CORES)
        at = slots.at[frm]
        rcopy(at, at, x_s.at[d], x_r.at[d], {"exp": frm}).wait_recv()
    high = weigh[...].astype(BF16)
    rest = (weigh[...] - high.astype(F32)).astype(BF16)
    for quarter in range(TPS):
        at = slots[:, :, columns(quarter)].reshape(CORES * PAD, width)
        mine_tx[quarter] = (
            jnp.dot(high, at, preferred_element_type=F32)
            + jnp.dot(rest, at, preferred_element_type=F32)
        ).astype(BF16)
    for d in range(1, TPS):
        to = lax.rem(t + d, TPS)
        copy = rcopy(mine_tx.at[to], mine.at[d], y_s.at[d], y_r.at[d], {"tp": to})
        copy.start()
        pending.append(copy)
    total = mine_tx[t].astype(F32)
    for d in range(1, TPS):
        frm = lax.rem(t + TPS - d, TPS)
        at = mine.at[d]
        rcopy(at, at, y_s.at[d], y_r.at[d], {"tp": frm}).wait_recv()
        total = total + mine[d].astype(F32)
    out[...] = total.astype(BF16)
    for copy in pending:
        copy.wait_send()


def gathered(part, unpack, weigh):
    vm = pl.BlockSpec(memory_space=VM)
    width = part.shape[-1]
    q = width // 4
    dma = pltpu.SemaphoreType.DMA
    return pl.pallas_call(
        gather_kernel,
        out_shape=jax.ShapeDtypeStruct((128, q), BF16),
        in_specs=[vm] * 3,
        out_specs=vm,
        scratch_shapes=[
            VM((4, STEPS - 1, ROWS, q), BF16),
            VM((4, STEPS - 1, ROWS, q), BF16),
            VM((CORES, PAD, width), BF16),
            VM((CORES, PAD, width), BF16),
            VM((TPS, 128, q), BF16),
            VM((TPS, 128, q), BF16),
            dma((4, STEPS - 1)), dma((4, STEPS - 1)), dma((8,)), dma((8,)), dma((4,)), dma((4,)),
        ],
        compiler_params=pltpu.CompilerParams(
            collective_id=2, has_side_effects=True, vmem_limit_bytes=40 << 20
        ),
        name="collect",
    )(part, unpack, weigh)


def local(
    query_heads, key_heads, value_head_rows, state_input, state_gate, state_inflow,
    state_readout, step_size, log_decay, skip_scale, state_gain, hidden_in, mlp_gain,
    router_weight, expert_ids, slot_index, gate_up, down_proj,
):
    s = lax.axis_index("seq")
    e = lax.axis_index("exp")
    tp = lax.axis_index("tp")
    wide_gate_up = lax.all_gather(gate_up, "tp", axis=1, tiled=True)
    wide_down = lax.all_gather(down_proj, "tp", axis=1, tiled=True)

    hidden = hidden_in.astype(F32)
    mean_square = jnp.mean(hidden * hidden, axis=-1, keepdims=True)
    normed = (hidden * lax.rsqrt(mean_square + EPSILON) * mlp_gain).astype(BF16)
    gate_values = jax.nn.sigmoid(jnp.dot(normed, router_weight, preferred_element_type=F32))
    one_hot = expert_ids[..., None] == jnp.arange(EXPERTS, dtype=jnp.int32)
    chosen = jnp.sum(jnp.where(one_hot, gate_values[:, None, :], 0.0), axis=-1)
    mixing = chosen / jnp.sum(chosen, axis=1, keepdims=True)
    is_live = slot_index >= 0
    inside = slot_index - tp * QUARTER
    taken = is_live & (inside >= 0) & (inside < QUARTER)
    place = jnp.where(taken, expert_ids * PAD + inside, -1)
    hits = place[..., None] == jnp.arange(EXPERTS * PAD, dtype=jnp.int32)
    picker = jnp.any(hits, axis=1).astype(BF16)
    weigh = jnp.sum(jnp.where(hits, mixing[..., None], 0.0), axis=1)
    outgoing = lax.dot_general(
        picker, normed, (((0,), (0,)), ((), ())), preferred_element_type=F32
    ).astype(BF16).reshape(EXPERTS, PAD, -1)
    flat = jnp.arange(ROWS)
    pack = ((flat // QUARTER) * PAD + flat % QUARTER)[:, None] == jnp.arange(CORES * PAD)[None]
    pack = pack.astype(BF16)

    cum = jnp.cumsum(log_decay, axis=0)
    block_total = cum[-1]
    weight_in = jnp.exp(block_total[None] - cum) * step_size
    states = summary(state_input, state_inflow.reshape(128, 256), weight_in)
    totals = lax.all_gather(lax.all_gather(block_total, "exp"), "seq")
    mine = lax.dynamic_slice_in_dim(totals, 2 * e, 2, 2)
    dec_s = jnp.exp(lax.dynamic_index_in_dim(mine, s, 0, keepdims=False))
    dec_o = jnp.exp(jnp.sum(mine, axis=1))

    kv_in = jnp.concatenate(
        [jnp.transpose(key_heads, (1, 0, 2)), jnp.transpose(value_head_rows, (1, 0, 2))], axis=0
    )
    kv, rows, entering = spread(kv_in, outgoing, pack, states, dec_s, dec_o)

    heads = attention(jnp.transpose(query_heads, (1, 0, 2)), kv)
    window_out = jnp.transpose(heads, (1, 0, 2))
    state_out = state_out_of(
        state_input, state_gate, state_inflow.reshape(128, 256), state_readout.reshape(128, 256),
        cum, cum.T, step_size.T, jnp.repeat(skip_scale, 64)[None], state_gain[None], entering,
    )

    flat_rows = rows.reshape(STEPS * ROWS, -1)
    projected = jnp.einsum(
        "rd,fsd->srf", flat_rows, wide_gate_up[0], preferred_element_type=F32
    )
    hidden_units = (jax.nn.silu(projected[0]) * projected[1]).astype(BF16)
    part = jnp.dot(hidden_units, wide_down[0], preferred_element_type=F32).astype(BF16)
    routed_out = gathered(part.reshape(STEPS, ROWS, -1), pack.T, weigh)
    return window_out, state_out, routed_out


def solution(mesh):
    both = ("seq", "exp")
    placed = (
        P(both, "tp", None), P(both, "tp", None), P(both, "tp", None),
        P(both, "tp"), P(both, "tp"), P(both, "tp", None), P(both, "tp", None),
        P(both, "tp"), P(both, "tp"), P("tp"), P("tp"), P(both, None), P(), P(),
        P(both, None), P(both, None),
        P("exp", ("seq", "tp"), None, None), P("exp", ("seq", "tp"), None),
    )
    return jax.shard_map(
        local,
        mesh=mesh,
        in_specs=placed,
        out_specs=(P(both, "tp", None), P(both, "tp"), P(both, "tp")),
        check_vma=False,
    )
```

time: 393 us -> 217 us (0.55)
  the two profiles are of different devices: /device:TPU:128 before, /device:TPU:1 now
where the time goes in v1:
time: 217 us; the launch traced here: 216 us
  Pallas kernels  132 us (61%)
  blocking collectives  36.3 us (17%)
  matrix products  16.3 us (8%)
  between operations  14.4 us (7%)
  local copies, waits for them, and re-layouts  9.27 us (4%)
  waiting for transfers between devices  6.96 us (3%)
    pallas_call x1, Pallas kernels, gathered(): pl.pallas_call(gather_kernel, out_shape=jax.ShapeDtypeStruct((128, q), BF...  61.9 us
    pallas_call x1, Pallas kernels, spread(): pl.pallas_call(spread_kernel, out_shape=(jax.ShapeDtypeStruct((4, 33, 128...  57 us
    all_gather x2, blocking collectives, local(): totals = lax.all_gather(lax.all_gather(block_total, 'exp'), 'seq')  36.3 us
    dot_general x1, matrix products, local(): jnp.einsum('rd,fsd->srf', flat_rows, wide_gate_up[0], preferred_element_t...  9.25 us
    unnamed x46, local copies, waits for them, and re-layouts  7.68 us
    pallas_call x1, Pallas kernels, attention(): pl.pallas_call(attention_kernel, out_shape=jax.ShapeDtypeStruct((8, 128,...  6.63 us
    dot_general x1, matrix products, local(): jnp.dot(hidden_units, wide_down[0], preferred_element_type=F32).astype(BF16)  6.32 us
    all_gather x1, waiting for transfers between devices, local(): wide_down = lax.all_gather(down_proj, 'tp', axis=1, tiled=True)  6.25 us
  transfers between devices with their start and end apart: 2, of which 1 were waited for; matrix products, arithmetic and copies ran while one was open for 7% of the time, Pallas kernels for 32%

profile of v1, /device:TPU:1, one launch (start us, length us, event | category | flops | bytes accessed | tf_op | source)
XLA Modules:
  0.0 216.4 jit_solution(8725489551856540391)
XLA Ops:
  7.2 0.0 copy-start
  7.2 0.0 all-gather.5.cloned.1.call-start
  7.2 3.5 %copy.55 = bf16[1,224,2,2048]{3,1,2,0:T(8,128)(2,1)} copy(bf16[1,224,2,2048]{3,2,1,0:T(2,128)(2,1)} %param.34) | data formatting | bytes 3670016 | tf_op args[16]
  10.8 0.0 copy-start.14
  10.8 0.0 copy-start.10
  10.8 0.0 copy-start.11
  10.8 0.0 copy-start.12
  10.8 0.0 all-gather.5.cloned.1.call-update
  10.8 0.0 all-gather.7.cloned.1.call-start
  10.9 0.7 all-gather.7.cloned.1.call-update
  11.6 0.1 copy.50
  11.7 0.2 reduce_window_sum.11.cum
  11.9 0.7 copy.54
  12.6 0.0 copy-done.7
  12.6 0.0 copy-done.15
  12.6 0.0 copy-done.16
  12.7 0.1 fusion.21
  12.8 0.2 fusion.16
  13.0 0.1 fusion.23.pack
  13.1 0.6 copy.68
  13.7 0.0 copy-done.14
  13.7 0.1 copy.51
  13.8 11.9 %all-gather.1 = f32[8,1,16]{2,1,0:T(1,128)S(1)} all-gather(f32[1,1,16]{2,1,0:T(1,128)S(1)} %get-tuple-element.20), channel_id=1, replica_groups=mesh['seq'=8,'exp'=8,'tp'=4] {'exp'}, dimensions={0}, use_global_device_ids=true | all-gather | bytes 576 | tf_op jit(solution)/shard_map/all_gather | solution.py:589
  25.7 24.5 %all-gather = f32[64,16]{1,0:T(8,128)S(1)} all-gather(f32[8,16]{1,0:T(8,128)S(1)} %bitcast.61), channel_id=2, replica_groups=mesh['seq'=8,'exp'=8,'tp'=4] {'seq'}, dimensions={0}, use_global_device_ids=true | all-gather | bytes 4608 | tf_op jit(solution)/shard_map/all_gather | solution.py:589
  50.1 0.1 dynamic-slice_reduce_fusion
  50.2 0.1 dynamic-slice_exponential_fusion
  50.3 0.1 copy.60
  50.4 0.1 copy.53.dec_s
  50.6 0.6 exponential_multiply_fusion.weight_in
  51.2 0.4 convolution_convert_fusion
  51.6 2.3 %summary.1.st_in = bf16[8,128,128]{2,1,0:T(8,128)(2,1)} custom-call(bf16[128,1024]{1,0:T(8,128)(2,1)} %inputs.3, bf16[128,256]{1,0:T(8,128)(2,1)} %bitcast.58, f32[128,16]{1,0:T(8,128)} %exponential_multiply_fusion.weight_in), custom_call_target="tpu_custom_call" | custom-call | flops 1000000000 | bytes 1000000 | tf_op jit(solution)/shard_map/summary/pallas_call | solution.py:374
  53.9 1.0 copy-done.3
  54.9 57.0 %spread.1 = (bf16[4,33,128,128]{3,2,1,0:T(8,128)(2,1)S(1)}, bf16[8,80,2048]{2,1,0:T(8,128)(2,1)S(1)}, bf16[8,128,128]{2,1,0:T(8,128)(2,1)S(1)}) custom-call(bf16[4,128,128]{2,1,0:T(8,128)(2,1)S(1)} %pad_maximum_fusion.kv_in, bf16[8,16,2048]{2,1,0:T(8,128)(2,1)S(1)} %bitcast.50, bf16[80,128]{1,0:T(8,128)(2,1)S(1)} %fusion.23.pack, ...), custom_call_target="tpu_custom_call" | custom-call | flops 30000001024 | bytes 20000000 | tf_op jit(solution)/shard_map/spread/pallas_call | solution.py:253
  111.9 0.0 copy-start.9
  111.9 0.0 copy-start.17
  111.9 6.6 %attend.1 = bf16[8,128,128]{2,1,0:T(8,128)(2,1)S(1)} custom-call(bf16[8,128,128]{2,1,0:T(8,128)(2,1)S(1)} %bitcast.51, bf16[4,33,128,128]{3,2,1,0:T(8,128)(2,1)S(1)} %get-tuple-element.6.kv), custom_call_target="tpu_custom_call" | custom-call | flops 10000000000 | bytes 5000000 | tf_op jit(solution)/shard_map/attend/pallas_call | solution.py:346
  118.6 0.9 copy.56
  119.4 0.6 copy.67
  120.1 0.1 broadcast_in_dim.46
  120.1 0.7 broadcast_in_dim_reshape.3.skip
  120.8 0.3 fusion.15
  121.2 0.1 select_reduce_fusion.weigh
  121.3 3.8 %state.1 = bf16[128,1024]{1,0:T(8,128)(2,1)} custom-call(bf16[128,1024]{1,0:T(8,128)(2,1)} %inputs.3, bf16[128,1024]{1,0:T(8,128)(2,1)} %gate.1, bf16[128,256]{1,0:T(8,128)(2,1)} %bitcast.59, bf16[128,256]{1,0:T(8,128)(2,1)} %bitcast.60, f32[128,16]{1,0:T(8,128)} %copy-done.6, f32[16,128]{1,0:T(8,128)} %bitcast.63, f32[16,128]{1,0:T(8,128)} %bitcast.62, ...), custom_call_target="tpu_custom_call" | custom-call | flops 4000000000 | bytes 2000000 | tf_op jit(solution)/shard_map/state/pallas_call | solution.py:429
  125.1 9.2 %fusion.8 = f32[2,640,896]{2,1,0:T(8,128)} fusion(bf16[640,2048,1]{1,0,2:T(8,128)(2,1)S(1)} %bitcast.53, bf16[1,896,2,2048]{3,1,2,0:T(8,128)(2,1)} %all-gather.5.cloned.1.call-done), kind=kOutput, calls=%fused_computation.8 | convolution fusion | flops 4697620480 | bytes 14548992 | tf_op jit(solution)/shard_map/rd,fsd->srf/dot_general | solution.py:607
  134.4 6.2 %all-gather.7.cloned.1.call-done = bf16[1,896,2048]{2,1,0:T(8,128)(2,1)} async-done(((bf16[1,224,2048]{2,1,0:T(8,128)(2,1)}), bf16[1,896,2048]{2,1,0:T(8,128)(2,1)}) %all-gather.7.cloned.1.call-update) | async-done | bytes 3670032 | tf_op jit(solution)/shard_map/all_gather | solution.py:562
  140.6 6.3 %fusion.4 = bf16[640,2048]{1,0:T(8,128)(2,1)S(1)} fusion(bf16[1,896,2048]{2,1,0:T(8,128)(2,1)} %all-gather.7.cloned.1.call-done, f32[2,640,896]{2,1,0:T(8,128)} %fusion.8), kind=kOutput, calls=%fused_computation.4 | convolution fusion | flops 2353561600 | bytes 10878976 | tf_op jit(solution)/shard_map/dot_general | solution.py:611
  147.0 61.9 %collect.1 = bf16[128,512]{1,0:T(8,128)(2,1)S(1)} custom-call(bf16[8,80,2048]{2,1,0:T(8,128)(2,1)S(1)} %bitcast.49, bf16[128,80]{1,0:T(8,128)(2,1)S(1)} %fusion.22.unpack, f32[128,128]{1,0:T(8,128)S(1)} %select_reduce_fusion.weigh), custom_call_target="tpu_custom_call" | custom-call | tf_op jit(solution)/shard_map/collect/pallas_call | solution.py:532
  208.9 0.7 copy.70
  (36 shorter events, 0.2 us)
Async XLA Ops:
  7.2 113.6 %copy-start = (bf16[2048,8]{0,1:T(8,128)(2,1)S(1)}, bf16[2048,8]{0,1:T(8,128)(2,1)}, u32[]{:S(2)}) copy-start(bf16[2048,8]{0,1:T(8,128)(2,1)} %param.31) | copy-start | bytes 98308
  7.2 4.4 %copy-start.13 = (f32[128,16]{0,1:T(8,128)S(1)}, f32[128,16]{0,1:T(8,128)}, u32[]{:S(2)}) copy-start(f32[128,16]{0,1:T(8,128)} %param.26) | copy-start | bytes 24580
  7.2 5.4 %copy-start.7 = (bf16[128,8,128]{2,1,0:T(8,128)(2,1)S(1)}, bf16[128,8,128]{2,1,0:T(8,128)(2,1)}, u32[]{:S(2)}) copy-start(bf16[128,8,128]{2,1,0:T(8,128)(2,1)} %param.18) | copy-start | bytes 786436
  7.2 117.9 %all-gather.5.cloned.1.call-start = ((), (), s32[]{:S(2)}) async-start(), calls=%async_computation | async-start | bytes 9175040 | tf_op jit(solution)/shard_map/all_gather | solution.py:561
  10.8 1.9 copy-start.15
  10.8 1.9 copy-start.16
  10.8 2.0 copy-start.5
  10.8 2.3 %copy-start.8 = (bf16[128,2,128]{2,1,0:T(2,128)(2,1)S(1)}, bf16[128,2,128]{2,1,0:T(2,128)(2,1)}, u32[]{:S(2)}) copy-start(bf16[128,2,128]{2,1,0:T(2,128)(2,1)} %param.23) | copy-start | bytes 196612
  10.8 2.9 %copy-start.14 = (f32[128,16]{0,1:T(8,128)S(1)}, f32[128,16]{0,1:T(8,128)}, u32[]{:S(2)}) copy-start(f32[128,16]{0,1:T(8,128)} %param.25) | copy-start | bytes 24580
  10.8 39.7 %copy-start.10 = (bf16[128,2,128]{2,1,0:T(2,128)(2,1)S(1)}, bf16[128,2,128]{2,1,0:T(2,128)(2,1)}, u32[]{:S(2)}) copy-start(bf16[128,2,128]{2,1,0:T(2,128)(2,1)} %param.20) | copy-start | bytes 196612
  10.8 39.7 %copy-start.11 = (bf16[128,2,128]{2,1,0:T(2,128)(2,1)S(1)}, bf16[128,2,128]{2,1,0:T(2,128)(2,1)}, u32[]{:S(2)}) copy-start(bf16[128,2,128]{2,1,0:T(2,128)(2,1)} %param.19) | copy-start | bytes 196612
  10.8 40.4 %copy-start.12 = (f32[2048]{0:T(1024)S(1)}, f32[2048]{0:T(1024)}, u32[]{:S(2)}) copy-start(f32[2048]{0:T(1024)} %param.30) | copy-start | bytes 24580
  10.8 129.8 %all-gather.7.cloned.1.call-start = ((), (), s32[]{:S(2)}) async-start(), calls=%async_computation.1 | async-start | bytes 4587520 | tf_op jit(solution)/shard_map/all_gather | solution.py:562
  11.9 42.0 %copy-start.6 = (f32[128,16]{1,0:T(8,128)}, f32[128,16]{1,0:T(8,128)S(1)}, u32[]{:S(2)}) copy-start(f32[128,16]{1,0:T(8,128)S(1)} %reduce_window_sum.11.cum) | copy-start | bytes 24580
  53.9 1.0 copy-start.3
  111.9 6.7 %copy-start.1 = (bf16[8,80,2048]{2,1,0:T(8,128)(2,1)}, bf16[8,80,2048]{2,1,0:T(8,128)(2,1)S(1)}, u32[]{:S(2)}) copy-start(bf16[8,80,2048]{2,1,0:T(8,128)(2,1)S(1)} %get-tuple-element.8) | copy-start | bytes 7864324
  111.9 6.7 %copy-start.4 = (bf16[8,128,128]{2,1,0:T(8,128)(2,1)}, bf16[8,128,128]{2,1,0:T(8,128)(2,1)S(1)}, u32[]{:S(2)}) copy-start(bf16[8,128,128]{2,1,0:T(8,128)(2,1)S(1)} %get-tuple-element.7.ent) | copy-start | bytes 786436
  111.9 7.6 %copy-start.9 = (bf16[128,2,128]{2,1,0:T(2,128)(2,1)S(1)}, bf16[128,2,128]{2,1,0:T(2,128)(2,1)}, u32[]{:S(2)}) copy-start(bf16[128,2,128]{2,1,0:T(2,128)(2,1)} %param.24) | copy-start | bytes 196612
  111.9 8.2 %copy-start.17 = (f32[16]{0:T(128)S(1)}, f32[16]{0:T(128)}, u32[]{:S(2)}) copy-start(f32[16]{0:T(128)} %param.27) | copy-start | bytes 196
  121.3 3.8 %copy-start.2 = (bf16[8,80,2048]{2,1,0:T(8,128)(2,1)S(1)}, bf16[8,80,2048]{2,1,0:T(8,128)(2,1)}, u32[]{:S(2)}) copy-start(bf16[8,80,2048]{2,1,0:T(8,128)(2,1)} %copy-done.1) | copy-start | bytes 7864324
Sparse Core Ops, SparseCore 0:
  11.0 80.5 all-gather.4
  93.4 47.2 all-gather.6

commit v2 on v1

v2 whole, which is shorter than its diff:
```python
import functools
import math

import jax
import jax.numpy as jnp
from jax import lax
from jax.experimental import pallas as pl
from jax.experimental.pallas import tpu as pltpu
from jax.sharding import PartitionSpec as P

EXPERTS = 8
CAP = 40
STEPS = 8
CORES = 8
TPS = 4
QUARTER = 10
PAD = 16
ROWS = 80
UNITS = 448
HALF = 112
EPSILON = 1e-05
VM = pltpu.VMEM
MESH = pl.DeviceIdType.MESH
F32 = jnp.float32
BF16 = jnp.bfloat16


def rcopy(src, dst, ss, rs, dev):
    return pltpu.make_async_remote_copy(
        src_ref=src, dst_ref=dst, send_sem=ss, recv_sem=rs, device_id=dev, device_id_type=MESH
    )


def guarded(cond, fn):
    if cond is True:
        fn()
    else:
        pl.when(cond)(fn)


def greet(groups):
    barrier = pltpu.get_barrier_semaphore()
    count = 0
    for axis, size, shifts in groups:
        me = lax.axis_index(axis)
        for d in shifts:
            pl.semaphore_signal(
                barrier, inc=1, device_id={axis: lax.rem(me + d, size)}, device_id_type=MESH
            )
            count += 1
    pl.semaphore_wait(barrier, count)


def attend_body(s, e, q, kv, out):
    row = lax.rem(lax.broadcasted_iota(jnp.int32, (512, 1024), 0), 128)
    col = lax.broadcasted_iota(jnp.int32, (512, 1024), 1)
    place = col // 128
    inside = lax.rem(col, 128)
    far_ok = s >= 4
    near = (place < e) | ((place == e) & (inside <= row)) | ((place > e) & far_ok)
    vrow = lax.broadcasted_iota(jnp.int32, (1024, 128), 0) // 128
    v_ok = (vrow <= e) | far_ok
    last = (
        lax.broadcasted_iota(jnp.int32, (512, 128), 1)
        > lax.rem(lax.broadcasted_iota(jnp.int32, (512, 128), 0), 128)
    ) & far_ok
    scale = 1.0 / math.sqrt(128) * math.log2(math.e)

    def chunk(carried, query, keys, values, mask):
        top, total, acc = carried
        scores = lax.dot_general(
            query, keys, (((1,), (1,)), ((), ())), preferred_element_type=F32
        )
        if mask is not None:
            scores = jnp.where(mask, scores, -1e30)
        new = jnp.maximum(top, jnp.max(scores, axis=1, keepdims=True))
        weights = jnp.exp2((scores - new) * scale)
        if mask is not None:
            weights = jnp.where(mask, weights, 0.0)
        factor = jnp.exp2((top - new) * scale)
        total = total * factor + jnp.sum(weights, axis=1, keepdims=True)
        acc = acc * factor + jnp.dot(
            weights.astype(BF16), values, preferred_element_type=F32
        )
        return new, total, acc

    def one_group(group, _):
        query = q[group]
        k0 = kv[group, 0:8].reshape(1024, 128)
        v0 = jnp.where(v_ok, kv[2 + group, 0:8].reshape(1024, 128), jnp.zeros((), BF16))
        state = (
            jnp.full((512, 1), -1e30, F32),
            jnp.zeros((512, 1), F32),
            jnp.zeros((512, 128), F32),
        )
        state = chunk(state, query, k0, v0, near)
        vl = jnp.where(far_ok, kv[2 + group, 32], jnp.zeros((), BF16))
        state = chunk(state, query, kv[group, 32], vl, last)

        def more(k, carried):
            keys = kv[group, pl.ds(k * 8, 8)].reshape(1024, 128)
            values = kv[2 + group, pl.ds(k * 8, 8)].reshape(1024, 128)
            return chunk(carried, query, keys, values, None)

        _, total, acc = lax.fori_loop(1, jnp.minimum(s, 3) + 1, more, state)
        out[group] = (acc / total).astype(BF16)
        return 0

    lax.fori_loop(0, 2, one_group, 0)


def spread_kernel(
    kv_in, rows_in, pack, st_in, dec_in, gu_in, dn_in, q,
    inputs, gate, inflow, readout, cum, cum_t, step_t, skip, gain,
    heads, state_out, h_all, h_oth, dn,
    gu, kv, rows, ent, disp, st_rx, dec_rx, t_tx, t_rx, td_tx, td_rx, ent_tx, inner, carry, gated,
    l_s, g_s, g_r, n_s, n_r, h_s, h_r,
    z_s, z_r, x_s, x_r, p_s, p_r, f_s, f_r,
    d_s, d_r, rf_s, rf_r, rb_s, rb_r, sa_s, sa_r, da_s, da_r, st_s, st_r, sd_s, sd_r, se_s, se_r,
):
    s = lax.axis_index("seq")
    e = lax.axis_index("exp")
    t = lax.axis_index("tp")
    x = e // 2
    c = lax.rem(e, 2)
    partner = e + 1 - 2 * c
    nxt = lax.rem(s + 1, STEPS)
    prv = lax.rem(s + STEPS - 1, STEPS)
    odd = lax.rem(t, 2)
    to_a = {"tp": t + 1 - 2 * odd}
    to_b = {"tp": lax.rem(t + 3 + 2 * odd, TPS)}
    to_mate = {"tp": lax.rem(t + 2, TPS)}
    greet(
        (
            ("tp", TPS, range(1, TPS)),
            ("exp", CORES, range(1, CORES)),
            ("seq", STEPS, range(1, STEPS)),
        )
    )
    pending = []

    def send(copy, cond=True):
        guarded(cond, copy.start)
        pending.append((copy, cond))

    def slot_of(k):
        return 32 if k == 4 else k * 8 + e

    def block(k):
        return kv_in if k == 0 else kv.at[:, slot_of(k)]

    def kv_hop(k):
        return rcopy(
            block(k - 1), kv.at[:, slot_of(k)], z_s.at[k - 1], z_r.at[k - 1], {"seq": nxt}
        )

    def kv_across(g, k):
        for dx in range(1, 4):
            tx = lax.rem(x + dx, 4)
            if k == 0:
                cond = tx > x
            elif k == 4:
                cond = (tx < x) & (s >= 4)
            else:
                cond = s >= k
            send(
                rcopy(
                    block(k), kv.at[:, g * 8 + e], x_s.at[k, dx], x_r.at[g, dx],
                    {"exp": 2 * tx + c},
                ),
                cond,
            )
        if k == 0:
            cond = c == 0
        elif k == 4:
            cond = (c == 1) & (s >= 4)
        else:
            cond = s >= k
        send(
            rcopy(block(k), kv.at[:, g * 8 + e], p_s.at[k], p_r.at[g], {"exp": partner}), cond
        )

    def kv_forward(g):
        for dx in range(1, 4):
            sx = lax.rem(x + 4 - dx, 4)
            cond = ((sx < x) | (s >= 4)) if g == 0 else s >= g
            slot = kv.at[:, g * 8 + 2 * sx + c]
            arrived = rcopy(slot, slot, x_s.at[g, dx], x_r.at[g, dx], {"exp": 2 * sx + c})
            onward = rcopy(slot, slot, f_s.at[g, dx], f_r.at[g, dx], {"exp": partner})

            def pass_on(arrived=arrived, onward=onward):
                arrived.wait_recv()
                onward.start()

            guarded(cond, pass_on)
            pending.append((onward, cond))

    def kv_finish(g):
        slot = kv.at[:, g * 8 + partner]
        cond = ((c == 1) | (s >= 4)) if g == 0 else s >= g
        guarded(cond, rcopy(slot, slot, p_s.at[g], p_r.at[g], {"exp": partner}).wait_recv)
        for dx in range(1, 4):
            sx = lax.rem(x + 4 - dx, 4)
            cond = ((sx < x) | (s >= 4)) if g == 0 else s >= g
            slot = kv.at[:, g * 8 + 2 * sx + 1 - c]
            guarded(
                cond, rcopy(slot, slot, f_s.at[g, dx], f_r.at[g, dx], {"exp": partner}).wait_recv
            )

    def kv_arrive(k):
        slot = kv.at[:, slot_of(k)]
        guarded(
            s >= k, rcopy(slot, slot, z_s.at[k - 1], z_r.at[k - 1], {"seq": prv}).wait_recv
        )
        if k < 4:
            send(kv_hop(k + 1), (s >= k) & (s < STEPS - 1))
        kv_across(0 if k == 4 else k, k)

    for d in range(1, CORES):
        to = lax.rem(e + d, CORES)
        send(rcopy(rows_in.at[to], disp.at[e], d_s.at[d], d_r.at[d], {"exp": to}))
    first, second = pl.ds(0, HALF), pl.ds(HALF, HALF)
    third, fourth = pl.ds(2 * HALF, HALF), pl.ds(3 * HALF, HALF)
    send(rcopy(gu_in.at[:, first], gu.at[:, third], g_s.at[0], g_r.at[0], to_a))
    send(rcopy(gu_in.at[:, second], gu.at[:, fourth], g_s.at[1], g_r.at[1], to_b))
    send(kv_hop(1), s < STEPS - 1)
    for d in range(1, CORES):
        to = lax.rem(e + d, CORES)
        send(rcopy(st_in.at[to], st_rx.at[e], sa_s.at[d], sa_r.at[d], {"exp": to}))
        send(rcopy(dec_in.at[to], dec_rx.at[e], da_s.at[d], da_r.at[d], {"exp": to}))
    kv_across(0, 0)
    send(rcopy(dn_in.at[first], dn.at[0, third], n_s.at[0], n_r.at[0], to_a))
    send(rcopy(dn_in.at[second], dn.at[0, fourth], n_s.at[1], n_r.at[1], to_b))
    send(rcopy(dn_in.at[second], dn.at[1, fourth], n_s.at[2], n_r.at[2], to_a))
    send(rcopy(dn_in.at[first], dn.at[1, third], n_s.at[3], n_r.at[3], to_b))
    own_gu = pltpu.make_async_copy(gu_in, gu.at[:, pl.ds(0, 2 * HALF)], l_s.at[0])
    own_dn = pltpu.make_async_copy(dn_in, dn.at[0, pl.ds(0, 2 * HALF)], l_s.at[1])
    own_gu.start()
    own_dn.start()
    kv[:, pl.ds(e, 1)] = kv_in[...][:, None]
    disp[pl.ds(e, 1)] = rows_in[pl.ds(e, 1)]
    st_rx[pl.ds(e, 1)] = st_in[pl.ds(e, 1)]
    dec_rx[pl.ds(e, 1)] = dec_in[pl.ds(e, 1)]
    h_all[...] = jnp.zeros_like(h_all)
    td_tx[...] = jnp.zeros_like(td_tx)

    kv_arrive(1)
    for d in range(1, CORES):
        frm = lax.rem(e + CORES - d, CORES)
        rcopy(disp.at[frm], disp.at[frm], d_s.at[d], d_r.at[d], {"exp": frm}).wait_recv()
    packed = jnp.dot(
        pack[...], disp[...].reshape(CORES * 2 * PAD, -1), preferred_element_type=F32
    ).astype(BF16)
    rows[pl.ds(s, 1)] = packed.reshape(1, 2, ROWS, -1)

    def rows_up(j, i):
        at = rows.at[lax.rem(s + STEPS - j, STEPS), i]
        return rcopy(at, at, rf_s.at[j, i], rf_r.at[j, i], {"seq": nxt})

    def rows_down(j, i):
        at = rows.at[lax.rem(s + j, STEPS), i]
        return rcopy(at, at, rb_s.at[j, i], rb_r.at[j, i], {"seq": prv})

    def rows_up_arrived(j, i):
        at = rows.at[lax.rem(s + STEPS - 1 - j, STEPS), i]
        return rcopy(at, at, rf_s.at[j, i], rf_r.at[j, i], {"seq": prv})

    def rows_down_arrived(j, i):
        at = rows.at[lax.rem(s + 1 + j, STEPS), i]
        return rcopy(at, at, rb_s.at[j, i], rb_r.at[j, i], {"seq": nxt})

    for i in range(2):
        send(rows_down(0, i))
        send(rows_up(0, i))
    kv_arrive(2)

    for d in range(1, CORES):
        frm = lax.rem(e + CORES - d, CORES)
        rcopy(st_rx.at[frm], st_rx.at[frm], sa_s.at[d], sa_r.at[d], {"exp": frm}).wait_recv()
        rcopy(dec_rx.at[frm], dec_rx.at[frm], da_s.at[d], da_r.at[d], {"exp": frm}).wait_recv()
    for h in range(2):
        part = slice(64 * h, 64 * h + 64)
        run = jnp.zeros((64, 128), F32)
        whole = jnp.ones((1, 128), F32)
        for k in range(CORES):
            inner[k, part, :] = run
            decay = dec_rx[k, h:h + 1, :]
            run = run * decay + st_rx[k, part, :].astype(F32)
            whole = whole * decay
        t_tx[part, :] = run.astype(BF16)
        td_tx[h:h + 1, :] = whole
    for d in range(1, STEPS):
        to = lax.rem(s + d, STEPS)
        send(rcopy(t_tx, t_rx.at[s], st_s.at[d], st_r.at[d], {"seq": to}), s + d < STEPS)
        send(rcopy(td_tx, td_rx.at[s], sd_s.at[d], sd_r.at[d], {"seq": to}), s + d < STEPS)

    kv_arrive(3)
    for d in range(1, STEPS):
        frm = lax.rem(s + STEPS - d, STEPS)
        at = t_rx.at[frm]
        guarded(d <= s, rcopy(at, at, st_s.at[d], st_r.at[d], {"seq": frm}).wait_recv)
        at = td_rx.at[frm]
        guarded(d <= s, rcopy(at, at, sd_s.at[d], sd_r.at[d], {"seq": frm}).wait_recv)
    carry[...] = jnp.zeros_like(carry)
    for k in range(STEPS - 1):

        def fold(k=k):
            for h in range(2):
                part = slice(64 * h, 64 * h + 64)
                carry[part, :] = carry[part, :] * td_rx[k, h:h + 1, :] + t_rx[
                    k, part, :
                ].astype(F32)

        pl.when(k < s)(fold)
    for h in range(2):
        part = slice(64 * h, 64 * h + 64)
        moved = carry[part, :]
        for k in range(CORES):
            ent_tx[k, part, :] = (inner[k, part, :] + moved).astype(BF16)
            moved = moved * dec_rx[k, h:h + 1, :]
    for d in range(1, CORES):
        to = lax.rem(e + d, CORES)
        send(rcopy(ent_tx.at[to], ent.at[e], se_s.at[d], se_r.at[d], {"exp": to}))
    ent[pl.ds(e, 1)] = ent_tx[pl.ds(e, 1)]
    kv_arrive(4)

    def to_mate_copy(b):
        return rcopy(h_all.at[b, 1 - t // 2], h_oth.at[b], h_s.at[b], h_r.at[b], to_mate)

    def expert_in(b):
        flat = rows[b].reshape(2 * ROWS, -1)
        nt = (((1,), (1,)), ((), ()))
        gated_part = lax.dot_general(flat, gu[0], nt, preferred_element_type=F32)
        up_part = lax.dot_general(flat, gu[1], nt, preferred_element_type=F32)
        units = (gated_part / (1.0 + jnp.exp(-gated_part)) * up_part).astype(BF16)
        h_all[b, 0, :, 0:UNITS] = units[0:ROWS]
        h_all[b, 1, :, 0:UNITS] = units[ROWS:2 * ROWS]
        to_mate_copy(b).start()

    def expert_pair(j):
        def one(i, _):
            expert_in(lax.rem(s + STEPS + (2 * i - 1) * (j + 1), STEPS))
            return 0

        lax.fori_loop(0, 2, one, 0)

    def rows_step(j):
        for i in range(2):
            rows_down_arrived(j, i).wait_recv()
            if j < 3:
                send(rows_down(j + 1, i))
            if j < 3:
                rows_up_arrived(j, i).wait_recv()
                if j < 2:
                    send(rows_up(j + 1, i))

    kv_forward(1)
    own_gu.wait()
    arrive_a = gu.at[:, third]
    arrive_b = gu.at[:, fourth]
    rcopy(arrive_a, arrive_a, g_s.at[0], g_r.at[0], to_a).wait_recv()
    rcopy(arrive_b, arrive_b, g_s.at[1], g_r.at[1], to_b).wait_recv()
    expert_in(s)
    rows_step(0)
    kv_forward(2)
    kv_forward(3)
    expert_pair(0)
    kv_forward(0)
    rows_step(1)
    at = dn.at[0, third]
    rcopy(at, at, n_s.at[0], n_r.at[0], to_a).wait_recv()
    send(rcopy(at, dn.at[1, first], n_s.at[4], n_r.at[4], to_b))
    at = dn.at[0, fourth]
    rcopy(at, at, n_s.at[1], n_r.at[1], to_b).wait_recv()
    send(rcopy(at, dn.at[1, second], n_s.at[5], n_r.at[5], to_a))
    expert_pair(1)
    rows_step(2)
    for g in (1, 2, 3, 0):
        kv_finish(g)
    attend_body(s, e, q, kv, heads)
    for d in range(1, CORES):
        frm = lax.rem(e + CORES - d, CORES)
        rcopy(ent.at[frm], ent.at[frm], se_s.at[d], se_r.at[d], {"exp": frm}).wait_recv()
    state_body(
        inputs, gate, inflow, readout, cum, cum_t, step_t, skip, gain, ent, state_out, gated
    )
    expert_pair(2)
    rows_step(3)
    expert_in(lax.rem(s + 4, STEPS))
    own_dn.wait()
    for n, at, dev in (
        (2, dn.at[1, fourth], to_a),
        (3, dn.at[1, third], to_b),
        (4, dn.at[1, first], to_b),
        (5, dn.at[1, second], to_a),
    ):
        rcopy(at, at, n_s.at[n], n_r.at[n], dev).wait_recv()
    for b in range(STEPS):
        to_mate_copy(b).wait()
    for copy, cond in pending:
        guarded(cond, copy.wait_send)


def spread(*operands):
    vm = pl.BlockSpec(memory_space=VM)
    hbm = pl.BlockSpec(memory_space=pl.ANY)
    width = operands[1].shape[-1]
    dma = pltpu.SemaphoreType.DMA
    return pl.pallas_call(
        spread_kernel,
        out_shape=(
            jax.ShapeDtypeStruct((2, 512, 128), BF16),
            jax.ShapeDtypeStruct((128, 1024), BF16),
            jax.ShapeDtypeStruct((STEPS, 2, ROWS, 512), BF16),
            jax.ShapeDtypeStruct((STEPS, ROWS, 512), BF16),
            jax.ShapeDtypeStruct((2, UNITS, width), BF16),
        ),
        in_specs=[vm] * 5 + [hbm] * 2 + [vm] * 10,
        out_specs=(vm,) * 5,
        scratch_shapes=[
            VM((2, UNITS, width), BF16),
            VM((4, 33, 128, 128), BF16),
            VM((STEPS, 2, ROWS, width), BF16),
            VM((CORES, 128, 128), BF16),
            VM((CORES, 2 * PAD, width), BF16),
            VM((CORES, 128, 128), BF16),
            VM((CORES, 8, 128), F32),
            VM((128, 128), BF16),
            VM((STEPS, 128, 128), BF16),
            VM((8, 128), F32),
            VM((STEPS, 8, 128), F32),
            VM((CORES, 128, 128), BF16),
            VM((CORES, 128, 128), F32),
            VM((128, 128), F32),
            VM((128, 512), F32),
            dma((2,)), dma((2,)), dma((2,)), dma((6,)), dma((6,)), dma((8,)), dma((8,)),
            dma((4,)), dma((4,)), dma((5, 4)), dma((4, 4)), dma((5,)), dma((4,)),
            dma((4, 4)), dma((4, 4)),
            dma((8,)), dma((8,)), dma((3, 2)), dma((3, 2)), dma((4, 2)), dma((4, 2)),
            dma((8,)), dma((8,)), dma((8,)), dma((8,)), dma((8,)), dma((8,)),
            dma((8,)), dma((8,)), dma((8,)), dma((8,)),
        ],
        compiler_params=pltpu.CompilerParams(
            collective_id=1, has_side_effects=True, vmem_limit_bytes=56 << 20
        ),
        name="spread",
    )(*operands)


def summary_kernel(inputs, inflow, weight_in, out):
    for pair in range(8):
        vectors = inflow[:, 128 * (pair // 4):128 * (pair // 4) + 128].astype(F32)
        both = inputs[:, 128 * pair:128 * pair + 128]
        for h in range(2):
            head = 2 * pair + h
            weighted = (weight_in[:, head:head + 1] * vectors).astype(BF16)
            res = lax.dot_general(
                both, weighted, (((0,), (0,)), ((), ())), preferred_element_type=F32
            )
            out[pair, 64 * h:64 * h + 64, :] = res[64 * h:64 * h + 64].astype(BF16)


def summary(inputs, inflow, weight_in):
    vm = pl.BlockSpec(memory_space=VM)
    return pl.pallas_call(
        summary_kernel,
        out_shape=jax.ShapeDtypeStruct((8, 128, 128), BF16),
        in_specs=[vm] * 3,
        out_specs=vm,
        cost_estimate=pl.CostEstimate(
            flops=1_000_000_000, bytes_accessed=1_000_000, transcendentals=0
        ),
        name="summary",
    )(inputs, inflow, weight_in)


def state_body(inputs, gate, inflow, readout, cum, cum_t, step_t, skip, gain, ent, out, gated):
    low = lax.broadcasted_iota(jnp.int32, (128, 128), 1) < 64
    causal = lax.broadcasted_iota(jnp.int32, (128, 128), 0) >= lax.broadcasted_iota(
        jnp.int32, (128, 128), 1)
    for g in range(2):
        cols = slice(128 * g, 128 * g + 128)
        read = readout[:, cols]
        rw = lax.dot_general(
            read, inflow[:, cols], (((1,), (1,)), ((), ())), preferred_element_type=F32
        )
        square = jnp.zeros((128, 1), F32)
        for p in range(4):
            pair = 4 * g + p
            at = slice(128 * pair, 128 * pair + 128)
            both = inputs[:, at]
            parts = []
            scales = []
            for h in range(2):
                head = 2 * pair + h
                own = cum[:, head:head + 1]
                gap = jnp.where(causal, own - cum_t[head:head + 1, :], 0.0)
                mixing = jnp.where(causal, jnp.exp(gap), 0.0) * rw * step_t[head:head + 1, :]
                parts.append(
                    jnp.dot(mixing.astype(BF16), both, preferred_element_type=F32)
                )
                scales.append(jnp.exp(own))
            intra = jnp.where(low, parts[0], parts[1])
            scale = jnp.where(low, scales[0], scales[1])
            inter = scale * lax.dot_general(
                read, ent[pair], (((1,), (1,)), ((), ())), preferred_element_type=F32
            )
            mixed = intra + inter + skip[:, at] * both.astype(F32)
            v = gate[:, at].astype(F32)
            value = mixed * (v / (1.0 + jnp.exp(-v)))
            gated[:, 128 * p:128 * p + 128] = value
            square = square + jnp.sum(value * value, axis=1, keepdims=True)
        inv = lax.rsqrt(square / 512.0 + EPSILON)
        wide = slice(512 * g, 512 * g + 512)
        out[:, wide] = (gated[...] * inv * gain[:, wide]).astype(BF16)


def gather_kernel(
    h_all, h_oth, dn, unpack, weigh, out,
    tx, rx, slots_tx, slots, mine_tx, mine,
    r_s, r_r, x_s, x_r, y_s, y_r,
):
    s = lax.axis_index("seq")
    e = lax.axis_index("exp")
    t = lax.axis_index("tp")
    nxt = lax.rem(s + 1, STEPS)
    prv = lax.rem(s + STEPS - 1, STEPS)
    greet(
        (
            ("exp", CORES, range(1, CORES)),
            ("seq", STEPS, (1, STEPS - 1)),
            ("tp", TPS, range(1, TPS)),
        )
    )
    pending = []
    width = dn.shape[-1] // 4

    def columns(stream):
        return slice(width * stream, width * stream + width)

    def ring(stream, j):
        to = nxt if stream < 2 else prv
        return rcopy(
            tx.at[stream, j], rx.at[stream, j], r_s.at[stream, j], r_r.at[stream, j], {"seq": to}
        )

    def owner(stream, j):
        if stream < 2:
            return lax.rem(s + 2 * STEPS - 1 - j, STEPS)
        return lax.rem(s + 1 + j, STEPS)

    def partial_of(q, half):
        cols = slice(2 * width * half, 2 * width * (half + 1))
        return jnp.dot(
            h_all[q, t // 2, :, 0:UNITS], dn[0, :, cols], preferred_element_type=F32
        ) + jnp.dot(h_oth[q, :, 0:UNITS], dn[1, :, cols], preferred_element_type=F32)

    for j in range(STEPS - 1):
        for half in range(2):
            value = partial_of(owner(2 * half, j), half)
            for i in range(2):
                stream = 2 * half + i
                piece = value[:, columns(i)]
                if j > 0:
                    ring(stream, j - 1).wait_recv()
                    piece = piece + rx[stream, j - 1].astype(F32)
                tx[stream, j] = piece.astype(BF16)
                copy = ring(stream, j)
                copy.start()
                pending.append(copy)
    for half in range(2):
        value = partial_of(s, half)
        for i in range(2):
            stream = 2 * half + i
            ring(stream, STEPS - 2).wait_recv()
            total = value[:, columns(i)] + rx[stream, STEPS - 2].astype(F32)
            spaced = jnp.dot(unpack[...], total.astype(BF16), preferred_element_type=F32)
            slots_tx[:, :, columns(stream)] = spaced.astype(BF16).reshape(CORES, PAD, width)
    for d in range(1, CORES):
        to = lax.rem(e + d, CORES)
        copy = rcopy(slots_tx.at[to], slots.at[e], x_s.at[d], x_r.at[d], {"exp": to})
        copy.start()
        pending.append(copy)
    slots[pl.ds(e, 1)] = slots_tx[pl.ds(e, 1)]
    for d in range(1, CORES):
        frm = lax.rem(e + CORES - d, CORES)
        at = slots.at[frm]
        rcopy(at, at, x_s.at[d], x_r.at[d], {"exp": frm}).wait_recv()
    high = weigh[...].astype(BF16)
    rest = (weigh[...] - high.astype(F32)).astype(BF16)
    for quarter in range(TPS):
        at = slots[:, :, columns(quarter)].reshape(CORES * PAD, width)
        mine_tx[quarter] = (
            jnp.dot(high, at, preferred_element_type=F32)
            + jnp.dot(rest, at, preferred_element_type=F32)
        ).astype(BF16)
    for d in range(1, TPS):
        to = lax.rem(t + d, TPS)
        copy = rcopy(mine_tx.at[to], mine.at[d], y_s.at[d], y_r.at[d], {"tp": to})
        copy.start()
        pending.append(copy)
    total = mine_tx[t].astype(F32)
    for d in range(1, TPS):
        frm = lax.rem(t + TPS - d, TPS)
        at = mine.at[d]
        rcopy(at, at, y_s.at[d], y_r.at[d], {"tp": frm}).wait_recv()
        total = total + mine[d].astype(F32)
    out[...] = total.astype(BF16)
    for copy in pending:
        copy.wait_send()


def gathered(h_all, h_oth, dn, unpack, weigh):
    vm = pl.BlockSpec(memory_space=VM)
    width = dn.shape[-1]
    q = width // 4
    dma = pltpu.SemaphoreType.DMA
    return pl.pallas_call(
        gather_kernel,
        out_shape=jax.ShapeDtypeStruct((128, q), BF16),
        in_specs=[vm] * 5,
        out_specs=vm,
        scratch_shapes=[
            VM((4, STEPS - 1, ROWS, q), BF16),
            VM((4, STEPS - 1, ROWS, q), BF16),
            VM((CORES, PAD, width), BF16),
            VM((CORES, PAD, width), BF16),
            VM((TPS, 128, q), BF16),
            VM((TPS, 128, q), BF16),
            dma((4, STEPS - 1)), dma((4, STEPS - 1)), dma((8,)), dma((8,)), dma((4,)), dma((4,)),
        ],
        compiler_params=pltpu.CompilerParams(
            collective_id=2, has_side_effects=True, vmem_limit_bytes=40 << 20
        ),
        name="collect",
    )(h_all, h_oth, dn, unpack, weigh)


def local(
    query_heads, key_heads, value_head_rows, state_input, state_gate, state_inflow,
    state_readout, step_size, log_decay, skip_scale, state_gain, hidden_in, mlp_gain,
    router_weight, expert_ids, slot_index, gate_up, down_proj,
):
    tp = lax.axis_index("tp")
    hidden = hidden_in.astype(F32)
    mean_square = jnp.mean(hidden * hidden, axis=-1, keepdims=True)
    normed = (hidden * lax.rsqrt(mean_square + EPSILON) * mlp_gain).astype(BF16)
    gate_values = jax.nn.sigmoid(jnp.dot(normed, router_weight, preferred_element_type=F32))
    one_hot = expert_ids[..., None] == jnp.arange(EXPERTS, dtype=jnp.int32)
    chosen = jnp.sum(jnp.where(one_hot, gate_values[:, None, :], 0.0), axis=-1)
    mixing = chosen / jnp.sum(chosen, axis=1, keepdims=True)
    is_live = slot_index >= 0
    quarter = slot_index // QUARTER
    inside = slot_index - quarter * QUARTER
    lanes = jnp.arange(EXPERTS * 2 * PAD, dtype=jnp.int32)
    near = is_live & (quarter % 2 == tp % 2)
    place = jnp.where(near, expert_ids * (2 * PAD) + (quarter // 2) * PAD + inside, -1)
    picker = jnp.any(place[..., None] == lanes, axis=1).astype(BF16)
    outgoing = lax.dot_general(
        picker, normed, (((0,), (0,)), ((), ())), preferred_element_type=F32
    ).astype(BF16).reshape(EXPERTS, 2 * PAD, -1)
    home = jnp.where(is_live & (quarter == tp), expert_ids * PAD + inside, -1)
    hits = home[..., None] == lanes[:EXPERTS * PAD]
    weigh = jnp.sum(jnp.where(hits, mixing[..., None], 0.0), axis=1)
    flat = jnp.arange(2 * ROWS)
    source = (flat % ROWS) // QUARTER * (2 * PAD) + flat // ROWS * PAD + flat % QUARTER
    pack = (source[:, None] == lanes[None]).astype(BF16)
    flat = jnp.arange(ROWS)
    unpack = (
        (flat // QUARTER * PAD + flat % QUARTER)[None] == jnp.arange(CORES * PAD)[:, None]
    ).astype(BF16)

    cum = jnp.cumsum(log_decay, axis=0)
    block_total = cum[-1]
    weight_in = jnp.exp(block_total[None] - cum) * step_size
    states = summary(state_input, state_inflow.reshape(128, 256), weight_in)
    decays = jnp.pad(jnp.exp(block_total).reshape(CORES, 2), ((0, 0), (0, 6)))
    decays = jnp.broadcast_to(decays[..., None], (CORES, 8, 128))
    kv_in = jnp.concatenate(
        [jnp.transpose(key_heads, (1, 0, 2)), jnp.transpose(value_head_rows, (1, 0, 2))], axis=0
    )
    heads, state_out, h_all, h_oth, down = spread(
        kv_in, outgoing, pack, states, decays,
        jnp.transpose(gate_up[0], (1, 0, 2)), down_proj[0],
        jnp.transpose(query_heads, (1, 0, 2)).reshape(2, 512, 128),
        state_input, state_gate, state_inflow.reshape(128, 256), state_readout.reshape(128, 256),
        cum, cum.T, step_size.T, jnp.repeat(skip_scale, 64)[None], state_gain[None],
    )
    window_out = jnp.transpose(heads.reshape(8, 128, 128), (1, 0, 2))
    routed_out = gathered(h_all, h_oth, down, unpack, weigh)
    return window_out, state_out, routed_out


def solution(mesh):
    both = ("seq", "exp")
    placed = (
        P(both, "tp", None), P(both, "tp", None), P(both, "tp", None),
        P(both, "tp"), P(both, "tp"), P(both, "tp", None), P(both, "tp", None),
        P(both, "tp"), P(both, "tp"), P("tp"), P("tp"), P(both, None), P(), P(),
        P(both, None), P(both, None),
        P("exp", ("seq", "tp"), None, None), P("exp", ("seq", "tp"), None),
    )
    return jax.shard_map(
        local,
        mesh=mesh,
        in_specs=placed,
        out_specs=(P(both, "tp", None), P(both, "tp"), P(both, "tp")),
        check_vma=False,
    )
```

time: 217 us -> 185 us (0.85)
  blocking collectives: 36.3 us -> 0 us
  Pallas kernels: 132 us -> 164 us
  between operations: 14.4 us -> 0.83 us
  matrix products: 16.3 us -> 2.85 us
  waiting for transfers between devices: 6.96 us -> 0 us
  local copies, waits for them, and re-layouts: 9.27 us -> 12.6 us
  other arithmetic: 1.51 us -> 4.53 us
    all_gather x2 -> x0, blocking collectives: 36.3 us -> none  [local(): totals = lax.all_gather(lax.all_gather(block_total, 'exp'), 'seq')]
    pallas_call x3 -> x1, Pallas kernels: 67.4 us -> 96.9 us  [spread(): pl.pallas_call(spread_kernel, out_shape=(jax.ShapeDtypeStruct((2, 512, 12...]
    dot_general x2 -> x0, matrix products: 15.6 us -> none  [the longest x1 9.25 us: local(): jnp.einsum('rd,fsd->srf', flat_rows, wide_gate_up[0], preferred_element_t...]
    all_gather x2 -> x0, waiting for transfers between devices: 6.25 us -> none  [the longest x1 6.25 us: local(): wide_down = lax.all_gather(down_proj, 'tp', axis=1, tiled=True)]
    pallas_call x1, Pallas kernels: 61.9 us -> 64.7 us  [gathered(): pl.pallas_call(gather_kernel, out_shape=jax.ShapeDtypeStruct((128, q), BF...]
    unnamed x46 -> x43, local copies, waits for them, and re-layouts: 7.68 us -> 8.05 us
  transfers between devices with their start and end apart: 2 -> 0, of which waited for: 1 -> 0; matrix products, arithmetic and copies ran while one was open for 7% -> 0% of each run, Pallas kernels for 32% -> 0%
where the time goes in v2:
time: 185 us
  Pallas kernels  164 us (89%)
  local copies, waits for them, and re-layouts  12.6 us (7%)
  other arithmetic  4.53 us (2%)
  matrix products  2.85 us (2%)
    pallas_call x1, Pallas kernels, spread(): pl.pallas_call(spread_kernel, out_shape=(jax.ShapeDtypeStruct((2, 512, 12...  96.9 us
    pallas_call x1, Pallas kernels, gathered(): pl.pallas_call(gather_kernel, out_shape=jax.ShapeDtypeStruct((128, q), BF...  64.7 us
    unnamed x43, local copies, waits for them, and re-layouts  8.05 us

profile of v2, /device:TPU:1, one launch (start us, length us, event | category | flops | bytes accessed | tf_op | source)
XLA Modules:
  0.0 184.8 jit_solution(9572898383232510242)
XLA Ops:
  0.6 0.0 copy-start
  0.6 0.0 copy-start.16
  0.7 0.0 copy-start.14
  0.7 0.0 copy-start.11
  0.7 0.0 copy-start.10
  0.7 0.8 and_select_fusion
  1.5 0.1 fusion.6
  1.6 1.2 fusion.3
  2.8 2.5 %convolution_convert_fusion = bf16[256,2048]{1,0:T(8,128)(2,1)} fusion(pred[128,256]{1,0:T(8,128)(4,1)S(1)} %fusion.6, bf16[128,2048]{1,0:T(8,128)(2,1)} %param.29, f32[2048]{0:T(1024)} %param.30, f32[128]{0:T(128)S(1)} %add_rsqrt_fusion), kind=kOutput, calls=%fused_computation | convolution fusion | flops 135790592 | bytes 1614336 | tf_op jit(solution)/shard_map/dot_general | solution.py:659
  5.4 0.0 copy-done.16
  5.4 0.1 copy.47
  5.5 0.2 reduce_window_sum.11.cum
  5.7 0.0 copy-done.14
  5.7 0.1 copy.48
  5.8 0.7 exponential_multiply_fusion.weight_in
  6.4 0.0 copy-done.11
  6.4 0.0 copy-done.10
  6.4 0.7 copy_bitcast_fusion.2
  7.1 2.4 %summary.1.st_in = bf16[8,128,128]{2,1,0:T(8,128)(2,1)} custom-call(bf16[128,1024]{1,0:T(8,128)(2,1)} %inputs.3, bf16[128,256]{1,0:T(8,128)(2,1)} %get-tuple-element.22.inflow, f32[128,16]{1,0:T(8,128)} %exponential_multiply_fusion.weight_in), custom_call_target="tpu_custom_call" | custom-call | flops 1000000000 | bytes 1000000 | tf_op jit(solution)/shard_map/summary/pallas_call | solution.py:465
  9.5 0.1 exp.15
  9.6 0.7 broadcast_in_dim.33.dec_in
  10.3 0.0 copy-done.6
  10.3 0.7 copy.51
  11.0 0.0 copy-done.12
  11.0 0.0 copy-done.13
  11.0 0.7 pad_maximum_fusion.kv_in
  11.7 0.0 copy-done.5
  11.7 2.0 %copy.61 = bf16[1,224,2,2048]{3,1,2,0:T(8,128)(2,1)} copy(bf16[1,224,2,2048]{3,2,1,0:T(2,128)(2,1)S(1)} %copy-done.5) | data formatting | bytes 3670016 | tf_op args[16]
  13.7 0.0 copy-done.7
  13.7 0.7 copy.50
  14.4 0.7 fusion.7.pack
  15.2 0.0 copy-done.18
  15.2 0.1 broadcast_in_dim.34
  15.2 0.7 broadcast_in_dim_reshape.3.skip
  15.9 96.9 %spread.1 = (bf16[2,512,128]{2,1,0:T(8,128)(2,1)}, bf16[128,1024]{1,0:T(8,128)(2,1)}, bf16[8,2,80,512]{3,2,1,0:T(8,128)(2,1)}, bf16[8,80,512]{2,1,0:T(8,128)(2,1)}, bf16[2,448,2048]{2,1,0:T(8,128)(2,1)}) custom-call(bf16[4,128,128]{2,1,0:T(8,128)(2,1)} %pad_maximum_fusion.kv_in, bf16[8,32,2048]{2,1,0:T(8,128)(2,1)} %bitcast.31, ...), custom_call_target="tpu_custom_call" | custom-call | tf_op jit(solution)/shard_map/spread/pallas_call | solution.py:409
  112.8 0.0 copy-done
  112.8 0.0 copy-done.4
  112.8 0.0 copy-done.15
  112.9 0.3 fusion.2
  113.2 0.0 copy-done.17
  113.2 0.1 select_reduce_fusion.weigh
  113.4 2.0 %copy-done.1 = bf16[2,448,2048]{2,1,0:T(8,128)(2,1)S(1)} copy-done((bf16[2,448,2048]{2,1,0:T(8,128)(2,1)S(1)}, bf16[2,448,2048]{2,1,0:T(8,128)(2,1)}, u32[]{:S(2)}) %copy-start.1) | copy-done | bytes 3670040
  115.5 1.3 copy-done.2
  116.8 1.1 copy-done.3
  117.9 64.7 %collect.1 = bf16[128,512]{1,0:T(8,128)(2,1)S(1)} custom-call(bf16[8,2,80,512]{3,2,1,0:T(8,128)(2,1)S(1)} %copy-done.2, bf16[8,80,512]{2,1,0:T(8,128)(2,1)S(1)} %copy-done.3, bf16[2,448,2048]{2,1,0:T(8,128)(2,1)S(1)} %copy-done.1, bf16[128,80]{1,0:T(8,128)(2,1)S(1)} %fusion.10.unpack, f32[128,128]{1,0:T(8,128)S(1)} %select_reduce_fusion.weigh), custom_call_target="tpu_custom_call" | custom-call | tf_op jit(solution)/shard_map/collect/pallas_call | solution.py:618
  182.6 0.9 copy.62
  183.5 0.7 copy.65
  184.2 0.7 copy.66
  (27 shorter events, 0.2 us)
Async XLA Ops:
  0.6 112.2 %copy-start = (bf16[2048,8]{0,1:T(8,128)(2,1)S(1)}, bf16[2048,8]{0,1:T(8,128)(2,1)}, u32[]{:S(2)}) copy-start(bf16[2048,8]{0,1:T(8,128)(2,1)} %param.31) | copy-start | bytes 98308
  0.6 4.7 %copy-start.16 = (f32[128,16]{0,1:T(8,128)S(1)}, f32[128,16]{0,1:T(8,128)}, u32[]{:S(2)}) copy-start(f32[128,16]{0,1:T(8,128)} %param.26) | copy-start | bytes 24580
  0.7 5.0 %copy-start.14 = (f32[128,16]{0,1:T(8,128)S(1)}, f32[128,16]{0,1:T(8,128)}, u32[]{:S(2)}) copy-start(f32[128,16]{0,1:T(8,128)} %param.25) | copy-start | bytes 24580
  0.7 5.7 %copy-start.11 = (bf16[128,2,128]{2,1,0:T(2,128)(2,1)S(1)}, bf16[128,2,128]{2,1,0:T(2,128)(2,1)}, u32[]{:S(2)}) copy-start(bf16[128,2,128]{2,1,0:T(2,128)(2,1)} %param.23) | copy-start | bytes 196612
  0.7 5.7 %copy-start.10 = (bf16[128,2,128]{2,1,0:T(2,128)(2,1)S(1)}, bf16[128,2,128]{2,1,0:T(2,128)(2,1)}, u32[]{:S(2)}) copy-start(bf16[128,2,128]{2,1,0:T(2,128)(2,1)} %param.24) | copy-start | bytes 196612
  5.6 4.7 %copy-start.6 = (f32[128,16]{1,0:T(8,128)}, f32[128,16]{1,0:T(8,128)S(1)}, u32[]{:S(2)}) copy-start(f32[128,16]{1,0:T(8,128)S(1)} %reduce_window_sum.11.cum) | copy-start | bytes 24580
  7.1 3.9 %copy-start.12 = (bf16[128,2,128]{2,1,0:T(2,128)(2,1)S(1)}, bf16[128,2,128]{2,1,0:T(2,128)(2,1)}, u32[]{:S(2)}) copy-start(bf16[128,2,128]{2,1,0:T(2,128)(2,1)} %param.20) | copy-start | bytes 196612
  7.1 3.9 %copy-start.13 = (bf16[128,2,128]{2,1,0:T(2,128)(2,1)S(1)}, bf16[128,2,128]{2,1,0:T(2,128)(2,1)}, u32[]{:S(2)}) copy-start(bf16[128,2,128]{2,1,0:T(2,128)(2,1)} %param.19) | copy-start | bytes 196612
  7.1 4.6 %copy-start.5 = (bf16[1,224,2,2048]{3,2,1,0:T(2,128)(2,1)S(1)}, bf16[1,224,2,2048]{3,2,1,0:T(2,128)(2,1)}, u32[]{:S(2)}) copy-start(bf16[1,224,2,2048]{3,2,1,0:T(2,128)(2,1)} %param.34) | copy-start | bytes 5505028
  11.7 2.0 %copy-start.7 = (bf16[128,8,128]{2,1,0:T(8,128)(2,1)S(1)}, bf16[128,8,128]{2,1,0:T(8,128)(2,1)}, u32[]{:S(2)}) copy-start(bf16[128,8,128]{2,1,0:T(8,128)(2,1)} %param.18) | copy-start | bytes 786436
  11.7 3.5 %copy-start.18 = (f32[16]{0:T(128)S(1)}, f32[16]{0:T(128)}, u32[]{:S(2)}) copy-start(f32[16]{0:T(128)} %param.27) | copy-start | bytes 196
  15.9 96.9 %copy-start.4 = (bf16[128,2048]{1,0:T(8,128)(2,1)S(1)}, bf16[128,2048]{1,0:T(8,128)(2,1)}, u32[]{:S(2)}) copy-start(bf16[128,2048]{1,0:T(8,128)(2,1)} %param.29) | copy-start | bytes 1572868
  15.9 97.0 %copy-start.15 = (f32[2048]{0:T(1024)S(1)}, f32[2048]{0:T(1024)}, u32[]{:S(2)}) copy-start(f32[2048]{0:T(1024)} %param.30) | copy-start | bytes 24580
  15.9 97.3 %copy-start.17 = (s32[128,2]{0,1:T(2,128)S(1)}, s32[128,2]{0,1:T(2,128)}, u32[]{:S(2)}) copy-start(s32[128,2]{0,1:T(2,128)} %param.32) | copy-start | bytes 3076
  113.4 2.0 %copy-start.1 = (bf16[2,448,2048]{2,1,0:T(8,128)(2,1)S(1)}, bf16[2,448,2048]{2,1,0:T(8,128)(2,1)}, u32[]{:S(2)}) copy-start(bf16[2,448,2048]{2,1,0:T(8,128)(2,1)} %get-tuple-element.12.dn) | copy-start | bytes 11010052
  115.5 1.3 copy-start.2
  116.8 1.1 copy-start.3
  117.9 64.7 %copy-start.9 = (bf16[2,512,128]{2,1,0:T(8,128)(2,1)S(1)}, bf16[2,512,128]{2,1,0:T(8,128)(2,1)}, u32[]{:S(2)}) copy-start(bf16[2,512,128]{2,1,0:T(8,128)(2,1)} %get-tuple-element.8) | copy-start | bytes 786436
  117.9 65.6 %copy-start.8 = (bf16[128,1024]{1,0:T(8,128)(2,1)S(1)}, bf16[128,1024]{1,0:T(8,128)(2,1)}, u32[]{:S(2)}) copy-start(bf16[128,1024]{1,0:T(8,128)(2,1)} %get-tuple-element.27) | copy-start | bytes 786436

commit v3 on v2

--- a/solution.py
+++ b/solution.py
@@ -51,7 +51,7 @@
     pl.semaphore_wait(barrier, count)
 
 
-def attend_body(s, e, q, kv, out):
+def attend_body(s, e, q, kv, out, group):
     row = lax.rem(lax.broadcasted_iota(jnp.int32, (512, 1024), 0), 128)
     col = lax.broadcasted_iota(jnp.int32, (512, 1024), 1)
     place = col // 128
@@ -84,36 +84,35 @@
         )
         return new, total, acc
 
-    def one_group(group, _):
-        query = q[group]
-        k0 = kv[group, 0:8].reshape(1024, 128)
-        v0 = jnp.where(v_ok, kv[2 + group, 0:8].reshape(1024, 128), jnp.zeros((), BF16))
-        state = (
-            jnp.full((512, 1), -1e30, F32),
-            jnp.zeros((512, 1), F32),
-            jnp.zeros((512, 128), F32),
-        )
-        state = chunk(state, query, k0, v0, near)
-        vl = jnp.where(far_ok, kv[2 + group, 32], jnp.zeros((), BF16))
-        state = chunk(state, query, kv[group, 32], vl, last)
-
-        def more(k, carried):
-            keys = kv[group, pl.ds(k * 8, 8)].reshape(1024, 128)
-            values = kv[2 + group, pl.ds(k * 8, 8)].reshape(1024, 128)
-            return chunk(carried, query, keys, values, None)
-
-        _, total, acc = lax.fori_loop(1, jnp.minimum(s, 3) + 1, more, state)
-        out[group] = (acc / total).astype(BF16)
-        return 0
-
-    lax.fori_loop(0, 2, one_group, 0)
+    query = q[group]
+    k0 = kv[group, 0:8].reshape(1024, 128)
+    v0 = jnp.where(v_ok, kv[2 + group, 0:8].reshape(1024, 128), jnp.zeros((), BF16))
+    state = (
+        jnp.full((512, 1), -1e30, F32),
+        jnp.zeros((512, 1), F32),
+        jnp.zeros((512, 128), F32),
+    )
+    state = chunk(state, query, k0, v0, near)
+    vl = jnp.where(far_ok, kv[2 + group, 32], jnp.zeros((), BF16))
+    state = chunk(state, query, kv[group, 32], vl, last)
+
+    def more(k, carried):
+        keys = kv[group, pl.ds(k * 8, 8)].reshape(1024, 128)
+        values = kv[2 + group, pl.ds(k * 8, 8)].reshape(1024, 128)
+        return chunk(carried, query, keys, values, None)
+
+    _, total, acc = lax.fori_loop(1, jnp.minimum(s, 3) + 1, more, state)
+    out[group] = (acc / total).astype(BF16)
 
 
 def spread_kernel(
-    kv_in, rows_in, pack, st_in, dec_in, gu_in, dn_in, q,
-    inputs, gate, inflow, readout, cum, cum_t, step_t, skip, gain,
-    heads, state_out, h_all, h_oth, dn,
+    kv_in, hidden, mlp_gain, router_t, ints, gu_in, dn_in, q,
+    inputs, gate, inflow, readout, decay_t, step_t, skip, gain,
+    heads, state_out, routed,
+    h_all, h_oth, dn, rows_in, st_in, dec_in, weigh, cum, cum_t,
+    tx_f, rx_f, tx_b, rx_b, slots_tx, slots, mine_tx, mine,
     gu, kv, rows, ent, disp, st_rx, dec_rx, t_tx, t_rx, td_tx, td_rx, ent_tx, inner, carry, gated,
+    qf_s, qf_r, qb_s, qb_r, o_s, o_r, y_s, y_r,
     l_s, g_s, g_r, n_s, n_r, h_s, h_r,
     z_s, z_r, x_s, x_r, p_s, p_r, f_s, f_r,
     d_s, d_r, rf_s, rf_r, rb_s, rb_r, sa_s, sa_r, da_s, da_r, st_s, st_r, sd_s, sd_r, se_s, se_r,
@@ -216,19 +215,11 @@
             send(kv_hop(k + 1), (s >= k) & (s < STEPS - 1))
         kv_across(0 if k == 4 else k, k)
 
-    for d in range(1, CORES):
-        to = lax.rem(e + d, CORES)
-        send(rcopy(rows_in.at[to], disp.at[e], d_s.at[d], d_r.at[d], {"exp": to}))
     first, second = pl.ds(0, HALF), pl.ds(HALF, HALF)
     third, fourth = pl.ds(2 * HALF, HALF), pl.ds(3 * HALF, HALF)
     send(rcopy(gu_in.at[:, first], gu.at[:, third], g_s.at[0], g_r.at[0], to_a))
     send(rcopy(gu_in.at[:, second], gu.at[:, fourth], g_s.at[1], g_r.at[1], to_b))
     send(kv_hop(1), s < STEPS - 1)
-    for d in range(1, CORES):
-        to = lax.rem(e + d, CORES)
-        send(rcopy(st_in.at[to], st_rx.at[e], sa_s.at[d], sa_r.at[d], {"exp": to}))
-        send(rcopy(dec_in.at[to], dec_rx.at[e], da_s.at[d], da_r.at[d], {"exp": to}))
-    kv_across(0, 0)
     send(rcopy(dn_in.at[first], dn.at[0, third], n_s.at[0], n_r.at[0], to_a))
     send(rcopy(dn_in.at[second], dn.at[0, fourth], n_s.at[1], n_r.at[1], to_b))
     send(rcopy(dn_in.at[second], dn.at[1, fourth], n_s.at[2], n_r.at[2], to_a))
@@ -237,21 +228,72 @@
     own_dn = pltpu.make_async_copy(dn_in, dn.at[0, pl.ds(0, 2 * HALF)], l_s.at[1])
     own_gu.start()
     own_dn.start()
+    h_all[...] = jnp.zeros_like(h_all)
+    wide = hidden[...].astype(F32)
+    level = lax.rsqrt(jnp.mean(wide * wide, axis=1, keepdims=True) + EPSILON)
+    normed = (wide * level * mlp_gain[...]).astype(BF16)
+    lanes = lax.broadcasted_iota(jnp.int32, (128, CORES * 2 * PAD), 1)
+    picker = ((ints[:, 0:1] == lanes) | (ints[:, 1:2] == lanes)).astype(F32).astype(BF16)
+    rows_in[...] = lax.dot_general(
+        picker, normed, (((0,), (0,)), ((), ())), preferred_element_type=F32
+    ).astype(BF16).reshape(CORES, 2, PAD, -1)
+    for i in range(2):
+        for d in range(1, CORES):
+            to = lax.rem(e + d, CORES)
+            send(rcopy(rows_in.at[to, i], disp.at[i, e], d_s.at[i, d], d_r.at[i, d], {"exp": to}))
+        disp[i, pl.ds(e, 1)] = rows_in[pl.ds(e, 1), i]
+
+    exact = lax.Precision.HIGHEST
+    low_tri = (
+        lax.broadcasted_iota(jnp.int32, (128, 128), 0)
+        >= lax.broadcasted_iota(jnp.int32, (128, 128), 1)
+    ).astype(F32)
+    eye = (
+        lax.broadcasted_iota(jnp.int32, (128, 128), 0)
+        == lax.broadcasted_iota(jnp.int32, (128, 128), 1)
+    ).astype(F32)
+    both_last = (((1,), (1,)), ((), ()))
+    cum[...] = lax.dot_general(
+        low_tri, decay_t[...], both_last, precision=exact, preferred_element_type=F32
+    )
+    cum_t[...] = lax.dot_general(
+        decay_t[...], low_tri, both_last, precision=exact, preferred_element_type=F32
+    )
+    block_total = cum_t[:, 127:128]
+    weight_t = jnp.exp(block_total - cum_t[...]) * step_t[...]
+    weight_in = lax.dot_general(
+        eye, weight_t, both_last, precision=exact, preferred_element_type=F32
+    )
+    whole_decay = jnp.broadcast_to(jnp.exp(block_total), (16, 128))
+    dec_in[...] = jnp.zeros_like(dec_in)
+    for pair in range(8):
+        dec_in[pair, 0:2, :] = whole_decay[2 * pair:2 * pair + 2]
+        vectors = inflow[:, 128 * (pair // 4):128 * (pair // 4) + 128].astype(F32)
+        both = inputs[:, 128 * pair:128 * pair + 128]
+        for h in range(2):
+            head = 2 * pair + h
+            weighted = (weight_in[:, head:head + 1] * vectors).astype(BF16)
+            res = lax.dot_general(
+                both, weighted, (((0,), (0,)), ((), ())), preferred_element_type=F32
+            )
+            st_in[pair, 64 * h:64 * h + 64, :] = res[64 * h:64 * h + 64].astype(BF16)
+    for d in range(1, CORES):
+        to = lax.rem(e + d, CORES)
+        send(rcopy(st_in.at[to], st_rx.at[e], sa_s.at[d], sa_r.at[d], {"exp": to}))
+        send(rcopy(dec_in.at[to], dec_rx.at[e], da_s.at[d], da_r.at[d], {"exp": to}))
+    kv_across(0, 0)
     kv[:, pl.ds(e, 1)] = kv_in[...][:, None]
-    disp[pl.ds(e, 1)] = rows_in[pl.ds(e, 1)]
     st_rx[pl.ds(e, 1)] = st_in[pl.ds(e, 1)]
     dec_rx[pl.ds(e, 1)] = dec_in[pl.ds(e, 1)]
-    h_all[...] = jnp.zeros_like(h_all)
     td_tx[...] = jnp.zeros_like(td_tx)
+    lane = lax.broadcasted_iota(jnp.int32, (ROWS, CORES * PAD), 1)
+    place = (lane // PAD) * QUARTER + lax.rem(lane, PAD)
+    fits = lax.rem(lane, PAD) < QUARTER
+    pack = (
+        (place == lax.broadcasted_iota(jnp.int32, (ROWS, CORES * PAD), 0)) & fits
+    ).astype(F32).astype(BF16)
 
     kv_arrive(1)
-    for d in range(1, CORES):
-        frm = lax.rem(e + CORES - d, CORES)
-        rcopy(disp.at[frm], disp.at[frm], d_s.at[d], d_r.at[d], {"exp": frm}).wait_recv()
-    packed = jnp.dot(
-        pack[...], disp[...].reshape(CORES * 2 * PAD, -1), preferred_element_type=F32
-    ).astype(BF16)
-    rows[pl.ds(s, 1)] = packed.reshape(1, 2, ROWS, -1)
 
     def rows_up(j, i):
         at = rows.at[lax.rem(s + STEPS - j, STEPS), i]
@@ -270,9 +312,32 @@
         return rcopy(at, at, rb_s.at[j, i], rb_r.at[j, i], {"seq": nxt})
 
     for i in range(2):
+        for d in range(1, CORES):
+            frm = lax.rem(e + CORES - d, CORES)
+            at = disp.at[i, frm]
+            rcopy(at, at, d_s.at[i, d], d_r.at[i, d], {"exp": frm}).wait_recv()
+        rows[pl.ds(s, 1), i] = jnp.dot(
+            pack, disp[i].reshape(CORES * PAD, -1), preferred_element_type=F32
+        ).astype(BF16)[None]
         send(rows_down(0, i))
         send(rows_up(0, i))
-    kv_arrive(2)
+        if i == 0:
+            logits = lax.dot_general(
+                normed, router_t[...], both_last, preferred_element_type=F32
+            )
+            gates = 1.0 / (1.0 + jnp.exp(-logits))
+            expert = lax.broadcasted_iota(jnp.int32, (128, EXPERTS), 1)
+            chosen = [
+                jnp.sum(jnp.where(ints[:, 4 + k:5 + k] == expert, gates, 0.0), axis=1,
+                        keepdims=True)
+                for k in range(2)
+            ]
+            home = lax.broadcasted_iota(jnp.int32, (128, CORES * PAD), 1)
+            weigh[...] = sum(
+                jnp.where(ints[:, 2 + k:3 + k] == home, chosen[k] / (chosen[0] + chosen[1]), 0.0)
+                for k in range(2)
+            )
+            kv_arrive(2)
 
     for d in range(1, CORES):
         frm = lax.rem(e + CORES - d, CORES)
@@ -374,19 +439,18 @@
     rcopy(at, at, n_s.at[1], n_r.at[1], to_b).wait_recv()
     send(rcopy(at, dn.at[1, second], n_s.at[5], n_r.at[5], to_a))
     expert_pair(1)
-    rows_step(2)
     for g in (1, 2, 3, 0):
         kv_finish(g)
-    attend_body(s, e, q, kv, heads)
+    attend_body(s, e, q, kv, heads, 0)
+    rows_step(2)
+    expert_pair(2)
+    attend_body(s, e, q, kv, heads, 1)
     for d in range(1, CORES):
         frm = lax.rem(e + CORES - d, CORES)
         rcopy(ent.at[frm], ent.at[frm], se_s.at[d], se_r.at[d], {"exp": frm}).wait_recv()
     state_body(
         inputs, gate, inflow, readout, cum, cum_t, step_t, skip, gain, ent, state_out, gated
     )
-    expert_pair(2)
-    rows_step(3)
-    expert_in(lax.rem(s + 4, STEPS))
     own_dn.wait()
     for n, at, dev in (
         (2, dn.at[1, fourth], to_a),
@@ -395,8 +459,118 @@
         (5, dn.at[1, second], to_a),
     ):
         rcopy(at, at, n_s.at[n], n_r.at[n], dev).wait_recv()
+
+    width = dn.shape[-1] // 4
+
+    def columns(stream):
+        return slice(width * stream, width * stream + width)
+
+    def mate_arrived(b):
+        to_mate_copy(b).wait_recv()
+
+    def partial_of(b, half):
+        cols = slice(2 * width * half, 2 * width * (half + 1))
+        return jnp.dot(
+            h_all[b, t // 2, :, 0:UNITS], dn[0, :, cols], preferred_element_type=F32
+        ) + jnp.dot(h_oth[b, :, 0:UNITS], dn[1, :, cols], preferred_element_type=F32)
+
+    def up(stream, j):
+        return rcopy(
+            tx_f.at[stream, j], rx_f.at[stream, j], qf_s.at[stream, j], qf_r.at[stream, j],
+            {"seq": nxt},
+        )
+
+    def down(stream, j):
+        return rcopy(
+            tx_b.at[stream, j], rx_b.at[stream, j], qb_s.at[stream, j], qb_r.at[stream, j],
+            {"seq": prv},
+        )
+
+    def hop(half, j, rising, value):
+        begin = 0 if (half == 0) == rising else 1
+        tx, rx, line = (tx_f, rx_f, up) if rising else (tx_b, rx_b, down)
+        for i in range(2):
+            stream = 2 * half + i
+            piece = value[:, columns(i)]
+            if j > begin:
+                line(stream, j - 1).wait_recv()
+                piece = piece + rx[stream, j - 1].astype(F32)
+            tx[stream, j] = piece.astype(BF16)
+            send(line(stream, j))
+
+    def ahead(d):
+        return lax.rem(s + d, STEPS)
+
+    def short_hop(j):
+        hop(1, j, True, partial_of(ahead(4 - j), 1))
+        hop(0, j, False, partial_of(ahead(4 + j), 0))
+
+    def long_hop(j):
+        hop(0, j, True, partial_of(ahead(4 - j), 0))
+        hop(1, j, False, partial_of(ahead(4 + j), 1))
+
+    mate_arrived(ahead(3))
+    mate_arrived(ahead(5))
+    short_hop(1)
+    rows_step(3)
+    expert_in(ahead(4))
+    for d in (2, 6, 1, 7, 0):
+        mate_arrived(ahead(d))
+    short_hop(2)
+    mate_arrived(ahead(4))
+    long_hop(0)
+    short_hop(3)
+    for j in range(1, 4):
+        long_hop(j)
+    finals = [partial_of(s, half) for half in range(2)]
+
+    def slot_copy(stream, d, there):
+        return rcopy(
+            slots_tx.at[stream, there], slots.at[stream, e], o_s.at[stream, d],
+            o_r.at[stream, d], {"exp": there},
+        )
+
+    for stream in (0, 2, 1, 3):
+        half, i = stream // 2, stream % 2
+        up(stream, 3).wait_recv()
+        down(stream, 3).wait_recv()
+        total = (
+            finals[half][:, columns(i)]
+            + rx_f[stream, 3].astype(F32)
+            + rx_b[stream, 3].astype(F32)
+        )
+        spaced = lax.dot_general(
+            pack, total.astype(BF16), (((0,), (0,)), ((), ())), preferred_element_type=F32
+        )
+        slots_tx[stream] = spaced.astype(BF16).reshape(CORES, PAD, width)
+        for d in range(1, CORES):
+            send(slot_copy(stream, d, lax.rem(e + d, CORES)))
+        slots[stream, pl.ds(e, 1)] = slots_tx[stream, pl.ds(e, 1)]
+    high = weigh[...].astype(BF16)
+    rest = (weigh[...] - high.astype(F32)).astype(BF16)
+    for stream in (0, 2, 1, 3):
+        for d in range(1, CORES):
+            frm = lax.rem(e + CORES - d, CORES)
+            at = slots.at[stream, frm]
+            rcopy(at, at, o_s.at[stream, d], o_r.at[stream, d], {"exp": frm}).wait_recv()
+        at = slots[stream].reshape(CORES * PAD, width)
+        mine_tx[stream] = (
+            jnp.dot(high, at, preferred_element_type=F32)
+            + jnp.dot(rest, at, preferred_element_type=F32)
+        ).astype(BF16)
+        send(
+            rcopy(mine_tx.at[stream], mine.at[t], y_s.at[stream], y_r.at[t], {"tp": stream}),
+            t != stream,
+        )
+    total = mine_tx[t].astype(F32)
+    for d in range(1, TPS):
+        frm = lax.rem(t + TPS - d, TPS)
+        at = mine.at[frm]
+        rcopy(at, at, y_s.at[frm], y_r.at[frm], {"tp": frm}).wait_recv()
+        total = total + mine[frm].astype(F32)
+    routed[...] = total.astype(BF16)
     for b in range(STEPS):
-        to_mate_copy(b).wait()
+        to_mate_copy(b).wait_send()
     for copy, cond in pending:
         guarded(cond, copy.wait_send)
 
@@ -405,24 +579,40 @@
     vm = pl.BlockSpec(memory_space=VM)
     hbm = pl.BlockSpec(memory_space=pl.ANY)
     width = operands[1].shape[-1]
+    quarter = width // 4
     dma = pltpu.SemaphoreType.DMA
     return pl.pallas_call(
         spread_kernel,
         out_shape=(
             jax.ShapeDtypeStruct((2, 512, 128), BF16),
             jax.ShapeDtypeStruct((128, 1024), BF16),
-            jax.ShapeDtypeStruct((STEPS, 2, ROWS, 512), BF16),
-            jax.ShapeDtypeStruct((STEPS, ROWS, 512), BF16),
-            jax.ShapeDtypeStruct((2, UNITS, width), BF16),
+            jax.ShapeDtypeStruct((128, quarter), BF16),
         ),
-        in_specs=[vm] * 5 + [hbm] * 2 + [vm] * 10,
-        out_specs=(vm,) * 5,
+        in_specs=[vm] * 5 + [hbm] * 2 + [vm] * 9,
+        out_specs=(vm,) * 3,
         scratch_shapes=[
+            VM((STEPS, 2, ROWS, 512), BF16),
+            VM((STEPS, ROWS, 512), BF16),
+            VM((2, UNITS, width), BF16),
+            VM((CORES, 2, PAD, width), BF16),
+            VM((CORES, 128, 128), BF16),
+            VM((CORES, 8, 128), F32),
+            VM((128, 128), F32),
+            VM((128, 16), F32),
+            VM((16, 128), F32),
+            VM((4, 4, ROWS, quarter), BF16),
+            VM((4, 4, ROWS, quarter), BF16),
+            VM((4, 4, ROWS, quarter), BF16),
+            VM((4, 4, ROWS, quarter), BF16),
+            VM((4, CORES, PAD, quarter), BF16),
+            VM((4, CORES, PAD, quarter), BF16),
+            VM((TPS, 128, quarter), BF16),
+            VM((TPS, 128, quarter), BF16),
             VM((2, UNITS, width), BF16),
             VM((4, 33, 128, 128), BF16),
             VM((STEPS, 2, ROWS, width), BF16),
             VM((CORES, 128, 128), BF16),
-            VM((CORES, 2 * PAD, width), BF16),
+            VM((2, CORES, PAD, width), BF16),
             VM((CORES, 128, 128), BF16),
             VM((CORES, 8, 128), F32),
             VM((128, 128), BF16),
@@ -433,45 +623,20 @@
             VM((CORES, 128, 128), F32),
             VM((128, 128), F32),
             VM((128, 512), F32),
+            dma((4, 4)), dma((4, 4)), dma((4, 4)), dma((4, 4)), dma((4, 8)), dma((4, 8)),
+            dma((4,)), dma((4,)),
             dma((2,)), dma((2,)), dma((2,)), dma((6,)), dma((6,)), dma((8,)), dma((8,)),
             dma((4,)), dma((4,)), dma((5, 4)), dma((4, 4)), dma((5,)), dma((4,)),
             dma((4, 4)), dma((4, 4)),
-            dma((8,)), dma((8,)), dma((3, 2)), dma((3, 2)), dma((4, 2)), dma((4, 2)),
+            dma((2, 8)), dma((2, 8)), dma((3, 2)), dma((3, 2)), dma((4, 2)), dma((4, 2)),
             dma((8,)), dma((8,)), dma((8,)), dma((8,)), dma((8,)), dma((8,)),
             dma((8,)), dma((8,)), dma((8,)), dma((8,)),
         ],
         compiler_params=pltpu.CompilerParams(
-            collective_id=1, has_side_effects=True, vmem_limit_bytes=56 << 20
+            collective_id=1, has_side_effects=True, vmem_limit_bytes=58 << 20
         ),
         name="spread",
     )(*operands)
-
-
-def summary_kernel(inputs, inflow, weight_in, out):
-    for pair in range(8):
-        vectors = inflow[:, 128 * (pair // 4):128 * (pair // 4) + 128].astype(F32)
-        both = inputs[:, 128 * pair:128 * pair + 128]
-        for h in range(2):
-            head = 2 * pair + h
-            weighted = (weight_in[:, head:head + 1] * vectors).astype(BF16)
-            res = lax.dot_general(
-                both, weighted, (((0,), (0,)), ((), ())), preferred_element_type=F32
-            )
-            out[pair, 64 * h:64 * h + 64, :] = res[64 * h:64 * h + 64].astype(BF16)
-
-
-def summary(inputs, inflow, weight_in):
-    vm = pl.BlockSpec(memory_space=VM)
-    return pl.pallas_call(
-        summary_kernel,
-        out_shape=jax.ShapeDtypeStruct((8, 128, 128), BF16),
-        in_specs=[vm] * 3,
-        out_specs=vm,
-        cost_estimate=pl.CostEstimate(
-            flops=1_000_000_000, bytes_accessed=1_000_000, transcendentals=0
-        ),
-        name="summary",
-    )(inputs, inflow, weight_in)
 
 
 def state_body(inputs, gate, inflow, readout, cum, cum_t, step_t, skip, gain, ent, out, gated):
@@ -505,7 +670,10 @@
             inter = scale * lax.dot_general(
                 read, ent[pair], (((1,), (1,)), ((), ())), preferred_element_type=F32
             )
-            mixed = intra + inter + skip[:, at] * both.astype(F32)
+            direct = jnp.where(
+                low, skip[:, 2 * pair:2 * pair + 1], skip[:, 2 * pair + 1:2 * pair + 2]
+            )
+            mixed = intra + inter + direct * both.astype(F32)
             v = gate[:, at].astype(F32)
             value = mixed * (v / (1.0 + jnp.exp(-v)))
             gated[:, 128 * p:128 * p + 128] = value
@@ -515,179 +683,30 @@
         out[:, wide] = (gated[...] * inv * gain[:, wide]).astype(BF16)
 
 
-def gather_kernel(
-    h_all, h_oth, dn, unpack, weigh, out,
-    tx, rx, slots_tx, slots, mine_tx, mine,
-    r_s, r_r, x_s, x_r, y_s, y_r,
-):
-    s = lax.axis_index("seq")
-    e = lax.axis_index("exp")
-    t = lax.axis_index("tp")
-    nxt = lax.rem(s + 1, STEPS)
-    prv = lax.rem(s + STEPS - 1, STEPS)
-    greet(
-        (
-            ("exp", CORES, range(1, CORES)),
-            ("seq", STEPS, (1, STEPS - 1)),
-            ("tp", TPS, range(1, TPS)),
-        )
-    )
-    pending = []
-    width = dn.shape[-1] // 4
-
-    def columns(stream):
-        return slice(width * stream, width * stream + width)
-
-    def ring(stream, j):
-        to = nxt if stream < 2 else prv
-        return rcopy(
-            tx.at[stream, j], rx.at[stream, j], r_s.at[stream, j], r_r.at[stream, j], {"seq": to}
-        )
-
-    def owner(stream, j):
-        if stream < 2:
-            return lax.rem(s + 2 * STEPS - 1 - j, STEPS)
-        return lax.rem(s + 1 + j, STEPS)
-
-    def partial_of(q, half):
-        cols = slice(2 * width * half, 2 * width * (half + 1))
-        return jnp.dot(
-            h_all[q, t // 2, :, 0:UNITS], dn[0, :, cols], preferred_element_type=F32
-        ) + jnp.dot(h_oth[q, :, 0:UNITS], dn[1, :, cols], preferred_element_type=F32)
-
-    for j in range(STEPS - 1):
-        for half in range(2):
-            value = partial_of(owner(2 * half, j), half)
-            for i in range(2):
-                stream = 2 * half + i
-                piece = value[:, columns(i)]
-                if j > 0:
-                    ring(stream, j - 1).wait_recv()
-                    piece = piece + rx[stream, j - 1].astype(F32)
-                tx[stream, j] = piece.astype(BF16)
-                copy = ring(stream, j)
-                copy.start()
-                pending.append(copy)
-    for half in range(2):
-        value = partial_of(s, half)
-        for i in range(2):
-            stream = 2 * half + i
-            ring(stream, STEPS - 2).wait_recv()
-            total = value[:, columns(i)] + rx[stream, STEPS - 2].astype(F32)
-            spaced = jnp.dot(unpack[...], total.astype(BF16), preferred_element_type=F32)
-            slots_tx[:, :, columns(stream)] = spaced.astype(BF16).reshape(CORES, PAD, width)
-    for d in range(1, CORES):
-        to = lax.rem(e + d, CORES)
-        copy = rcopy(slots_tx.at[to], slots.at[e], x_s.at[d], x_r.at[d], {"exp": to})
-        copy.start()
-        pending.append(copy)
-    slots[pl.ds(e, 1)] = slots_tx[pl.ds(e, 1)]
-    for d in range(1, CORES):
-        frm = lax.rem(e + CORES - d, CORES)
-        at = slots.at[frm]
-        rcopy(at, at, x_s.at[d], x_r.at[d], {"exp": frm}).wait_recv()
-    high = weigh[...].astype(BF16)
-    rest = (weigh[...] - high.astype(F32)).astype(BF16)
-    for quarter in range(TPS):
-        at = slots[:, :, columns(quarter)].reshape(CORES * PAD, width)
-        mine_tx[quarter] = (
-            jnp.dot(high, at, preferred_element_type=F32)
-            + jnp.dot(rest, at, preferred_element_type=F32)
-        ).astype(BF16)
-    for d in range(1, TPS):
-        to = lax.rem(t + d, TPS)
-        copy = rcopy(mine_tx.at[to], mine.at[d], y_s.at[d], y_r.at[d], {"tp": to})
-        copy.start()
-        pending.append(copy)
-    total = mine_tx[t].astype(F32)
-    for d in range(1, TPS):
-        frm = lax.rem(t + TPS - d, TPS)
-        at = mine.at[d]
-        rcopy(at, at, y_s.at[d], y_r.at[d], {"tp": frm}).wait_recv()
-        total = total + mine[d].astype(F32)
-    out[...] = total.astype(BF16)
-    for copy in pending:
-        copy.wait_send()
-
-
-def gathered(h_all, h_oth, dn, unpack, weigh):
-    vm = pl.BlockSpec(memory_space=VM)
-    width = dn.shape[-1]
-    q = width // 4
-    dma = pltpu.SemaphoreType.DMA
-    return pl.pallas_call(
-        gather_kernel,
-        out_shape=jax.ShapeDtypeStruct((128, q), BF16),
-        in_specs=[vm] * 5,
-        out_specs=vm,
-        scratch_shapes=[
-            VM((4, STEPS - 1, ROWS, q), BF16),
-            VM((4, STEPS - 1, ROWS, q), BF16),
-            VM((CORES, PAD, width), BF16),
-            VM((CORES, PAD, width), BF16),
-            VM((TPS, 128, q), BF16),
-            VM((TPS, 128, q), BF16),
-            dma((4, STEPS - 1)), dma((4, STEPS - 1)), dma((8,)), dma((8,)), dma((4,)), dma((4,)),
-        ],
-        compiler_params=pltpu.CompilerParams(
-            collective_id=2, has_side_effects=True, vmem_limit_bytes=40 << 20
-        ),
-        name="collect",
-    )(h_all, h_oth, dn, unpack, weigh)
-
-
 def local(
     query_heads, key_heads, value_head_rows, state_input, state_gate, state_inflow,
     state_readout, step_size, log_decay, skip_scale, state_gain, hidden_in, mlp_gain,
     router_weight, expert_ids, slot_index, gate_up, down_proj,
 ):
     tp = lax.axis_index("tp")
-    hidden = hidden_in.astype(F32)
-    mean_square = jnp.mean(hidden * hidden, axis=-1, keepdims=True)
-    normed = (hidden * lax.rsqrt(mean_square + EPSILON) * mlp_gain).astype(BF16)
-    gate_values = jax.nn.sigmoid(jnp.dot(normed, router_weight, preferred_element_type=F32))
-    one_hot = expert_ids[..., None] == jnp.arange(EXPERTS, dtype=jnp.int32)
-    chosen = jnp.sum(jnp.where(one_hot, gate_values[:, None, :], 0.0), axis=-1)
-    mixing = chosen / jnp.sum(chosen, axis=1, keepdims=True)
     is_live = slot_index >= 0
     quarter = slot_index // QUARTER
     inside = slot_index - quarter * QUARTER
-    lanes = jnp.arange(EXPERTS * 2 * PAD, dtype=jnp.int32)
     near = is_live & (quarter % 2 == tp % 2)
     place = jnp.where(near, expert_ids * (2 * PAD) + (quarter // 2) * PAD + inside, -1)
-    picker = jnp.any(place[..., None] == lanes, axis=1).astype(BF16)
-    outgoing = lax.dot_general(
-        picker, normed, (((0,), (0,)), ((), ())), preferred_element_type=F32
-    ).astype(BF16).reshape(EXPERTS, 2 * PAD, -1)
     home = jnp.where(is_live & (quarter == tp), expert_ids * PAD + inside, -1)
-    hits = home[..., None] == lanes[:EXPERTS * PAD]
-    weigh = jnp.sum(jnp.where(hits, mixing[..., None], 0.0), axis=1)
-    flat = jnp.arange(2 * ROWS)
-    source = (flat % ROWS) // QUARTER * (2 * PAD) + flat // ROWS * PAD + flat % QUARTER
-    pack = (source[:, None] == lanes[None]).astype(BF16)
-    flat = jnp.arange(ROWS)
-    unpack = (
-        (flat // QUARTER * PAD + flat % QUARTER)[None] == jnp.arange(CORES * PAD)[:, None]
-    ).astype(BF16)
-
-    cum = jnp.cumsum(log_decay, axis=0)
-    block_total = cum[-1]
-    weight_in = jnp.exp(block_total[None] - cum) * step_size
-    states = summary(state_input, state_inflow.reshape(128, 256), weight_in)
-    decays = jnp.pad(jnp.exp(block_total).reshape(CORES, 2), ((0, 0), (0, 6)))
-    decays = jnp.broadcast_to(decays[..., None], (CORES, 8, 128))
+    ints = jnp.concatenate([place, home, expert_ids], axis=1)
     kv_in = jnp.concatenate(
         [jnp.transpose(key_heads, (1, 0, 2)), jnp.transpose(value_head_rows, (1, 0, 2))], axis=0
     )
-    heads, state_out, h_all, h_oth, down = spread(
-        kv_in, outgoing, pack, states, decays,
+    heads, state_out, routed_out = spread(
+        kv_in, hidden_in, mlp_gain[None], router_weight.T, ints,
         jnp.transpose(gate_up[0], (1, 0, 2)), down_proj[0],
         jnp.transpose(query_heads, (1, 0, 2)).reshape(2, 512, 128),
         state_input, state_gate, state_inflow.reshape(128, 256), state_readout.reshape(128, 256),
-        cum, cum.T, step_size.T, jnp.repeat(skip_scale, 64)[None], state_gain[None],
+        log_decay.T, step_size.T, skip_scale[None], state_gain[None],
     )
     window_out = jnp.transpose(heads.reshape(8, 128, 128), (1, 0, 2))
-    routed_out = gathered(h_all, h_oth, down, unpack, weigh)
     return window_out, state_out, routed_out
 
 

time: 185 us -> 154 us (0.83)
  Pallas kernels: 164 us -> 137 us
  matrix products: 2.85 us -> 0 us
  other arithmetic: 4.53 us -> 2.08 us
    pallas_call x2 -> x0, Pallas kernels: 67.2 us -> none  [the longest x1 64.7 us: gathered(): pl.pallas_call(gather_kernel, out_shape=jax.ShapeDtypeStruct((128, q), BF...]
    pallas_call x1, Pallas kernels: 96.9 us -> 137 us  [spread(): pl.pallas_call(spread_kernel, out_shape=(jax.ShapeDtypeStruct((2, 512, 12...]
    dot_general x2 -> x0, matrix products: 2.85 us -> none  [the longest x1 2.54 us: local(): lax.dot_general(picker, normed, (((0,), (0,)), ((), ())), preferred_eleme...]
    unnamed x43 -> x3, local copies, waits for them, and re-layouts: 8.05 us -> 6.74 us
where the time goes in v3:
time: 154 us; the launch traced here: 153 us
  Pallas kernels  137 us (89%)
  local copies, waits for them, and re-layouts  13.4 us (9%)
  other arithmetic  2.08 us (1%)
    pallas_call x1, Pallas kernels, spread(): pl.pallas_call(spread_kernel, out_shape=(jax.ShapeDtypeStruct((2, 512, 12...  137 us
    unnamed x3, local copies, waits for them, and re-layouts  6.74 us

profile of v3, /device:TPU:1, one launch (start us, length us, event | category | flops | bytes accessed | tf_op | source)
XLA Modules:
  0.0 152.9 jit_solution(12421456069127857578)
XLA Ops:
  0.6 0.7 and_select_fusion.2
  1.4 0.7 pad_add_fusion
  2.1 0.7 copy.45.ints
  2.8 0.9 copy_bitcast_fusion.4
  3.7 0.7 pad_maximum_fusion.kv_in
  4.4 1.5 copy_bitcast_fusion.2
  5.9 1.7 %copy.44 = bf16[8,128,128]{2,1,0:T(8,128)(2,1)} copy(bf16[8,128,128]{2,0,1:T(8,128)(2,1)} %bitcast.31) | data formatting | bytes 524288 | tf_op jit(solution)/shard_map/transpose | solution.py:705
  7.6 3.5 %copy.55 = bf16[1,224,2,2048]{3,1,2,0:T(8,128)(2,1)} copy(bf16[1,224,2,2048]{3,2,1,0:T(2,128)(2,1)} %param.34) | data formatting | bytes 3670016 | tf_op args[16]
  11.1 136.8 %spread.1 = (bf16[2,512,128]{2,1,0:T(8,128)(2,1)}, bf16[128,1024]{1,0:T(8,128)(2,1)}, bf16[128,512]{1,0:T(8,128)(2,1)}) custom-call(bf16[4,128,128]{2,1,0:T(8,128)(2,1)} %pad_maximum_fusion.kv_in, bf16[128,2048]{1,0:T(8,128)(2,1)} %hidden.1, f32[1,2048]{1,0:T(1,128)} %bitcast.37, bf16[8,2048]{1,0:T(8,128)(2,1)} %bitcast.36, s32[128,6]{1,0:T(8,128)} %copy.45.ints, ...), custom_call_target="tpu_custom_call" | custom-call | tf_op jit(solution)/shard_map/spread/pallas_call | solution.py:584
  147.8 1.8 %copy.56 = bf16[8,128,128]{2,0,1:T(8,128)(2,1)} copy(bf16[8,128,128]{2,1,0:T(8,128)(2,1)} %bitcast.33) | data formatting | bytes 524288 | tf_op jit(solution)/shard_map/reshape | solution.py:709
  149.7 1.7 %copy.59 = bf16[128,1024]{1,0:T(8,128)(2,1)} copy(bf16[128,1024]{1,0:T(8,128)(2,1)} %get-tuple-element.19) | data formatting | bytes 524288
  151.3 1.6 %copy.60 = bf16[128,512]{1,0:T(8,128)(2,1)} copy(bf16[128,512]{1,0:T(8,128)(2,1)} %get-tuple-element.20) | data formatting | bytes 262144

commit v4 on v3

--- a/solution.py
+++ b/solution.py
@@ -48,7 +48,7 @@
                 barrier, inc=1, device_id={axis: lax.rem(me + d, size)}, device_id_type=MESH
             )
             count += 1
-    pl.semaphore_wait(barrier, count)
+    return lambda: pl.semaphore_wait(barrier, count)
 
 
 def attend_body(s, e, q, kv, out, group):
@@ -106,8 +106,8 @@
 
 
 def spread_kernel(
-    kv_in, hidden, mlp_gain, router_t, ints, gu_in, dn_in, q,
-    inputs, gate, inflow, readout, decay_t, step_t, skip, gain,
+    kv_in, hidden, mlp_gain, router_t, expert_t, slot_t, gu_in, dn_in, q,
+    inputs, gate, inflow, readout, decay_t, step_t, skip,
     heads, state_out, routed,
     h_all, h_oth, dn, rows_in, st_in, dec_in, weigh, cum, cum_t,
     tx_f, rx_f, tx_b, rx_b, slots_tx, slots, mine_tx, mine,
@@ -128,14 +128,31 @@
     odd = lax.rem(t, 2)
     to_a = {"tp": t + 1 - 2 * odd}
     to_b = {"tp": lax.rem(t + 3 + 2 * odd, TPS)}
+    own = t // 2
+    turn = (1 - own, own)
     to_mate = {"tp": lax.rem(t + 2, TPS)}
-    greet(
+    all_here = greet(
         (
             ("tp", TPS, range(1, TPS)),
             ("exp", CORES, range(1, CORES)),
             ("seq", STEPS, range(1, STEPS)),
         )
     )
+    wide = hidden[...].astype(F32)
+    level = lax.rsqrt(jnp.mean(wide * wide, axis=1, keepdims=True) + EPSILON)
+    normed = (wide * level * mlp_gain[...]).astype(BF16)
+    spot = slot_t[...]
+    quarter = sum((spot >= QUARTER * k).astype(jnp.int32) for k in range(1, TPS))
+    inside = spot - QUARTER * quarter
+    near = (spot >= 0) & ((quarter & 1) == odd)
+    place = jnp.where(near, expert_t[...] * (2 * PAD) + (quarter >> 1) * PAD + inside, -1)
+    home = jnp.where((spot >= 0) & (quarter == t), expert_t[...] * PAD + inside, -1)
+    spots = lax.broadcasted_iota(jnp.int32, (CORES * 2 * PAD, 128), 0)
+    picker = ((place[0:1] == spots) | (place[1:2] == spots)).astype(F32).astype(BF16)
+    rows_in[...] = jnp.dot(
+        picker, normed, preferred_element_type=F32
+    ).astype(BF16).reshape(CORES, 2, PAD, -1)
+    all_here()
     pending = []
 
     def send(copy, cond=True):
@@ -215,6 +232,12 @@
             send(kv_hop(k + 1), (s >= k) & (s < STEPS - 1))
         kv_across(0 if k == 4 else k, k)
 
+    for i in range(2):
+        for d in range(1, CORES):
+            to = lax.rem(e + d, CORES)
+            send(rcopy(rows_in.at[to, turn[i]], disp.at[i, e], d_s.at[i, d], d_r.at[i, d], {"exp": to}))
+        disp[i, pl.ds(e, 1)] = rows_in[pl.ds(e, 1), turn[i]]
+
     first, second = pl.ds(0, HALF), pl.ds(HALF, HALF)
     third, fourth = pl.ds(2 * HALF, HALF), pl.ds(3 * HALF, HALF)
     send(rcopy(gu_in.at[:, first], gu.at[:, third], g_s.at[0], g_r.at[0], to_a))
@@ -228,21 +251,6 @@
     own_dn = pltpu.make_async_copy(dn_in, dn.at[0, pl.ds(0, 2 * HALF)], l_s.at[1])
     own_gu.start()
     own_dn.start()
-    h_all[...] = jnp.zeros_like(h_all)
-    wide = hidden[...].astype(F32)
-    level = lax.rsqrt(jnp.mean(wide * wide, axis=1, keepdims=True) + EPSILON)
-    normed = (wide * level * mlp_gain[...]).astype(BF16)
-    lanes = lax.broadcasted_iota(jnp.int32, (128, CORES * 2 * PAD), 1)
-    picker = ((ints[:, 0:1] == lanes) | (ints[:, 1:2] == lanes)).astype(F32).astype(BF16)
-    rows_in[...] = lax.dot_general(
-        picker, normed, (((0,), (0,)), ((), ())), preferred_element_type=F32
-    ).astype(BF16).reshape(CORES, 2, PAD, -1)
-    for i in range(2):
-        for d in range(1, CORES):
-            to = lax.rem(e + d, CORES)
-            send(rcopy(rows_in.at[to, i], disp.at[i, e], d_s.at[i, d], d_r.at[i, d], {"exp": to}))
-        disp[i, pl.ds(e, 1)] = rows_in[pl.ds(e, 1), i]
-
     exact = lax.Precision.HIGHEST
     low_tri = (
         lax.broadcasted_iota(jnp.int32, (128, 128), 0)
@@ -286,6 +294,7 @@
     st_rx[pl.ds(e, 1)] = st_in[pl.ds(e, 1)]
     dec_rx[pl.ds(e, 1)] = dec_in[pl.ds(e, 1)]
     td_tx[...] = jnp.zeros_like(td_tx)
+    h_all[...] = jnp.zeros_like(h_all)
     lane = lax.broadcasted_iota(jnp.int32, (ROWS, CORES * PAD), 1)
     place = (lane // PAD) * QUARTER + lax.rem(lane, PAD)
     fits = lax.rem(lane, PAD) < QUARTER
@@ -296,19 +305,19 @@
     kv_arrive(1)
 
     def rows_up(j, i):
-        at = rows.at[lax.rem(s + STEPS - j, STEPS), i]
+        at = rows.at[lax.rem(s + STEPS - j, STEPS), turn[i]]
         return rcopy(at, at, rf_s.at[j, i], rf_r.at[j, i], {"seq": nxt})
 
     def rows_down(j, i):
-        at = rows.at[lax.rem(s + j, STEPS), i]
+        at = rows.at[lax.rem(s + j, STEPS), turn[i]]
         return rcopy(at, at, rb_s.at[j, i], rb_r.at[j, i], {"seq": prv})
 
     def rows_up_arrived(j, i):
-        at = rows.at[lax.rem(s + STEPS - 1 - j, STEPS), i]
+        at = rows.at[lax.rem(s + STEPS - 1 - j, STEPS), turn[i]]
         return rcopy(at, at, rf_s.at[j, i], rf_r.at[j, i], {"seq": prv})
 
     def rows_down_arrived(j, i):
-        at = rows.at[lax.rem(s + 1 + j, STEPS), i]
+        at = rows.at[lax.rem(s + 1 + j, STEPS), turn[i]]
         return rcopy(at, at, rb_s.at[j, i], rb_r.at[j, i], {"seq": nxt})
 
     for i in range(2):
@@ -316,25 +325,25 @@
             frm = lax.rem(e + CORES - d, CORES)
             at = disp.at[i, frm]
             rcopy(at, at, d_s.at[i, d], d_r.at[i, d], {"exp": frm}).wait_recv()
-        rows[pl.ds(s, 1), i] = jnp.dot(
+        rows[pl.ds(s, 1), turn[i]] = jnp.dot(
             pack, disp[i].reshape(CORES * PAD, -1), preferred_element_type=F32
         ).astype(BF16)[None]
         send(rows_down(0, i))
         send(rows_up(0, i))
         if i == 0:
             logits = lax.dot_general(
-                normed, router_t[...], both_last, preferred_element_type=F32
+                router_t[...], normed, both_last, preferred_element_type=F32
             )
             gates = 1.0 / (1.0 + jnp.exp(-logits))
-            expert = lax.broadcasted_iota(jnp.int32, (128, EXPERTS), 1)
+            expert = lax.broadcasted_iota(jnp.int32, (EXPERTS, 128), 0)
             chosen = [
-                jnp.sum(jnp.where(ints[:, 4 + k:5 + k] == expert, gates, 0.0), axis=1,
+                jnp.sum(jnp.where(expert_t[k:k + 1, :] == expert, gates, 0.0), axis=0,
                         keepdims=True)
                 for k in range(2)
             ]
-            home = lax.broadcasted_iota(jnp.int32, (128, CORES * PAD), 1)
+            base = lax.broadcasted_iota(jnp.int32, (CORES * PAD, 128), 0)
             weigh[...] = sum(
-                jnp.where(ints[:, 2 + k:3 + k] == home, chosen[k] / (chosen[0] + chosen[1]), 0.0)
+                jnp.where(home[k:k + 1] == base, chosen[k] / (chosen[0] + chosen[1]), 0.0)
                 for k in range(2)
             )
             kv_arrive(2)
@@ -359,38 +368,8 @@
         send(rcopy(t_tx, t_rx.at[s], st_s.at[d], st_r.at[d], {"seq": to}), s + d < STEPS)
         send(rcopy(td_tx, td_rx.at[s], sd_s.at[d], sd_r.at[d], {"seq": to}), s + d < STEPS)
 
-    kv_arrive(3)
-    for d in range(1, STEPS):
-        frm = lax.rem(s + STEPS - d, STEPS)
-        at = t_rx.at[frm]
-        guarded(d <= s, rcopy(at, at, st_s.at[d], st_r.at[d], {"seq": frm}).wait_recv)
-        at = td_rx.at[frm]
-        guarded(d <= s, rcopy(at, at, sd_s.at[d], sd_r.at[d], {"seq": frm}).wait_recv)
-    carry[...] = jnp.zeros_like(carry)
-    for k in range(STEPS - 1):
-
-        def fold(k=k):
-            for h in range(2):
-                part = slice(64 * h, 64 * h + 64)
-                carry[part, :] = carry[part, :] * td_rx[k, h:h + 1, :] + t_rx[
-                    k, part, :
-                ].astype(F32)
-
-        pl.when(k < s)(fold)
-    for h in range(2):
-        part = slice(64 * h, 64 * h + 64)
-        moved = carry[part, :]
-        for k in range(CORES):
-            ent_tx[k, part, :] = (inner[k, part, :] + moved).astype(BF16)
-            moved = moved * dec_rx[k, h:h + 1, :]
-    for d in range(1, CORES):
-        to = lax.rem(e + d, CORES)
-        send(rcopy(ent_tx.at[to], ent.at[e], se_s.at[d], se_r.at[d], {"exp": to}))
-    ent[pl.ds(e, 1)] = ent_tx[pl.ds(e, 1)]
-    kv_arrive(4)
-
     def to_mate_copy(b):
-        return rcopy(h_all.at[b, 1 - t // 2], h_oth.at[b], h_s.at[b], h_r.at[b], to_mate)
+        return rcopy(h_all.at[b, 1 - own], h_oth.at[b], h_s.at[b], h_r.at[b], to_mate)
 
     def expert_in(b):
         flat = rows[b].reshape(2 * ROWS, -1)
@@ -402,6 +381,14 @@
         h_all[b, 1, :, 0:UNITS] = units[ROWS:2 * ROWS]
         to_mate_copy(b).start()
 
+    def expert_half(b, which):
+        flat = rows[b, which]
+        nt = (((1,), (1,)), ((), ()))
+        gated_part = lax.dot_general(flat, gu[0], nt, preferred_element_type=F32)
+        up_part = lax.dot_general(flat, gu[1], nt, preferred_element_type=F32)
+        units = (gated_part / (1.0 + jnp.exp(-gated_part)) * up_part).astype(BF16)
+        h_all[b, which, :, 0:UNITS] = units
+
     def expert_pair(j):
         def one(i, _):
             expert_in(lax.rem(s + STEPS + (2 * i - 1) * (j + 1), STEPS))
@@ -409,16 +396,46 @@
 
         lax.fori_loop(0, 2, one, 0)
 
-    def rows_step(j):
-        for i in range(2):
-            rows_down_arrived(j, i).wait_recv()
-            if j < 3:
-                send(rows_down(j + 1, i))
-            if j < 3:
-                rows_up_arrived(j, i).wait_recv()
-                if j < 2:
-                    send(rows_up(j + 1, i))
-
+    def states_in():
+        for d in range(1, STEPS):
+            frm = lax.rem(s + STEPS - d, STEPS)
+            at = t_rx.at[frm]
+            guarded(d <= s, rcopy(at, at, st_s.at[d], st_r.at[d], {"seq": frm}).wait_recv)
+            at = td_rx.at[frm]
+            guarded(d <= s, rcopy(at, at, sd_s.at[d], sd_r.at[d], {"seq": frm}).wait_recv)
+        carry[...] = jnp.zeros_like(carry)
+        for k in range(STEPS - 1):
+
+            def fold(k=k):
+                for h in range(2):
+                    part = slice(64 * h, 64 * h + 64)
+                    carry[part, :] = carry[part, :] * td_rx[k, h:h + 1, :] + t_rx[
+                        k, part, :
+                    ].astype(F32)
+
+            pl.when(k < s)(fold)
+        for h in range(2):
+            part = slice(64 * h, 64 * h + 64)
+            moved = carry[part, :]
+            for k in range(CORES):
+                ent_tx[k, part, :] = (inner[k, part, :] + moved).astype(BF16)
+                moved = moved * dec_rx[k, h:h + 1, :]
+        for d in range(1, CORES):
+            to = lax.rem(e + d, CORES)
+            send(rcopy(ent_tx.at[to], ent.at[e], se_s.at[d], se_r.at[d], {"exp": to}))
+        ent[pl.ds(e, 1)] = ent_tx[pl.ds(e, 1)]
+
+    def rows_step(j, i):
+        rows_down_arrived(j, i).wait_recv()
+        if j < 3:
+            send(rows_down(j + 1, i))
+            rows_up_arrived(j, i).wait_recv()
+            if j < 2:
+                send(rows_up(j + 1, i))
+
+    rows_step(0, 0)
+    kv_arrive(3)
+    rows_step(0, 1)
     kv_forward(1)
     own_gu.wait()
     arrive_a = gu.at[:, third]
@@ -426,31 +443,28 @@
     rcopy(arrive_a, arrive_a, g_s.at[0], g_r.at[0], to_a).wait_recv()
     rcopy(arrive_b, arrive_b, g_s.at[1], g_r.at[1], to_b).wait_recv()
     expert_in(s)
-    rows_step(0)
+    expert_pair(0)
+    rows_step(1, 0)
+    kv_arrive(4)
+    states_in()
     kv_forward(2)
-    kv_forward(3)
-    expert_pair(0)
-    kv_forward(0)
-    rows_step(1)
+    rows_step(1, 1)
     at = dn.at[0, third]
     rcopy(at, at, n_s.at[0], n_r.at[0], to_a).wait_recv()
     send(rcopy(at, dn.at[1, first], n_s.at[4], n_r.at[4], to_b))
     at = dn.at[0, fourth]
     rcopy(at, at, n_s.at[1], n_r.at[1], to_b).wait_recv()
     send(rcopy(at, dn.at[1, second], n_s.at[5], n_r.at[5], to_a))
+    kv_forward(3)
+    kv_forward(0)
     expert_pair(1)
     for g in (1, 2, 3, 0):
         kv_finish(g)
     attend_body(s, e, q, kv, heads, 0)
-    rows_step(2)
+    rows_step(2, 0)
+    rows_step(2, 1)
     expert_pair(2)
     attend_body(s, e, q, kv, heads, 1)
-    for d in range(1, CORES):
-        frm = lax.rem(e + CORES - d, CORES)
-        rcopy(ent.at[frm], ent.at[frm], se_s.at[d], se_r.at[d], {"exp": frm}).wait_recv()
-    state_body(
-        inputs, gate, inflow, readout, cum, cum_t, step_t, skip, gain, ent, state_out, gated
-    )
     own_dn.wait()
     for n, at, dev in (
         (2, dn.at[1, fourth], to_a),
@@ -471,7 +485,7 @@
     def partial_of(b, half):
         cols = slice(2 * width * half, 2 * width * (half + 1))
         return jnp.dot(
-            h_all[b, t // 2, :, 0:UNITS], dn[0, :, cols], preferred_element_type=F32
+            h_all[b, own, :, 0:UNITS], dn[0, :, cols], preferred_element_type=F32
         ) + jnp.dot(h_oth[b, :, 0:UNITS], dn[1, :, cols], preferred_element_type=F32)
 
     def up(stream, j):
@@ -509,19 +523,34 @@
         hop(0, j, True, partial_of(ahead(4 - j), 0))
         hop(1, j, False, partial_of(ahead(4 + j), 1))
 
+    rows_step(3, 0)
+    expert_half(ahead(4), 1 - own)
+    to_mate_copy(ahead(4)).start()
     mate_arrived(ahead(3))
     mate_arrived(ahead(5))
     short_hop(1)
-    rows_step(3)
-    expert_in(ahead(4))
+    rows_step(3, 1)
+    expert_half(ahead(4), own)
     for d in (2, 6, 1, 7, 0):
         mate_arrived(ahead(d))
-    short_hop(2)
     mate_arrived(ahead(4))
     long_hop(0)
+    short_hop(2)
+    long_hop(1)
+    for d in range(1, CORES):
+        frm = lax.rem(e + CORES - d, CORES)
+        rcopy(ent.at[frm], ent.at[frm], se_s.at[d], se_r.at[d], {"exp": frm}).wait_recv()
+
+    def recurrence(g):
+        state_body(
+            inputs, gate, inflow, readout, cum, cum_t, step_t, skip, ent, state_out, gated, g
+        )
+
+    recurrence(0)
+    long_hop(2)
     short_hop(3)
-    for j in range(1, 4):
-        long_hop(j)
+    recurrence(1)
+    long_hop(3)
     finals = [partial_of(s, half) for half in range(2)]
 
     def slot_copy(stream, d, there):
@@ -546,6 +575,7 @@
         for d in range(1, CORES):
             send(slot_copy(stream, d, lax.rem(e + d, CORES)))
         slots[stream, pl.ds(e, 1)] = slots_tx[stream, pl.ds(e, 1)]
+    both_first = (((0,), (0,)), ((), ()))
     high = weigh[...].astype(BF16)
     rest = (weigh[...] - high.astype(F32)).astype(BF16)
     for stream in (0, 2, 1, 3):
@@ -555,8 +585,8 @@
             rcopy(at, at, o_s.at[stream, d], o_r.at[stream, d], {"exp": frm}).wait_recv()
         at = slots[stream].reshape(CORES * PAD, width)
         mine_tx[stream] = (
-            jnp.dot(high, at, preferred_element_type=F32)
-            + jnp.dot(rest, at, preferred_element_type=F32)
+            lax.dot_general(high, at, both_first, preferred_element_type=F32)
+            + lax.dot_general(rest, at, both_first, preferred_element_type=F32)
         ).astype(BF16)
         send(
             rcopy(mine_tx.at[stream], mine.at[t], y_s.at[stream], y_r.at[t], {"tp": stream}),
@@ -568,7 +598,7 @@
         at = mine.at[frm]
         rcopy(at, at, y_s.at[frm], y_r.at[frm], {"tp": frm}).wait_recv()
         total = total + mine[frm].astype(F32)
-    routed[...] = total.astype(BF16)
+    routed[...] = total
     for b in range(STEPS):
         to_mate_copy(b).wait_send()
     for copy, cond in pending:
@@ -585,10 +615,10 @@
         spread_kernel,
         out_shape=(
             jax.ShapeDtypeStruct((2, 512, 128), BF16),
-            jax.ShapeDtypeStruct((128, 1024), BF16),
-            jax.ShapeDtypeStruct((128, quarter), BF16),
+            jax.ShapeDtypeStruct((128, 1024), F32),
+            jax.ShapeDtypeStruct((128, quarter), F32),
         ),
-        in_specs=[vm] * 5 + [hbm] * 2 + [vm] * 9,
+        in_specs=[vm] * 6 + [hbm] * 2 + [vm] * 8,
         out_specs=(vm,) * 3,
         scratch_shapes=[
             VM((STEPS, 2, ROWS, 512), BF16),
@@ -639,48 +669,47 @@
     )(*operands)
 
 
-def state_body(inputs, gate, inflow, readout, cum, cum_t, step_t, skip, gain, ent, out, gated):
+def state_body(inputs, gate, inflow, readout, cum, cum_t, step_t, skip, ent, out, gated, g):
     low = lax.broadcasted_iota(jnp.int32, (128, 128), 1) < 64
     causal = lax.broadcasted_iota(jnp.int32, (128, 128), 0) >= lax.broadcasted_iota(
         jnp.int32, (128, 128), 1)
-    for g in range(2):
-        cols = slice(128 * g, 128 * g + 128)
-        read = readout[:, cols]
-        rw = lax.dot_general(
-            read, inflow[:, cols], (((1,), (1,)), ((), ())), preferred_element_type=F32
-        )
-        square = jnp.zeros((128, 1), F32)
-        for p in range(4):
-            pair = 4 * g + p
-            at = slice(128 * pair, 128 * pair + 128)
-            both = inputs[:, at]
-            parts = []
-            scales = []
-            for h in range(2):
-                head = 2 * pair + h
-                own = cum[:, head:head + 1]
-                gap = jnp.where(causal, own - cum_t[head:head + 1, :], 0.0)
-                mixing = jnp.where(causal, jnp.exp(gap), 0.0) * rw * step_t[head:head + 1, :]
-                parts.append(
-                    jnp.dot(mixing.astype(BF16), both, preferred_element_type=F32)
-                )
-                scales.append(jnp.exp(own))
-            intra = jnp.where(low, parts[0], parts[1])
-            scale = jnp.where(low, scales[0], scales[1])
-            inter = scale * lax.dot_general(
-                read, ent[pair], (((1,), (1,)), ((), ())), preferred_element_type=F32
+    cols = slice(128 * g, 128 * g + 128)
+    read = readout[:, cols]
+    rw = lax.dot_general(
+        read, inflow[:, cols], (((1,), (1,)), ((), ())), preferred_element_type=F32
+    )
+    square = jnp.zeros((128, 1), F32)
+    for p in range(4):
+        pair = 4 * g + p
+        at = slice(128 * pair, 128 * pair + 128)
+        both = inputs[:, at]
+        parts = []
+        scales = []
+        for h in range(2):
+            head = 2 * pair + h
+            own = cum[:, head:head + 1]
+            gap = jnp.where(causal, own - cum_t[head:head + 1, :], 0.0)
+            mixing = jnp.where(causal, jnp.exp(gap), 0.0) * rw * step_t[head:head + 1, :]
+            parts.append(
+                jnp.dot(mixing.astype(BF16), both, preferred_element_type=F32)
             )
-            direct = jnp.where(
-                low, skip[:, 2 * pair:2 * pair + 1], skip[:, 2 * pair + 1:2 * pair + 2]
-            )
-            mixed = intra + inter + direct * both.astype(F32)
-            v = gate[:, at].astype(F32)
-            value = mixed * (v / (1.0 + jnp.exp(-v)))
-            gated[:, 128 * p:128 * p + 128] = value
-            square = square + jnp.sum(value * value, axis=1, keepdims=True)
-        inv = lax.rsqrt(square / 512.0 + EPSILON)
-        wide = slice(512 * g, 512 * g + 512)
-        out[:, wide] = (gated[...] * inv * gain[:, wide]).astype(BF16)
+            scales.append(jnp.exp(own))
+        intra = jnp.where(low, parts[0], parts[1])
+        scale = jnp.where(low, scales[0], scales[1])
+        inter = scale * lax.dot_general(
+            read, ent[pair], (((1,), (1,)), ((), ())), preferred_element_type=F32
+        )
+        direct = jnp.where(
+            low, skip[:, 2 * pair:2 * pair + 1], skip[:, 2 * pair + 1:2 * pair + 2]
+        )
+        mixed = intra + inter + direct * both.astype(F32)
+        v = gate[:, at].astype(F32)
+        value = mixed * (v / (1.0 + jnp.exp(-v)))
+        gated[:, 128 * p:128 * p + 128] = value
+        square = square + jnp.sum(value * value, axis=1, keepdims=True)
+    inv = lax.rsqrt(square / 512.0 + EPSILON)
+    wide = slice(512 * g, 512 * g + 512)
+    out[:, wide] = gated[...] * inv
 
 
 def local(
@@ -688,26 +717,18 @@
     state_readout, step_size, log_decay, skip_scale, state_gain, hidden_in, mlp_gain,
     router_weight, expert_ids, slot_index, gate_up, down_proj,
 ):
-    tp = lax.axis_index("tp")
-    is_live = slot_index >= 0
-    quarter = slot_index // QUARTER
-    inside = slot_index - quarter * QUARTER
-    near = is_live & (quarter % 2 == tp % 2)
-    place = jnp.where(near, expert_ids * (2 * PAD) + (quarter // 2) * PAD + inside, -1)
-    home = jnp.where(is_live & (quarter == tp), expert_ids * PAD + inside, -1)
-    ints = jnp.concatenate([place, home, expert_ids], axis=1)
     kv_in = jnp.concatenate(
         [jnp.transpose(key_heads, (1, 0, 2)), jnp.transpose(value_head_rows, (1, 0, 2))], axis=0
     )
-    heads, state_out, routed_out = spread(
-        kv_in, hidden_in, mlp_gain[None], router_weight.T, ints,
+    heads, states, total = spread(
+        kv_in, hidden_in, mlp_gain[None], router_weight.T, expert_ids.T, slot_index.T,
         jnp.transpose(gate_up[0], (1, 0, 2)), down_proj[0],
         jnp.transpose(query_heads, (1, 0, 2)).reshape(2, 512, 128),
         state_input, state_gate, state_inflow.reshape(128, 256), state_readout.reshape(128, 256),
-        log_decay.T, step_size.T, skip_scale[None], state_gain[None],
+        log_decay.T, step_size.T, skip_scale[None],
     )
     window_out = jnp.transpose(heads.reshape(8, 128, 128), (1, 0, 2))
-    return window_out, state_out, routed_out
+    return window_out, (states * state_gain).astype(BF16), total.astype(BF16)
 
 
 def solution(mesh):

time: 154 us -> 143 us (0.929)
  Pallas kernels: 137 us -> 128 us
  local copies, waits for them, and re-layouts: 13.4 us -> 9.44 us
  other arithmetic: 2.08 us -> 4.08 us
    pallas_call x1, Pallas kernels: 137 us -> 128 us  [spread(): pl.pallas_call(spread_kernel, out_shape=(jax.ShapeDtypeStruct((2, 512, 12...]
    convert_element_type x0 -> x2, other arithmetic: none -> 3.41 us  [local(): return (window_out, (states * state_gain).astype(BF16), total.astype(BF16))]
    unnamed x3, local copies, waits for them, and re-layouts: 6.74 us -> 3.51 us
where the time goes in v4:
time: 143 us; the launch traced here: 142 us
  Pallas kernels  128 us (90%)
  local copies, waits for them, and re-layouts  9.44 us (7%)
  other arithmetic  4.08 us (3%)
    pallas_call x1, Pallas kernels, spread(): pl.pallas_call(spread_kernel, out_shape=(jax.ShapeDtypeStruct((2, 512, 12...  128 us
    unnamed x3, local copies, waits for them, and re-layouts  3.51 us
    convert_element_type x2, other arithmetic, local(): return (window_out, (states * state_gain).astype(BF16), total.astype(BF16))  3.41 us

profile of v4, /device:TPU:1, one launch (start us, length us, event | category | flops | bytes accessed | tf_op | source)
XLA Modules:
  0.0 142.2 jit_solution(11845649621017825175)
XLA Ops:
  0.6 0.9 copy_bitcast_fusion.4
  1.5 0.7 pad_maximum_fusion.kv_in
  2.2 1.5 %copy_bitcast_fusion.2 = (bf16[128,256]{1,0:T(8,128)(2,1)}, bf16[128,256]{1,0:T(8,128)(2,1)}) fusion(bf16[16,8,2,128]{3,2,1,0:T(2,128)(2,1)} %bitcast.35, bf16[16,8,2,128]{3,2,1,0:T(2,128)(2,1)} %bitcast.36), kind=kLoop, calls=%fused_computation.4 | loop fusion | bytes 262144 | tf_op jit(solution)/shard_map/reshape | solution.py:727
  3.7 1.7 %copy.24 = bf16[8,128,128]{2,1,0:T(8,128)(2,1)} copy(bf16[8,128,128]{2,0,1:T(8,128)(2,1)} %bitcast.32) | data formatting | bytes 524288 | tf_op jit(solution)/shard_map/transpose | solution.py:726
  5.4 3.5 %copy.34 = bf16[1,224,2,2048]{3,1,2,0:T(8,128)(2,1)} copy(bf16[1,224,2,2048]{3,2,1,0:T(2,128)(2,1)} %param.34) | data formatting | bytes 3670016 | tf_op args[16]
  8.9 0.0 copy-start
  8.9 128.1 %spread.1 = (bf16[2,512,128]{2,1,0:T(8,128)(2,1)}, f32[128,1024]{1,0:T(8,128)}, f32[128,512]{1,0:T(8,128)}) custom-call(bf16[4,128,128]{2,1,0:T(8,128)(2,1)} %pad_maximum_fusion.kv_in, bf16[128,2048]{1,0:T(8,128)(2,1)} %hidden.1, f32[1,2048]{1,0:T(1,128)} %bitcast.38, bf16[8,2048]{1,0:T(8,128)(2,1)} %bitcast.37, s32[2,128]{1,0:T(2,128)} %bitcast.41, ...), custom_call_target="tpu_custom_call" | custom-call | tf_op jit(solution)/shard_map/spread/pallas_call | solution.py:614
  137.0 1.8 %copy.35 = bf16[8,128,128]{2,0,1:T(8,128)(2,1)} copy(bf16[8,128,128]{2,1,0:T(8,128)(2,1)} %bitcast.34) | data formatting | bytes 524288 | tf_op jit(solution)/shard_map/reshape | solution.py:730
  138.8 1.6 %convert_element_type.7 = bf16[128,512]{1,0:T(8,128)(2,1)} convert(f32[128,512]{1,0:T(8,128)} %get-tuple-element.8) | non-fusion elementwise | flops 65536 | bytes 393216 | tf_op jit(solution)/shard_map/convert_element_type | solution.py:731
  140.4 0.0 copy-done
  140.5 1.8 %multiply_convert_fusion = bf16[128,1024]{1,0:T(8,128)(2,1)} fusion(f32[128,1024]{1,0:T(8,128)} %get-tuple-element.7, f32[1024]{0:T(1024)S(1)} %copy-done), kind=kLoop, calls=%fused_computation.1 | loop fusion | flops 262144 | bytes 790528 | tf_op jit(solution)/shard_map/convert_element_type | solution.py:731
Async XLA Ops:
  8.9 131.5 %copy-start = (f32[1024]{0:T(1024)S(1)}, f32[1024]{0:T(1024)}, u32[]{:S(2)}) copy-start(f32[1024]{0:T(1024)} %param.28) | copy-start | bytes 12292

commit v5 on v4

--- a/solution.py
+++ b/solution.py
@@ -84,7 +84,7 @@
         )
         return new, total, acc
 
-    query = q[group]
+    query = jnp.concatenate([q[:, 4 * group + k, :] for k in range(4)], axis=0)
     k0 = kv[group, 0:8].reshape(1024, 128)
     v0 = jnp.where(v_ok, kv[2 + group, 0:8].reshape(1024, 128), jnp.zeros((), BF16))
     state = (
@@ -276,7 +276,7 @@
     dec_in[...] = jnp.zeros_like(dec_in)
     for pair in range(8):
         dec_in[pair, 0:2, :] = whole_decay[2 * pair:2 * pair + 2]
-        vectors = inflow[:, 128 * (pair // 4):128 * (pair // 4) + 128].astype(F32)
+        vectors = inflow[:, pair // 4, :].astype(F32)
         both = inputs[:, 128 * pair:128 * pair + 128]
         for h in range(2):
             head = 2 * pair + h
@@ -500,28 +500,31 @@
             {"seq": prv},
         )
 
-    def hop(half, j, rising, value):
+    def hop(half, j, rising, value, i):
         begin = 0 if (half == 0) == rising else 1
         tx, rx, line = (tx_f, rx_f, up) if rising else (tx_b, rx_b, down)
-        for i in range(2):
-            stream = 2 * half + i
-            piece = value[:, columns(i)]
-            if j > begin:
-                line(stream, j - 1).wait_recv()
-                piece = piece + rx[stream, j - 1].astype(F32)
-            tx[stream, j] = piece.astype(BF16)
-            send(line(stream, j))
+        stream = 2 * half + i
+        piece = value[:, columns(i)]
+        if j > begin:
+            line(stream, j - 1).wait_recv()
+            piece = piece + rx[stream, j - 1].astype(F32)
+        tx[stream, j] = piece.astype(BF16)
+        send(line(stream, j))
 
     def ahead(d):
         return lax.rem(s + d, STEPS)
 
     def short_hop(j):
-        hop(1, j, True, partial_of(ahead(4 - j), 1))
-        hop(0, j, False, partial_of(ahead(4 + j), 0))
+        rise, fall = partial_of(ahead(4 - j), 1), partial_of(ahead(4 + j), 0)
+        for i in range(2):
+            hop(1, j, True, rise, i)
+            hop(0, j, False, fall, i)
 
     def long_hop(j):
-        hop(0, j, True, partial_of(ahead(4 - j), 0))
-        hop(1, j, False, partial_of(ahead(4 + j), 1))
+        rise, fall = partial_of(ahead(4 - j), 0), partial_of(ahead(4 + j), 1)
+        for i in range(2):
+            hop(0, j, True, rise, i)
+            hop(1, j, False, fall, i)
 
     rows_step(3, 0)
     expert_half(ahead(4), 1 - own)
@@ -674,9 +677,9 @@
     causal = lax.broadcasted_iota(jnp.int32, (128, 128), 0) >= lax.broadcasted_iota(
         jnp.int32, (128, 128), 1)
     cols = slice(128 * g, 128 * g + 128)
-    read = readout[:, cols]
+    read = readout[:, g, :]
     rw = lax.dot_general(
-        read, inflow[:, cols], (((1,), (1,)), ((), ())), preferred_element_type=F32
+        read, inflow[:, g, :], (((1,), (1,)), ((), ())), preferred_element_type=F32
     )
     square = jnp.zeros((128, 1), F32)
     for p in range(4):
@@ -723,8 +726,8 @@
     heads, states, total = spread(
         kv_in, hidden_in, mlp_gain[None], router_weight.T, expert_ids.T, slot_index.T,
         jnp.transpose(gate_up[0], (1, 0, 2)), down_proj[0],
-        jnp.transpose(query_heads, (1, 0, 2)).reshape(2, 512, 128),
-        state_input, state_gate, state_inflow.reshape(128, 256), state_readout.reshape(128, 256),
+        query_heads,
+        state_input, state_gate, state_inflow, state_readout,
         log_decay.T, step_size.T, skip_scale[None],
     )
     window_out = jnp.transpose(heads.reshape(8, 128, 128), (1, 0, 2))

time: 143 us -> 140 us (0.979)
  local copies, waits for them, and re-layouts: 9.44 us -> 6.23 us
    transpose x1 -> x0, local copies, waits for them, and re-layouts: 1.69 us -> none  [local(): jnp.transpose(query_heads, (1, 0, 2)).reshape(2, 512, 128)]
    reshape x1 -> x0, local copies, waits for them, and re-layouts: 1.52 us -> none  [local(): state_readout.reshape(128, 256)]
where the time goes in v5:
time: 140 us; the launch traced here: 139 us
  Pallas kernels  128 us (91%)
  local copies, waits for them, and re-layouts  6.23 us (4%)
  other arithmetic  4.08 us (3%)
    pallas_call x1, Pallas kernels, spread(): pl.pallas_call(spread_kernel, out_shape=(jax.ShapeDtypeStruct((2, 512, 12...  128 us
    unnamed x3, local copies, waits for them, and re-layouts  3.51 us
    convert_element_type x2, other arithmetic, local(): return (window_out, (states * state_gain).astype(BF16), total.astype(BF16))  3.41 us

profile of v5, /device:TPU:1, one launch (start us, length us, event | category | flops | bytes accessed | tf_op | source)
XLA Modules:
  0.0 139.3 jit_solution(6840419871347639043)
XLA Ops:
  0.6 0.9 copy_bitcast_fusion.2
  1.5 0.7 pad_maximum_fusion.kv_in
  2.2 3.5 %copy.29 = bf16[1,224,2,2048]{3,1,2,0:T(8,128)(2,1)} copy(bf16[1,224,2,2048]{3,2,1,0:T(2,128)(2,1)} %param.34) | data formatting | bytes 3670016 | tf_op args[16]
  5.7 0.0 copy-start
  5.7 128.3 %spread.1 = (bf16[2,512,128]{2,1,0:T(8,128)(2,1)}, f32[128,1024]{1,0:T(8,128)}, f32[128,512]{1,0:T(8,128)}) custom-call(bf16[4,128,128]{2,1,0:T(8,128)(2,1)} %pad_maximum_fusion.kv_in, bf16[128,2048]{1,0:T(8,128)(2,1)} %hidden.1, f32[1,2048]{1,0:T(1,128)} %bitcast.26, bf16[8,2048]{1,0:T(8,128)(2,1)} %bitcast.25, s32[2,128]{1,0:T(2,128)} %bitcast.29, ...), custom_call_target="tpu_custom_call" | custom-call | tf_op jit(solution)/shard_map/spread/pallas_call | solution.py:617
  134.0 1.8 %copy.30 = bf16[8,128,128]{2,0,1:T(8,128)(2,1)} copy(bf16[8,128,128]{2,1,0:T(8,128)(2,1)} %bitcast.24) | data formatting | bytes 524288 | tf_op jit(solution)/shard_map/reshape | solution.py:733
  135.9 1.6 %convert_element_type.7 = bf16[128,512]{1,0:T(8,128)(2,1)} convert(f32[128,512]{1,0:T(8,128)} %get-tuple-element.8) | non-fusion elementwise | flops 65536 | bytes 393216 | tf_op jit(solution)/shard_map/convert_element_type | solution.py:734
  137.5 0.0 copy-done
  137.5 1.8 %multiply_convert_fusion = bf16[128,1024]{1,0:T(8,128)(2,1)} fusion(f32[128,1024]{1,0:T(8,128)} %get-tuple-element.7, f32[1024]{0:T(1024)S(1)} %copy-done), kind=kLoop, calls=%fused_computation.1 | loop fusion | flops 262144 | bytes 790528 | tf_op jit(solution)/shard_map/convert_element_type | solution.py:734
Async XLA Ops:
  5.7 131.8 %copy-start = (f32[1024]{0:T(1024)S(1)}, f32[1024]{0:T(1024)}, u32[]{:S(2)}) copy-start(f32[1024]{0:T(1024)} %param.28) | copy-start | bytes 12292
